TPU v7x, 128 devices: a whole 4x4x4 slice. The times are simulated.
128 devices in a mesh: seq: 64 (over z_hi, x, y, core), dp: 2 (over z_lo).
Axes of the slice: x: 4, y: 4, z: 4 (z_hi: 2, z_lo: 2; z = z_hi * 2 + z_lo), core: 2. Of those that a mesh axis runs over, the one named last changes fastest.
Arguments:
- block_pos: int32 [2, 128], P('dp'), may hold values from 0 to 127, as said below
- queries: bfloat16 [2, 8192, 2048], P('dp', 'seq'), may hold values from -8 to 8
- keys: bfloat16 [2, 8192, 2048], P('dp', 'seq'), may hold values from -4 to 4
- values: bfloat16 [2, 8192, 2048], P('dp', 'seq'), may hold values from -4 to 4
- attn_out: bfloat16 [2, 8192, 2048], P('dp', 'seq'), may hold values from -4 to 4, as said below
- log_sums: float32 [2, 16, 8192], P('dp', None, 'seq'), as said below
- grad_out: bfloat16 [2, 8192, 2048], P('dp', 'seq'), may hold values from -0.375 to 0.375
- out_weight: bfloat16 [2048, 2048], replicated, may hold values from -12 to 12
Outputs:
- grad_queries: bfloat16 [2, 8192, 2048], P('dp', 'seq')
- grad_keys: bfloat16 [2, 8192, 2048], P('dp', 'seq')
- grad_values: bfloat16 [2, 8192, 2048], P('dp', 'seq')
- grad_weight: float32 [2048, 2048], P('seq')
Inputs may be any that keep to these rules, and one draw needn't show every extreme that they name: Each row is a permutation of 0 to 127; row block c (rows c * 64 to c * 64 + 63) holds the rows at positions block_pos[b, c] * 64 onward, in order. attn_out is the forward attention output: per head, exp(scores - log_sums) on the allowed keys times values, rounded to bfloat16. log_sums[b, h, t] is the log of the sum of exp(scores[b, h, t, u]) over the keys u with pos[b, u] <= pos[b, t].
All inputs are finite; a program needn't handle non-finite values.
Results may differ from a plain program's by a relative error of at most 0.0075.
Values may be sent and summed in bfloat16 or wider, within the bound.
No kernel may reach another device: no remote copies, remote signals or barrier semaphores. Data moves between devices by JAX's collectives and lax.ppermute only.
A program may use at most 320 MiB of HBM per device.

v0:
```python
import jax
import jax.numpy as jnp
from jax import lax
from jax.sharding import Mesh
from jax.sharding import PartitionSpec as P

SEQ = ("seq_0", "seq_1", "seq_2", "seq_3")


def shifted(shard, axis, by):
    count = lax.axis_size(axis)
    return lax.ppermute(shard, axis, [(i, (i + by) % count) for i in range(count)])


def cut_along(shard, dim, count):
    dims = shard.shape
    tiles = shard.reshape(*dims[:dim], count, dims[dim] // count, *dims[dim + 1 :])
    return jnp.moveaxis(tiles, dim, 0)


def summed_rows(shard, chips, core, dim):
    sizes = (lax.axis_size(chips), lax.axis_size(core))
    tiles = cut_along(shard, dim, sizes[0] * sizes[1])
    inside = tiles.shape[1:]
    tiles = tiles.reshape(*sizes, *inside).swapaxes(0, 1).reshape(-1, *inside)
    tiles = lax.psum_scatter(tiles, core, scatter_dimension=0, tiled=True)
    return lax.psum_scatter(tiles, chips, scatter_dimension=0, tiled=True)[0]


def slot_positions(table_row, owners, half_rows):
    slot_ids = owners[:, None] * 2 + jnp.arange(2, dtype=jnp.int32)[None, :]
    pick_rows = (
        slot_ids[:, :, None] == jnp.arange(table_row.shape[0], dtype=jnp.int32)[None, None, :]
    ).astype(jnp.int32)
    block_ids = jnp.sum(pick_rows * table_row[None, None, :], axis=-1)
    offsets = jnp.arange(half_rows, dtype=jnp.int32)
    return (block_ids[:, :, None] * half_rows + offsets[None, None, :]).reshape(
        owners.shape[0], 2 * half_rows
    )


def block_core(
    query_rows, grad_rows, log_block, delta_block, key_rows, value_rows, allowed, scaling
):
    head_count = log_block.shape[0]
    query_len = query_rows.shape[0]
    key_len = key_rows.shape[0]
    query_heads = query_rows.reshape(query_len, head_count, -1)
    grad_split = grad_rows.reshape(query_len, head_count, -1)
    key_heads = key_rows.reshape(key_len, head_count, -1)
    value_heads = value_rows.reshape(key_len, head_count, -1)
    scores = (
        jnp.einsum("ahd,bhd->hab", query_heads, key_heads, preferred_element_type=jnp.float32)
        * scaling
    )
    attn_probs = jnp.where(allowed[None], jnp.exp(scores - log_block[:, :, None]), 0.0)
    probs_low = attn_probs.astype(jnp.bfloat16)
    dprobs = jnp.einsum("ahd,bhd->hab", grad_split, value_heads, preferred_element_type=jnp.float32)
    dscores = attn_probs * (dprobs - delta_block[:, :, None])
    dscores_low = dscores.astype(jnp.bfloat16)
    value_part = jnp.einsum(
        "hab,ahd->bhd", probs_low, grad_split, preferred_element_type=jnp.float32
    )
    key_part = (
        jnp.einsum("hab,ahd->bhd", dscores_low, query_heads, preferred_element_type=jnp.float32)
        * scaling
    )
    query_part = (
        jnp.einsum("hab,bhd->ahd", dscores_low, key_heads, preferred_element_type=jnp.float32)
        * scaling
    )
    return (
        query_part.reshape(query_len, -1),
        key_part.reshape(key_len, -1),
        value_part.reshape(key_len, -1),
    )


def block_grads(
    query_rows, grad_rows, log_block, delta_block, key_rows, value_rows, allowed, scaling
):
    parts = block_core(
        query_rows, grad_rows, log_block, delta_block, key_rows, value_rows, allowed, scaling
    )
    return (parts[0], parts[1].astype(jnp.bfloat16), parts[2].astype(jnp.bfloat16))


def per_device(block_pos, queries, keys, values, attn_out, log_sums, grad_out, out_weight):
    dev_count = lax.axis_size(SEQ)
    grid_side = 4 + 4 * (dev_count // 64)
    my_index = lax.axis_index(SEQ)
    table_row = block_pos[0]
    own_queries = queries[0]
    tok_rows = own_queries.shape[0]
    half_rows = tok_rows // 2
    head_count = log_sums.shape[1]
    width_all = own_queries.shape[1]
    scaling = (width_all // head_count) ** (-0.5)
    cotangent = grad_out[0]
    grad_heads = lax.dot_general(
        cotangent, out_weight, (((1,), (1,)), ((), ())), preferred_element_type=jnp.float32
    ).astype(jnp.bfloat16)
    deltas = jnp.einsum(
        "ahd,ahd->ha",
        grad_heads.reshape(tok_rows, head_count, -1),
        attn_out[0].reshape(tok_rows, head_count, -1),
        preferred_element_type=jnp.float32,
    )
    query_pack = (own_queries[None], grad_heads[None], log_sums[0][None], deltas[None])
    key_pack = (keys[0][None], values[0][None])
    query_list = [query_pack]
    key_list = [key_pack]
    for offset in range(1, grid_side):
        query_list.append(
            (
                shifted(query_pack[0].astype(jnp.float32), SEQ, offset).astype(jnp.bfloat16),
                shifted(query_pack[1].astype(jnp.float32), SEQ, offset).astype(jnp.bfloat16),
                shifted(query_pack[2], SEQ, offset),
                shifted(query_pack[3], SEQ, offset),
            )
        )
        key_list.append(shifted((key_pack[0], key_pack[1]), SEQ, offset * grid_side))
    query_stack = tuple(
        (jnp.concatenate([parcel[member] for parcel in query_list], axis=0) for member in range(4))
    )
    key_stack = tuple(
        (jnp.concatenate([parcel[member] for parcel in key_list], axis=0) for member in range(2))
    )
    query_rows = query_stack[0].reshape(-1, width_all)
    grad_rows = query_stack[1].reshape(-1, width_all)
    log_block = jnp.transpose(query_stack[2], (1, 0, 2)).reshape(head_count, -1)
    delta_block = jnp.transpose(query_stack[3], (1, 0, 2)).reshape(head_count, -1)
    query_owners = (my_index - jnp.arange(grid_side, dtype=jnp.int32)) % dev_count
    key_owners = (my_index - jnp.arange(grid_side, dtype=jnp.int32) * grid_side) % dev_count
    query_pos = slot_positions(table_row, query_owners, half_rows).reshape(-1)
    key_pos = slot_positions(table_row, key_owners, half_rows)
    query_total = jnp.zeros((grid_side * tok_rows, width_all), jnp.float32)
    key_results = []
    for offset in range(grid_side):
        key_now = key_stack[0][offset]
        value_now = key_stack[1][offset]
        allowed = key_pos[offset][None, :] <= query_pos[:, None]
        results = block_grads(
            query_rows, grad_rows, log_block, delta_block, key_now, value_now, allowed, scaling
        )
        query_total = query_total + results[0]
        key_results.append((results[1], results[2]))
    query_parts = query_total.astype(jnp.bfloat16).reshape(grid_side, tok_rows, width_all)
    query_sum = query_parts[0].astype(jnp.float32)
    for offset in range(1, grid_side):
        query_sum = query_sum + shifted(query_parts[offset], SEQ, -offset).astype(jnp.float32)
    key_sum = key_results[0][0].astype(jnp.float32)
    value_sum = key_results[0][1].astype(jnp.float32)
    for offset in range(1, grid_side):
        returned = shifted(
            (key_results[offset][0], key_results[offset][1]), SEQ, -offset * grid_side
        )
        key_sum = key_sum + returned[0].astype(jnp.float32)
        value_sum = value_sum + returned[1].astype(jnp.float32)
    columns = attn_out[0]
    weight_share = summed_rows(
        lax.dot_general(
            columns, cotangent, (((0,), (0,)), ((), ())), preferred_element_type=jnp.float32
        ),
        ("seq_0", "seq_1", "seq_2"),
        "seq_3",
        0,
    )
    weight_share = lax.psum(weight_share.astype(jnp.bfloat16), "dp").astype(jnp.float32)
    return (
        query_sum.astype(jnp.bfloat16)[None],
        key_sum.astype(jnp.bfloat16)[None],
        value_sum.astype(jnp.bfloat16)[None],
        weight_share,
    )


def solution(mesh):
    split = Mesh(
        mesh.devices.reshape(2, 4, 4, 2, mesh.shape["dp"]),
        ("seq_0", "seq_1", "seq_2", "seq_3", "dp"),
    )
    placed = (
        P("dp", None),
        P("dp", SEQ, None),
        P("dp", SEQ, None),
        P("dp", SEQ, None),
        P("dp", SEQ, None),
        P("dp", None, SEQ),
        P("dp", SEQ, None),
        P(),
    )
    return jax.shard_map(
        per_device,
        mesh=split,
        in_specs=placed,
        out_specs=(P("dp", SEQ, None), P("dp", SEQ, None), P("dp", SEQ, None), P(SEQ, None)),
        check_vma=False,
    )
```

profile of v0, /device:TPU:1, one launch (start us, length us, event | category | flops | bytes accessed | tf_op | source)
XLA Modules:
  0.0 761.4 jit_solution(5213341884822088571)
XLA Ops:
  10.9 6.4 copy.269
  29.1 8.0 %bitcast_dynamic-update-slice_fusion = (bf16[8,128,2048]{2,1,0:T(8,128)(2,1)}, bf16[128,2048]{1,0:T(8,128)(2,1)S(1)}) fusion(bf16[2048,2048]{1,0:T(8,128)(2,1)} %param.15, bf16[1,128,2048]{2,1,0:T(8,128)(2,1)S(1)} %copy-done), kind=kOutput, calls=%fused_computation.110 | convolution fusion | flops 1074003968 | bytes 9961472 | tf_op jit(solution)/shard_map/dot_general | solution.py:100
  43.8 6.7 collective-permute-done.8
  50.8 3.7 collective-permute-start.27
  58.5 15.3 %collective-permute-start.24 = (f32[1,16,128]{2,0,1:T(1,128)S(1)}, f32[1,16,128]{2,0,1:T(1,128)S(1)}, u32[]{:S(2)}, u32[]{:S(2)}) collective-permute-start(f32[1,16,128]{2,0,1:T(1,128)S(1)} %bitcast.285), channel_id=1, source_target_pairs={{0,8},{2,10},{4,12},{6,14},{8,16},{10,18},{12,20},{14,22},{16,24},... | collective-permute-start | bytes 24584 | tf_op jit(solution)/shard_map/ppermute | solution.py:12
  78.4 4.7 collective-permute-done.23
  83.7 4.4 collective-permute-start.21
  88.2 7.1 collective-permute-done.22
  100.8 4.8 collective-permute-start.5
  106.5 20.8 %collective-permute-done.3 = bf16[1,128,2048]{2,1,0:T(8,128)(2,1)S(1)} collective-permute-done((bf16[1,128,2048]{2,1,0:T(8,128)(2,1)S(1)}, bf16[1,128,2048]{2,1,0:T(8,128)(2,1)S(1)}, u32[]{:S(2)}, u32[]{:S(2)}) %collective-permute-start.3) | collective-permute-done | bytes 524320 | tf_op jit(solution)/shard_map/ppermute | solution.py:12
  128.1 10.7 %collective-permute-done.4 = bf16[1,128,2048]{2,1,0:T(8,128)(2,1)S(1)} collective-permute-done((bf16[1,128,2048]{2,1,0:T(8,128)(2,1)S(1)}, bf16[1,128,2048]{2,1,0:T(8,128)(2,1)S(1)}, u32[]{:S(2)}, u32[]{:S(2)}) %collective-permute-start.4) | collective-permute-done | bytes 524320 | tf_op jit(solution)/shard_map/ppermute | solution.py:12
  139.7 13.6 %collective-permute-done.5 = bf16[1,128,2048]{2,1,0:T(8,128)(2,1)S(1)} collective-permute-done((bf16[1,128,2048]{2,1,0:T(8,128)(2,1)S(1)}, bf16[1,128,2048]{2,1,0:T(8,128)(2,1)S(1)}, u32[]{:S(2)}, u32[]{:S(2)}) %collective-permute-start.5) | collective-permute-done | bytes 524320 | tf_op jit(solution)/shard_map/ppermute | solution.py:12
  154.8 6.5 collective-permute-start.16
  163.3 40.8 %collective-permute-done.15 = bf16[1,128,2048]{2,1,0:T(8,128)(2,1)S(1)} collective-permute-done((bf16[1,128,2048]{2,1,0:T(8,128)(2,1)S(1)}, bf16[1,128,2048]{2,1,0:T(8,128)(2,1)S(1)}, u32[]{:S(2)}, u32[]{:S(2)}) %collective-permute-start.15) | collective-permute-done | bytes 524320 | tf_op jit(solution)/shard_map/ppermute | solution.py:12
  210.1 15.9 %collective-permute-done.18 = bf16[1,128,2048]{2,1,0:T(8,128)(2,1)S(1)} collective-permute-done((bf16[1,128,2048]{2,1,0:T(8,128)(2,1)S(1)}, bf16[1,128,2048]{2,1,0:T(8,128)(2,1)S(1)}, u32[]{:S(2)}, u32[]{:S(2)}) %collective-permute-start.18) | collective-permute-done | bytes 524320 | tf_op jit(solution)/shard_map/ppermute | solution.py:12
  230.2 6.7 copy.236
  237.8 7.5 collective-permute-done.20
  246.0 5.6 copy.305
  251.6 6.7 copy.252
  258.8 3.7 fusion.142
  266.8 8.6 %multiply_convert_fusion.1 = bf16[16,1024,128]{2,1,0:T(8,128)(2,1)S(1)} fusion(f32[16,1024,128]{2,1,0:T(8,128)} %copy-done.15, f32[16,1024]{1,0:T(8,128)S(1)} %bitcast.274, f32[16,1024]{1,0:T(8,128)S(1)} %copy_bitcast_fusion.1, pred[1024,128]{1,0:T(8,128)(4,1)S(1)} %copy-done.55, bf16[1024,16,128]{0,2,1:T(8,128)(2,1)} %copy.252, ...), kind=kOutput, calls=%fused_computation.1 | convolution fusion | flops 549453824 | bytes 17563648 | tf_op jit(solution)/shard_map/ahd,bhd->hab/dot_general | solution.py:58
  279.9 4.7 collective-permute-start.31
  284.6 3.7 fusion.140
  294.4 8.6 %multiply_convert_fusion.2 = bf16[16,1024,128]{2,1,0:T(8,128)(2,1)S(1)} fusion(f32[16,1024,128]{2,1,0:T(8,128)} %copy-done.16, f32[16,1024]{1,0:T(8,128)S(1)} %bitcast.275, f32[16,1024]{1,0:T(8,128)S(1)} %copy_bitcast_fusion.1, pred[1024,128]{1,0:T(8,128)(4,1)S(1)} %copy-done.54, bf16[1024,16,128]{0,2,1:T(8,128)(2,1)} %copy.252, ...), kind=kOutput, calls=%fused_computation.3 | convolution fusion | flops 549453824 | bytes 17563648 | tf_op jit(solution)/shard_map/ahd,bhd->hab/dot_general | solution.py:58
  309.7 3.7 fusion.138
  319.5 8.6 %multiply_convert_fusion.3 = bf16[16,1024,128]{2,1,0:T(8,128)(2,1)S(1)} fusion(f32[16,1024,128]{2,1,0:T(8,128)} %copy-done.17, f32[16,1024]{1,0:T(8,128)S(1)} %bitcast.276, f32[16,1024]{1,0:T(8,128)S(1)} %copy_bitcast_fusion.1, pred[1024,128]{1,0:T(8,128)(4,1)S(1)} %copy-done.53, bf16[1024,16,128]{0,2,1:T(8,128)(2,1)} %copy.252, ...), kind=kOutput, calls=%fused_computation.5 | convolution fusion | flops 549453824 | bytes 17563648 | tf_op jit(solution)/shard_map/ahd,bhd->hab/dot_general | solution.py:58
  332.3 4.4 collective-permute-done.34
  336.9 3.7 fusion.136
  340.6 3.8 fusion.81
  347.3 8.6 %multiply_convert_fusion.4 = bf16[16,1024,128]{2,1,0:T(8,128)(2,1)S(1)} fusion(f32[16,1024,128]{2,1,0:T(8,128)} %copy-done.18, f32[16,1024]{1,0:T(8,128)S(1)} %bitcast.277, f32[16,1024]{1,0:T(8,128)S(1)} %copy_bitcast_fusion.1, pred[1024,128]{1,0:T(8,128)(4,1)S(1)} %copy-done.52, bf16[1024,16,128]{0,2,1:T(8,128)(2,1)} %copy.252, ...), kind=kOutput, calls=%fused_computation.7 | convolution fusion | flops 549453824 | bytes 17563648 | tf_op jit(solution)/shard_map/ahd,bhd->hab/dot_general | solution.py:58
  361.9 3.8 fusion.134
  367.0 8.2 %multiply_convert_fusion.5 = bf16[16,1024,128]{2,1,0:T(8,128)(2,1)S(1)} fusion(f32[16,1024,128]{2,1,0:T(8,128)S(1)} %fusion.134, f32[16,1024]{1,0:T(8,128)S(1)} %bitcast.278, f32[16,1024]{1,0:T(8,128)S(1)} %copy_bitcast_fusion.1, pred[1024,128]{1,0:T(8,128)(4,1)S(1)} %copy-done.50, bf16[1024,16,128]{0,2,1:T(8,128)(2,1)S(1)} %copy-done.36, ...), kind=kOutput, calls=%fused_computation.9 | convolution fusion | flops 549453824 | bytes 17563648 | tf_op jit(solution)/shard_map/ahd,bhd->hab/dot_general | solution.py:58
  382.8 7.0 fusion.132
  390.9 8.6 %multiply_convert_fusion.6 = bf16[16,1024,128]{2,1,0:T(8,128)(2,1)S(1)} fusion(f32[16,1024,128]{2,1,0:T(8,128)} %fusion.132, f32[16,1024]{1,0:T(8,128)S(1)} %bitcast.279, f32[16,1024]{1,0:T(8,128)S(1)} %copy_bitcast_fusion.1, pred[1024,128]{1,0:T(8,128)(4,1)S(1)} %copy-done.48, bf16[1024,16,128]{0,2,1:T(8,128)(2,1)} %copy.252, ...), kind=kOutput, calls=%fused_computation.11 | convolution fusion | flops 549453824 | bytes 17563648 | tf_op jit(solution)/shard_map/ahd,bhd->hab/dot_general | solution.py:58
  406.9 3.8 fusion.130
  412.0 8.2 %multiply_convert_fusion.7 = bf16[16,1024,128]{2,1,0:T(8,128)(2,1)S(1)} fusion(f32[16,1024,128]{2,1,0:T(8,128)S(1)} %fusion.130, f32[16,1024]{1,0:T(8,128)S(1)} %bitcast.280, f32[16,1024]{1,0:T(8,128)S(1)} %copy_bitcast_fusion.1, pred[1024,128]{1,0:T(8,128)(4,1)S(1)} %get-tuple-element.30, bf16[1024,16,128]{0,2,1:T(8,128)(2,1)S(1)} %copy-done.37, ...), kind=kOutput, calls=%fused_computation.13 | convolution fusion | flops 549453824 | bytes 17563648 | tf_op jit(solution)/shard_map/ahd,bhd->hab/dot_general | solution.py:58
  424.5 6.9 fusion.141
  431.4 4.6 fusion.139
  436.0 4.6 fusion.137
  440.6 5.7 fusion.135
  446.3 5.9 fusion.133
  452.1 5.8 fusion.131
  459.3 4.2 copy-done.14
  463.6 6.5 multiply_convert_fusion.8
  472.1 4.6 fusion.129
  479.9 3.8 fusion.75
  483.7 22.9 %fusion.24 = bf16[1024,16,128]{2,0,1:T(8,128)(2,1)} fusion(f32[16,1024,128]{2,1,0:T(8,128)} %fusion.141, f32[16,1024,128]{2,1,0:T(8,128)} %fusion.139, f32[16,1024,128]{2,1,0:T(8,128)} %fusion.137, f32[16,1024,128]{2,1,0:T(8,128)} %fusion.135, f32[16,1024,128]{2,1,0:T(8,128)} %fusion.133, f32[16,1024,128]{2,1,0:T(8,128)} %fusion.129, ...), kind=kOutput, calls=%fused_computation.34 | convolution fusion | flops 555745280 | bytes 67633152 | tf_op jit(solution)/shard_map/hab,bhd->ahd/dot_general | solution.py:69
  506.6 7.1 fusion.72
  515.2 6.0 fusion.69
  529.8 7.3 collective-permute-done.60
  548.1 4.0 fusion.126
  567.1 3.9 collective-permute-done.59
  571.0 20.8 %collective-permute-start.57 = (bf16[128,2048]{1,0:T(8,128)(2,1)}, bf16[128,2048]{1,0:T(8,128)(2,1)S(1)}, u32[]{:S(2)}, u32[]{:S(2)}) collective-permute-start(bf16[128,2048]{1,0:T(8,128)(2,1)} %copy.257), channel_id=1, source_target_pairs={{0,96},{2,98},{4,100},{6,102},{8,104},{10,106},{12,108},{14,110},{... | collective-permute-start | bytes 1572872 | tf_op jit(solution)/shard_map/ppermute | solution.py:12
  591.8 18.6 %collective-permute-start.48 = (bf16[128,2048]{0,1:T(8,128)(2,1)}, bf16[128,2048]{0,1:T(8,128)(2,1)}, u32[]{:S(2)}, u32[]{:S(2)}) collective-permute-start(bf16[128,2048]{0,1:T(8,128)(2,1)} %bitcast.258), channel_id=1, source_target_pairs={{0,114},{2,116},{4,118},{6,120},{8,122},{10,124},{12,126},{14,0},{... | collective-permute-start | bytes 1572872 | tf_op jit(solution)/shard_map/ppermute | solution.py:12
  610.4 30.6 %collective-permute-start.43 = (bf16[128,2048]{0,1:T(8,128)(2,1)}, bf16[128,2048]{0,1:T(8,128)(2,1)}, u32[]{:S(2)}, u32[]{:S(2)}) collective-permute-start(bf16[128,2048]{0,1:T(8,128)(2,1)} %bitcast.257), channel_id=1, source_target_pairs={{0,124},{2,126},{4,0},{6,2},{8,4},{10,6},{12,8},{14,10},{16,12},{1... | collective-permute-start | bytes 1572872 | tf_op jit(solution)/shard_map/ppermute | solution.py:12
  641.0 3.7 fusion.101
  644.8 4.1 collective-permute-start.44
  648.9 3.6 collective-permute-start.45
  655.5 11.4 %collective-permute-start.47 = (bf16[128,2048]{0,1:T(8,128)(2,1)}, bf16[128,2048]{0,1:T(8,128)(2,1)}, u32[]{:S(2)}, u32[]{:S(2)}) collective-permute-start(bf16[128,2048]{0,1:T(8,128)(2,1)} %bitcast.29), channel_id=1, source_target_pairs={{0,116},{2,118},{4,120},{6,122},{8,124},{10,126},{12,0},{14,2},{16... | collective-permute-start | bytes 1572872 | tf_op jit(solution)/shard_map/ppermute | solution.py:12
  666.8 15.6 %collective-permute-start.42 = (bf16[128,2048]{0,1:T(8,128)(2,1)}, bf16[128,2048]{0,1:T(8,128)(2,1)}, u32[]{:S(2)}, u32[]{:S(2)}) collective-permute-start(bf16[128,2048]{0,1:T(8,128)(2,1)} %bitcast.24), channel_id=1, source_target_pairs={{0,126},{2,0},{4,2},{6,4},{8,6},{10,8},{12,10},{14,12},{16,14},{18... | collective-permute-start | bytes 1572872 | tf_op jit(solution)/shard_map/ppermute | solution.py:12
  687.0 9.6 %collective-permute-done.45 = bf16[128,2048]{0,1:T(8,128)(2,1)} collective-permute-done((bf16[128,2048]{0,1:T(8,128)(2,1)}, bf16[128,2048]{0,1:T(8,128)(2,1)}, u32[]{:S(2)}, u32[]{:S(2)}) %collective-permute-start.45) | collective-permute-done | bytes 524320 | tf_op jit(solution)/shard_map/ppermute | solution.py:12
  696.5 16.5 %collective-permute-done.46 = bf16[128,2048]{0,1:T(8,128)(2,1)} collective-permute-done((bf16[128,2048]{0,1:T(8,128)(2,1)}, bf16[128,2048]{0,1:T(8,128)(2,1)}, u32[]{:S(2)}, u32[]{:S(2)}) %collective-permute-start.46) | collective-permute-done | bytes 524320 | tf_op jit(solution)/shard_map/ppermute | solution.py:12
  713.0 11.3 %collective-permute-done.47 = bf16[128,2048]{0,1:T(8,128)(2,1)} collective-permute-done((bf16[128,2048]{0,1:T(8,128)(2,1)}, bf16[128,2048]{0,1:T(8,128)(2,1)}, u32[]{:S(2)}, u32[]{:S(2)}) %collective-permute-start.47) | collective-permute-done | bytes 524320 | tf_op jit(solution)/shard_map/ppermute | solution.py:12
  727.9 24.9 %all-reduce.2.cloned.1.call-done = bf16[32,2048]{1,0:T(8,128)(2,1)} async-done(((bf16[32,2048]{1,0:T(8,128)(2,1)}), bf16[32,2048]{1,0:T(8,128)(2,1)}) %all-reduce.2.cloned.1.call-update) | async-done | bytes 131088 | tf_op jit(solution)/shard_map/psum | solution.py:169
  (344 shorter events, 174.3 us)
Async XLA Ops:
  7.2 382.6 %reduce-scatter.3.cloned.1.call-start = ((), (), s32[]{:S(2)}) async-start(), calls=%async_computation.2 | async-start | bytes 25165824 | tf_op jit(solution)/shard_map/reduce_scatter | solution.py:26
  17.3 668.0 %reduce-scatter.5.cloned.1.call-start = ((), (), s32[]{:S(2)}) async-start(), calls=%async_computation.3 | async-start | bytes 8650752 | tf_op jit(solution)/shard_map/reduce_scatter | solution.py:27
  18.0 36.4 %collective-permute-start.12 = (f32[1,16,128]{2,1,0:T(8,128)S(1)}, f32[1,16,128]{2,1,0:T(8,128)S(1)}, u32[]{:S(2)}, u32[]{:S(2)}) collective-permute-start(f32[1,16,128]{2,1,0:T(8,128)S(1)} %copy-done.63), channel_id=1, source_target_pairs={{0,12},{2,14},{4,16},{6,18},{8,20},{10,22},{12,24},{14,26},{16,28}... | collective-permute-start | bytes 24584 | tf_op jit(solution)/shard_map/ppermute | solution.py:12
  21.6 29.2 %collective-permute-start.11 = (f32[1,16,128]{2,1,0:T(8,128)S(1)}, f32[1,16,128]{2,1,0:T(8,128)S(1)}, u32[]{:S(2)}, u32[]{:S(2)}) collective-permute-start(f32[1,16,128]{2,1,0:T(8,128)S(1)} %copy-done.63), channel_id=1, source_target_pairs={{0,10},{2,12},{4,14},{6,16},{8,18},{10,20},{12,22},{14,24},{16,26}... | collective-permute-start | bytes 24584 | tf_op jit(solution)/shard_map/ppermute | solution.py:12
  23.8 26.9 %collective-permute-start.10 = (f32[1,16,128]{2,1,0:T(8,128)S(1)}, f32[1,16,128]{2,1,0:T(8,128)S(1)}, u32[]{:S(2)}, u32[]{:S(2)}) collective-permute-start(f32[1,16,128]{2,1,0:T(8,128)S(1)} %copy-done.63), channel_id=1, source_target_pairs={{0,8},{2,10},{4,12},{6,14},{8,16},{10,18},{12,20},{14,22},{16,24},... | collective-permute-start | bytes 24584 | tf_op jit(solution)/shard_map/ppermute | solution.py:12
  24.8 25.8 %collective-permute-start.9 = (f32[1,16,128]{2,1,0:T(8,128)S(1)}, f32[1,16,128]{2,1,0:T(8,128)S(1)}, u32[]{:S(2)}, u32[]{:S(2)}) collective-permute-start(f32[1,16,128]{2,1,0:T(8,128)S(1)} %copy-done.63), channel_id=1, source_target_pairs={{0,6},{2,8},{4,10},{6,12},{8,14},{10,16},{12,18},{14,20},{16,22},{... | collective-permute-start | bytes 24584 | tf_op jit(solution)/shard_map/ppermute | solution.py:12
  27.3 15.0 %collective-permute-start.7 = (f32[1,16,128]{2,1,0:T(8,128)S(1)}, f32[1,16,128]{2,1,0:T(8,128)S(1)}, u32[]{:S(2)}, u32[]{:S(2)}) collective-permute-start(f32[1,16,128]{2,1,0:T(8,128)S(1)} %copy-done.63), channel_id=1, source_target_pairs={{0,2},{2,4},{4,6},{6,8},{8,10},{10,12},{12,14},{14,16},{16,18},{18... | collective-permute-start | bytes 24584 | tf_op jit(solution)/shard_map/ppermute | solution.py:12
  42.3 8.3 %collective-permute-start.8 = (f32[1,16,128]{2,1,0:T(8,128)S(1)}, f32[1,16,128]{2,1,0:T(8,128)S(1)}, u32[]{:S(2)}, u32[]{:S(2)}) collective-permute-start(f32[1,16,128]{2,1,0:T(8,128)S(1)} %copy-done.63), channel_id=1, source_target_pairs={{0,4},{2,6},{4,8},{6,10},{8,12},{10,14},{12,16},{14,18},{16,20},{1... | collective-permute-start | bytes 24584 | tf_op jit(solution)/shard_map/ppermute | solution.py:12
  50.6 48.3 %collective-permute-start.1 = (bf16[1,128,2048]{2,1,0:T(8,128)(2,1)S(1)}, bf16[1,128,2048]{2,1,0:T(8,128)(2,1)S(1)}, u32[]{:S(2)}, u32[]{:S(2)}) collective-permute-start(bf16[1,128,2048]{2,1,0:T(8,128)(2,1)S(1)} %copy-done.45), channel_id=1, source_target_pairs={{0,4},{2,6},{4,8},{6,10},{8,12},{10,14},{12,16},{14,18},{16,20},{1... | collective-permute-start | bytes 1572872 | tf_op jit(solution)/shard_map/ppermute | solution.py:12
  50.7 47.3 %collective-permute-start = (bf16[1,128,2048]{2,1,0:T(8,128)(2,1)S(1)}, bf16[1,128,2048]{2,1,0:T(8,128)(2,1)S(1)}, u32[]{:S(2)}, u32[]{:S(2)}) collective-permute-start(bf16[1,128,2048]{2,1,0:T(8,128)(2,1)S(1)} %copy-done.45), channel_id=1, source_target_pairs={{0,2},{2,4},{4,6},{6,8},{8,10},{10,12},{12,14},{14,16},{16,18},{18... | collective-permute-start | bytes 1572872 | tf_op jit(solution)/shard_map/ppermute | solution.py:12
  54.4 19.4 %collective-permute-start.26 = (f32[1,16,128]{2,0,1:T(1,128)S(1)}, f32[1,16,128]{2,0,1:T(1,128)S(1)}, u32[]{:S(2)}, u32[]{:S(2)}) collective-permute-start(f32[1,16,128]{2,0,1:T(1,128)S(1)} %bitcast.283), channel_id=1, source_target_pairs={{0,12},{2,14},{4,16},{6,18},{8,20},{10,22},{12,24},{14,26},{16,28}... | collective-permute-start | bytes 24584 | tf_op jit(solution)/shard_map/ppermute | solution.py:12
  58.2 16.6 %collective-permute-start.25 = (f32[1,16,128]{2,0,1:T(1,128)S(1)}, f32[1,16,128]{2,0,1:T(1,128)S(1)}, u32[]{:S(2)}, u32[]{:S(2)}) collective-permute-start(f32[1,16,128]{2,0,1:T(1,128)S(1)} %bitcast.284), channel_id=1, source_target_pairs={{0,10},{2,12},{4,14},{6,16},{8,18},{10,20},{12,22},{14,24},{16,26}... | collective-permute-start | bytes 24584 | tf_op jit(solution)/shard_map/ppermute | solution.py:12
  58.5 19.9 %collective-permute-start.24 = (f32[1,16,128]{2,0,1:T(1,128)S(1)}, f32[1,16,128]{2,0,1:T(1,128)S(1)}, u32[]{:S(2)}, u32[]{:S(2)}) collective-permute-start(f32[1,16,128]{2,0,1:T(1,128)S(1)} %bitcast.285), channel_id=1, source_target_pairs={{0,8},{2,10},{4,12},{6,14},{8,16},{10,18},{12,20},{14,22},{16,24},... | collective-permute-start | bytes 24584 | tf_op jit(solution)/shard_map/ppermute | solution.py:12
  73.8 9.3 %collective-permute-start.23 = (f32[1,16,128]{2,0,1:T(1,128)S(1)}, f32[1,16,128]{2,0,1:T(1,128)S(1)}, u32[]{:S(2)}, u32[]{:S(2)}) collective-permute-start(f32[1,16,128]{2,0,1:T(1,128)S(1)} %bitcast.286), channel_id=1, source_target_pairs={{0,6},{2,8},{4,10},{6,12},{8,14},{10,16},{12,18},{14,20},{16,22},{... | collective-permute-start | bytes 24584 | tf_op jit(solution)/shard_map/ppermute | solution.py:12
  74.8 26.1 %collective-permute-start.2 = (bf16[1,128,2048]{2,1,0:T(8,128)(2,1)S(1)}, bf16[1,128,2048]{2,1,0:T(8,128)(2,1)S(1)}, u32[]{:S(2)}, u32[]{:S(2)}) collective-permute-start(bf16[1,128,2048]{2,1,0:T(8,128)(2,1)S(1)} %copy-done.45), channel_id=1, source_target_pairs={{0,6},{2,8},{4,10},{6,12},{8,14},{10,16},{12,18},{14,20},{16,22},{... | collective-permute-start | bytes 1572872 | tf_op jit(solution)/shard_map/ppermute | solution.py:12
  78.4 16.9 %collective-permute-start.22 = (f32[1,16,128]{2,0,1:T(1,128)S(1)}, f32[1,16,128]{2,0,1:T(1,128)S(1)}, u32[]{:S(2)}, u32[]{:S(2)}) collective-permute-start(f32[1,16,128]{2,0,1:T(1,128)S(1)} %bitcast.287), channel_id=1, source_target_pairs={{0,4},{2,6},{4,8},{6,10},{8,12},{10,14},{12,16},{14,18},{16,20},{1... | collective-permute-start | bytes 24584 | tf_op jit(solution)/shard_map/ppermute | solution.py:12
  83.7 11.6 %collective-permute-start.21 = (f32[1,16,128]{2,0,1:T(1,128)S(1)}, f32[1,16,128]{2,0,1:T(1,128)S(1)}, u32[]{:S(2)}, u32[]{:S(2)}) collective-permute-start(f32[1,16,128]{2,0,1:T(1,128)S(1)} %bitcast.288), channel_id=1, source_target_pairs={{0,2},{2,4},{4,6},{6,8},{8,10},{10,12},{12,14},{14,16},{16,18},{18... | collective-permute-start | bytes 24584 | tf_op jit(solution)/shard_map/ppermute | solution.py:12
  95.3 171.5 %collective-permute-start.41 = (bf16[1,128,2048]{1,2,0:T(8,128)(2,1)}, bf16[1,128,2048]{1,2,0:T(8,128)(2,1)}, u32[]{:S(2)}, u32[]{:S(2)}) collective-permute-start(bf16[1,128,2048]{1,2,0:T(8,128)(2,1)} %copy.181), channel_id=1, source_target_pairs={{0,112},{2,114},{4,116},{6,118},{8,120},{10,122},{12,124},{14,126}... | collective-permute-start | bytes 1572872 | tf_op jit(solution)/shard_map/ppermute | solution.py:12
  96.5 196.1 %collective-permute-start.39 = (bf16[1,128,2048]{1,2,0:T(8,128)(2,1)}, bf16[1,128,2048]{1,2,0:T(8,128)(2,1)}, u32[]{:S(2)}, u32[]{:S(2)}) collective-permute-start(bf16[1,128,2048]{1,2,0:T(8,128)(2,1)} %copy.181), channel_id=1, source_target_pairs={{0,96},{2,98},{4,100},{6,102},{8,104},{10,106},{12,108},{14,110},{... | collective-permute-start | bytes 1572872 | tf_op jit(solution)/shard_map/ppermute | solution.py:12
  98.0 29.2 %collective-permute-start.3 = (bf16[1,128,2048]{2,1,0:T(8,128)(2,1)S(1)}, bf16[1,128,2048]{2,1,0:T(8,128)(2,1)S(1)}, u32[]{:S(2)}, u32[]{:S(2)}) collective-permute-start(bf16[1,128,2048]{2,1,0:T(8,128)(2,1)S(1)} %copy-done.45), channel_id=1, source_target_pairs={{0,8},{2,10},{4,12},{6,14},{8,16},{10,18},{12,20},{14,22},{16,24},... | collective-permute-start | bytes 1572872 | tf_op jit(solution)/shard_map/ppermute | solution.py:12
  98.9 40.0 %collective-permute-start.4 = (bf16[1,128,2048]{2,1,0:T(8,128)(2,1)S(1)}, bf16[1,128,2048]{2,1,0:T(8,128)(2,1)S(1)}, u32[]{:S(2)}, u32[]{:S(2)}) collective-permute-start(bf16[1,128,2048]{2,1,0:T(8,128)(2,1)S(1)} %copy-done.45), channel_id=1, source_target_pairs={{0,10},{2,12},{4,14},{6,16},{8,18},{10,20},{12,22},{14,24},{16,26}... | collective-permute-start | bytes 1572872 | tf_op jit(solution)/shard_map/ppermute | solution.py:12
  100.8 52.4 %collective-permute-start.5 = (bf16[1,128,2048]{2,1,0:T(8,128)(2,1)S(1)}, bf16[1,128,2048]{2,1,0:T(8,128)(2,1)S(1)}, u32[]{:S(2)}, u32[]{:S(2)}) collective-permute-start(bf16[1,128,2048]{2,1,0:T(8,128)(2,1)S(1)} %copy-done.45), channel_id=1, source_target_pairs={{0,12},{2,14},{4,16},{6,18},{8,20},{10,22},{12,24},{14,26},{16,28}... | collective-permute-start | bytes 1572872 | tf_op jit(solution)/shard_map/ppermute | solution.py:12
  127.2 27.6 %collective-permute-start.6 = (bf16[1,128,2048]{2,1,0:T(8,128)(2,1)S(1)}, bf16[1,128,2048]{2,1,0:T(8,128)(2,1)S(1)}, u32[]{:S(2)}, u32[]{:S(2)}) collective-permute-start(bf16[1,128,2048]{2,1,0:T(8,128)(2,1)S(1)} %copy-done.45), channel_id=1, source_target_pairs={{0,14},{2,16},{4,18},{6,20},{8,22},{10,24},{12,26},{14,28},{16,30}... | collective-permute-start | bytes 1572872 | tf_op jit(solution)/shard_map/ppermute | solution.py:12
  138.8 23.3 %collective-permute-start.14 = (bf16[1,128,2048]{2,1,0:T(8,128)(2,1)S(1)}, bf16[1,128,2048]{2,1,0:T(8,128)(2,1)S(1)}, u32[]{:S(2)}, u32[]{:S(2)}) collective-permute-start(bf16[1,128,2048]{2,1,0:T(8,128)(2,1)S(1)} %bitcast.243), channel_id=1, source_target_pairs={{0,2},{2,4},{4,6},{6,8},{8,10},{10,12},{12,14},{14,16},{16,18},{18... | collective-permute-start | bytes 1572872 | tf_op jit(solution)/shard_map/ppermute | solution.py:12
  153.2 50.9 %collective-permute-start.15 = (bf16[1,128,2048]{2,1,0:T(8,128)(2,1)S(1)}, bf16[1,128,2048]{2,1,0:T(8,128)(2,1)S(1)}, u32[]{:S(2)}, u32[]{:S(2)}) collective-permute-start(bf16[1,128,2048]{2,1,0:T(8,128)(2,1)S(1)} %bitcast.244), channel_id=1, source_target_pairs={{0,4},{2,6},{4,8},{6,10},{8,12},{10,14},{12,16},{14,18},{16,20},{1... | collective-permute-start | bytes 1572872 | tf_op jit(solution)/shard_map/ppermute | solution.py:12
  154.8 50.1 %collective-permute-start.16 = (bf16[1,128,2048]{2,1,0:T(8,128)(2,1)S(1)}, bf16[1,128,2048]{2,1,0:T(8,128)(2,1)S(1)}, u32[]{:S(2)}, u32[]{:S(2)}) collective-permute-start(bf16[1,128,2048]{2,1,0:T(8,128)(2,1)S(1)} %bitcast.245), channel_id=1, source_target_pairs={{0,6},{2,8},{4,10},{6,12},{8,14},{10,16},{12,18},{14,20},{16,22},{... | collective-permute-start | bytes 1572872 | tf_op jit(solution)/shard_map/ppermute | solution.py:12
  162.1 47.1 %collective-permute-start.17 = (bf16[1,128,2048]{2,1,0:T(8,128)(2,1)S(1)}, bf16[1,128,2048]{2,1,0:T(8,128)(2,1)S(1)}, u32[]{:S(2)}, u32[]{:S(2)}) collective-permute-start(bf16[1,128,2048]{2,1,0:T(8,128)(2,1)S(1)} %bitcast.246), channel_id=1, source_target_pairs={{0,8},{2,10},{4,12},{6,14},{8,16},{10,18},{12,20},{14,22},{16,24},... | collective-permute-start | bytes 1572872 | tf_op jit(solution)/shard_map/ppermute | solution.py:12
  204.1 21.9 %collective-permute-start.18 = (bf16[1,128,2048]{2,1,0:T(8,128)(2,1)S(1)}, bf16[1,128,2048]{2,1,0:T(8,128)(2,1)S(1)}, u32[]{:S(2)}, u32[]{:S(2)}) collective-permute-start(bf16[1,128,2048]{2,1,0:T(8,128)(2,1)S(1)} %bitcast.247), channel_id=1, source_target_pairs={{0,10},{2,12},{4,14},{6,16},{8,18},{10,20},{12,22},{14,24},{16,26}... | collective-permute-start | bytes 1572872 | tf_op jit(solution)/shard_map/ppermute | solution.py:12
  204.9 32.0 %collective-permute-start.19 = (bf16[1,128,2048]{2,1,0:T(8,128)(2,1)S(1)}, bf16[1,128,2048]{2,1,0:T(8,128)(2,1)S(1)}, u32[]{:S(2)}, u32[]{:S(2)}) collective-permute-start(bf16[1,128,2048]{2,1,0:T(8,128)(2,1)S(1)} %bitcast.248), channel_id=1, source_target_pairs={{0,12},{2,14},{4,16},{6,18},{8,20},{10,22},{12,24},{14,26},{16,28}... | collective-permute-start | bytes 1572872 | tf_op jit(solution)/shard_map/ppermute | solution.py:12
  209.2 36.0 %collective-permute-start.20 = (bf16[1,128,2048]{2,1,0:T(8,128)(2,1)S(1)}, bf16[1,128,2048]{2,1,0:T(8,128)(2,1)S(1)}, u32[]{:S(2)}, u32[]{:S(2)}) collective-permute-start(bf16[1,128,2048]{2,1,0:T(8,128)(2,1)S(1)} %bitcast.249), channel_id=1, source_target_pairs={{0,14},{2,16},{4,18},{6,20},{8,22},{10,24},{12,26},{14,28},{16,30}... | collective-permute-start | bytes 1572872 | tf_op jit(solution)/shard_map/ppermute | solution.py:12
  226.0 32.3 %collective-permute-start.40 = (bf16[1,128,2048]{1,2,0:T(8,128)(2,1)S(1)}, bf16[1,128,2048]{1,2,0:T(8,128)(2,1)S(1)}, u32[]{:S(2)}, u32[]{:S(2)}) collective-permute-start(bf16[1,128,2048]{1,2,0:T(8,128)(2,1)S(1)} %copy.302), channel_id=1, source_target_pairs={{0,112},{2,114},{4,116},{6,118},{8,120},{10,122},{12,124},{14,126}... | collective-permute-start | bytes 1572872 | tf_op jit(solution)/shard_map/ppermute | solution.py:12
  236.9 80.8 %collective-permute-start.37 = (bf16[1,128,2048]{1,2,0:T(8,128)(2,1)}, bf16[1,128,2048]{1,2,0:T(8,128)(2,1)}, u32[]{:S(2)}, u32[]{:S(2)}) collective-permute-start(bf16[1,128,2048]{1,2,0:T(8,128)(2,1)} %copy.181), channel_id=1, source_target_pairs={{0,80},{2,82},{4,84},{6,86},{8,88},{10,90},{12,92},{14,94},{16,96}... | collective-permute-start | bytes 1572872 | tf_op jit(solution)/shard_map/ppermute | solution.py:12
  245.2 101.2 %collective-permute-start.35 = (bf16[1,128,2048]{1,2,0:T(8,128)(2,1)}, bf16[1,128,2048]{1,2,0:T(8,128)(2,1)}, u32[]{:S(2)}, u32[]{:S(2)}) collective-permute-start(bf16[1,128,2048]{1,2,0:T(8,128)(2,1)} %copy.181), channel_id=1, source_target_pairs={{0,64},{2,66},{4,68},{6,70},{8,72},{10,74},{12,76},{14,78},{16,80}... | collective-permute-start | bytes 1572872 | tf_op jit(solution)/shard_map/ppermute | solution.py:12
  258.4 107.4 %collective-permute-start.33 = (bf16[1,128,2048]{1,2,0:T(8,128)(2,1)}, bf16[1,128,2048]{1,2,0:T(8,128)(2,1)}, u32[]{:S(2)}, u32[]{:S(2)}) collective-permute-start(bf16[1,128,2048]{1,2,0:T(8,128)(2,1)} %copy.181), channel_id=1, source_target_pairs={{0,48},{2,50},{4,52},{6,54},{8,56},{10,58},{12,60},{14,62},{16,64}... | collective-permute-start | bytes 1572872 | tf_op jit(solution)/shard_map/ppermute | solution.py:12
  266.8 13.1 %collective-permute-start.38 = (bf16[1,128,2048]{1,2,0:T(8,128)(2,1)S(1)}, bf16[1,128,2048]{1,2,0:T(8,128)(2,1)S(1)}, u32[]{:S(2)}, u32[]{:S(2)}) collective-permute-start(bf16[1,128,2048]{1,2,0:T(8,128)(2,1)S(1)} %copy.302), channel_id=1, source_target_pairs={{0,96},{2,98},{4,100},{6,102},{8,104},{10,106},{12,108},{14,110},{... | collective-permute-start | bytes 1572872 | tf_op jit(solution)/shard_map/ppermute | solution.py:12
  279.9 110.0 %collective-permute-start.31 = (bf16[1,128,2048]{1,2,0:T(8,128)(2,1)}, bf16[1,128,2048]{1,2,0:T(8,128)(2,1)}, u32[]{:S(2)}, u32[]{:S(2)}) collective-permute-start(bf16[1,128,2048]{1,2,0:T(8,128)(2,1)} %copy.181), channel_id=1, source_target_pairs={{0,32},{2,34},{4,36},{6,38},{8,40},{10,42},{12,44},{14,46},{16,48}... | collective-permute-start | bytes 1572872 | tf_op jit(solution)/shard_map/ppermute | solution.py:12
  292.5 15.2 %collective-permute-start.36 = (bf16[1,128,2048]{1,2,0:T(8,128)(2,1)S(1)}, bf16[1,128,2048]{1,2,0:T(8,128)(2,1)S(1)}, u32[]{:S(2)}, u32[]{:S(2)}) collective-permute-start(bf16[1,128,2048]{1,2,0:T(8,128)(2,1)S(1)} %copy.302), channel_id=1, source_target_pairs={{0,80},{2,82},{4,84},{6,86},{8,88},{10,90},{12,92},{14,94},{16,96}... | collective-permute-start | bytes 1572872 | tf_op jit(solution)/shard_map/ppermute | solution.py:12
  307.8 103.0 %collective-permute-start.29 = (bf16[1,128,2048]{1,2,0:T(8,128)(2,1)}, bf16[1,128,2048]{1,2,0:T(8,128)(2,1)}, u32[]{:S(2)}, u32[]{:S(2)}) collective-permute-start(bf16[1,128,2048]{1,2,0:T(8,128)(2,1)} %copy.181), channel_id=1, source_target_pairs={{0,16},{2,18},{4,20},{6,22},{8,24},{10,26},{12,28},{14,30},{16,32}... | collective-permute-start | bytes 1572872 | tf_op jit(solution)/shard_map/ppermute | solution.py:12
  317.7 19.0 %collective-permute-start.34 = (bf16[1,128,2048]{1,2,0:T(8,128)(2,1)S(1)}, bf16[1,128,2048]{1,2,0:T(8,128)(2,1)S(1)}, u32[]{:S(2)}, u32[]{:S(2)}) collective-permute-start(bf16[1,128,2048]{1,2,0:T(8,128)(2,1)S(1)} %copy.302), channel_id=1, source_target_pairs={{0,64},{2,66},{4,68},{6,70},{8,72},{10,74},{12,76},{14,78},{16,80}... | collective-permute-start | bytes 1572872 | tf_op jit(solution)/shard_map/ppermute | solution.py:12
  336.7 23.4 %collective-permute-start.32 = (bf16[1,128,2048]{1,2,0:T(8,128)(2,1)S(1)}, bf16[1,128,2048]{1,2,0:T(8,128)(2,1)}, u32[]{:S(2)}, u32[]{:S(2)}) collective-permute-start(bf16[1,128,2048]{1,2,0:T(8,128)(2,1)S(1)} %copy.302), channel_id=1, source_target_pairs={{0,48},{2,50},{4,52},{6,54},{8,56},{10,58},{12,60},{14,62},{16,64}... | collective-permute-start | bytes 1572872 | tf_op jit(solution)/shard_map/ppermute | solution.py:12
  346.4 33.1 %collective-permute-start.30 = (bf16[1,128,2048]{1,2,0:T(8,128)(2,1)S(1)}, bf16[1,128,2048]{1,2,0:T(8,128)(2,1)}, u32[]{:S(2)}, u32[]{:S(2)}) collective-permute-start(bf16[1,128,2048]{1,2,0:T(8,128)(2,1)S(1)} %copy.302), channel_id=1, source_target_pairs={{0,32},{2,34},{4,36},{6,38},{8,40},{10,42},{12,44},{14,46},{16,48}... | collective-permute-start | bytes 1572872 | tf_op jit(solution)/shard_map/ppermute | solution.py:12
  360.1 43.7 %collective-permute-start.28 = (bf16[1,128,2048]{1,2,0:T(8,128)(2,1)S(1)}, bf16[1,128,2048]{1,2,0:T(8,128)(2,1)}, u32[]{:S(2)}, u32[]{:S(2)}) collective-permute-start(bf16[1,128,2048]{1,2,0:T(8,128)(2,1)S(1)} %copy.302), channel_id=1, source_target_pairs={{0,16},{2,18},{4,20},{6,22},{8,24},{10,26},{12,28},{14,30},{16,32}... | collective-permute-start | bytes 1572872 | tf_op jit(solution)/shard_map/ppermute | solution.py:12
  365.8 147.9 %collective-permute-start.55 = (bf16[128,2048]{1,0:T(8,128)(2,1)}, bf16[128,2048]{1,0:T(8,128)(2,1)}, u32[]{:S(2)}, u32[]{:S(2)}) collective-permute-start(bf16[128,2048]{1,0:T(8,128)(2,1)} %copy.251), channel_id=1, source_target_pairs={{0,16},{2,18},{4,20},{6,22},{8,24},{10,26},{12,28},{14,30},{16,32}... | collective-permute-start | bytes 1572872 | tf_op jit(solution)/shard_map/ppermute | solution.py:12
  379.6 141.6 %collective-permute-start.62 = (bf16[128,2048]{1,0:T(8,128)(2,1)}, bf16[128,2048]{1,0:T(8,128)(2,1)}, u32[]{:S(2)}, u32[]{:S(2)}) collective-permute-start(bf16[128,2048]{1,0:T(8,128)(2,1)} %copy.267), channel_id=1, source_target_pairs={{0,16},{2,18},{4,20},{6,22},{8,24},{10,26},{12,28},{14,30},{16,32}... | collective-permute-start | bytes 1572872 | tf_op jit(solution)/shard_map/ppermute | solution.py:12
  389.8 363.0 %all-reduce.2.cloned.1.call-start = ((), (), s32[]{:S(2)}) async-start(), calls=%async_computation.4 | async-start | bytes 262144 | tf_op jit(solution)/shard_map/psum | solution.py:169
  389.8 132.9 %collective-permute-start.54 = (bf16[128,2048]{1,0:T(8,128)(2,1)}, bf16[128,2048]{1,0:T(8,128)(2,1)}, u32[]{:S(2)}, u32[]{:S(2)}) collective-permute-start(bf16[128,2048]{1,0:T(8,128)(2,1)} %copy.249), channel_id=1, source_target_pairs={{0,32},{2,34},{4,36},{6,38},{8,40},{10,42},{12,44},{14,46},{16,48}... | collective-permute-start | bytes 1572872 | tf_op jit(solution)/shard_map/ppermute | solution.py:12
  403.7 120.4 %collective-permute-start.61 = (bf16[128,2048]{1,0:T(8,128)(2,1)}, bf16[128,2048]{1,0:T(8,128)(2,1)}, u32[]{:S(2)}, u32[]{:S(2)}) collective-permute-start(bf16[128,2048]{1,0:T(8,128)(2,1)} %copy.265), channel_id=1, source_target_pairs={{0,32},{2,34},{4,36},{6,38},{8,40},{10,42},{12,44},{14,46},{16,48}... | collective-permute-start | bytes 1572872 | tf_op jit(solution)/shard_map/ppermute | solution.py:12
  410.8 115.8 %collective-permute-start.53 = (bf16[128,2048]{1,0:T(8,128)(2,1)}, bf16[128,2048]{1,0:T(8,128)(2,1)}, u32[]{:S(2)}, u32[]{:S(2)}) collective-permute-start(bf16[128,2048]{1,0:T(8,128)(2,1)} %copy.247), channel_id=1, source_target_pairs={{0,48},{2,50},{4,52},{6,54},{8,56},{10,58},{12,60},{14,62},{16,64}... | collective-permute-start | bytes 1572872 | tf_op jit(solution)/shard_map/ppermute | solution.py:12
  513.7 23.4 %collective-permute-start.60 = (bf16[128,2048]{1,0:T(8,128)(2,1)S(1)}, bf16[128,2048]{1,0:T(8,128)(2,1)S(1)}, u32[]{:S(2)}, u32[]{:S(2)}) collective-permute-start(bf16[128,2048]{1,0:T(8,128)(2,1)S(1)} %copy-done.47), channel_id=1, source_target_pairs={{0,48},{2,50},{4,52},{6,54},{8,56},{10,58},{12,60},{14,62},{16,64}... | collective-permute-start | bytes 1572872 | tf_op jit(solution)/shard_map/ppermute | solution.py:12
  521.2 42.7 %collective-permute-start.52 = (bf16[128,2048]{1,0:T(8,128)(2,1)}, bf16[128,2048]{1,0:T(8,128)(2,1)}, u32[]{:S(2)}, u32[]{:S(2)}) collective-permute-start(bf16[128,2048]{1,0:T(8,128)(2,1)} %copy.245), channel_id=1, source_target_pairs={{0,64},{2,66},{4,68},{6,70},{8,72},{10,74},{12,76},{14,78},{16,80}... | collective-permute-start | bytes 1572872 | tf_op jit(solution)/shard_map/ppermute | solution.py:12
  522.7 48.2 %collective-permute-start.59 = (bf16[128,2048]{1,0:T(8,128)(2,1)}, bf16[128,2048]{1,0:T(8,128)(2,1)}, u32[]{:S(2)}, u32[]{:S(2)}) collective-permute-start(bf16[128,2048]{1,0:T(8,128)(2,1)} %copy.261), channel_id=1, source_target_pairs={{0,64},{2,66},{4,68},{6,70},{8,72},{10,74},{12,76},{14,78},{16,80}... | collective-permute-start | bytes 1572872 | tf_op jit(solution)/shard_map/ppermute | solution.py:12
  524.1 67.6 %collective-permute-start.51 = (bf16[128,2048]{1,0:T(8,128)(2,1)}, bf16[128,2048]{1,0:T(8,128)(2,1)}, u32[]{:S(2)}, u32[]{:S(2)}) collective-permute-start(bf16[128,2048]{1,0:T(8,128)(2,1)} %copy.243), channel_id=1, source_target_pairs={{0,80},{2,82},{4,84},{6,86},{8,88},{10,90},{12,92},{14,94},{16,96}... | collective-permute-start | bytes 1572872 | tf_op jit(solution)/shard_map/ppermute | solution.py:12
  526.6 65.2 %collective-permute-start.50 = (bf16[128,2048]{1,0:T(8,128)(2,1)}, bf16[128,2048]{1,0:T(8,128)(2,1)}, u32[]{:S(2)}, u32[]{:S(2)}) collective-permute-start(bf16[128,2048]{1,0:T(8,128)(2,1)} %copy.241), channel_id=1, source_target_pairs={{0,96},{2,98},{4,100},{6,102},{8,104},{10,106},{12,108},{14,110},{... | collective-permute-start | bytes 1572872 | tf_op jit(solution)/shard_map/ppermute | solution.py:12
  537.1 73.3 %collective-permute-start.49 = (bf16[128,2048]{1,0:T(8,128)(2,1)}, bf16[128,2048]{1,0:T(8,128)(2,1)}, u32[]{:S(2)}, u32[]{:S(2)}) collective-permute-start(bf16[128,2048]{1,0:T(8,128)(2,1)} %copy.238), channel_id=1, source_target_pairs={{0,112},{2,114},{4,116},{6,118},{8,120},{10,122},{12,124},{14,126}... | collective-permute-start | bytes 1572872 | tf_op jit(solution)/shard_map/ppermute | solution.py:12
  563.9 80.9 %collective-permute-start.58 = (bf16[128,2048]{1,0:T(8,128)(2,1)}, bf16[128,2048]{1,0:T(8,128)(2,1)S(1)}, u32[]{:S(2)}, u32[]{:S(2)}) collective-permute-start(bf16[128,2048]{1,0:T(8,128)(2,1)} %copy.259), channel_id=1, source_target_pairs={{0,80},{2,82},{4,84},{6,86},{8,88},{10,90},{12,92},{14,94},{16,96}... | collective-permute-start | bytes 1572872 | tf_op jit(solution)/shard_map/ppermute | solution.py:12
  571.0 77.9 %collective-permute-start.57 = (bf16[128,2048]{1,0:T(8,128)(2,1)}, bf16[128,2048]{1,0:T(8,128)(2,1)S(1)}, u32[]{:S(2)}, u32[]{:S(2)}) collective-permute-start(bf16[128,2048]{1,0:T(8,128)(2,1)} %copy.257), channel_id=1, source_target_pairs={{0,96},{2,98},{4,100},{6,102},{8,104},{10,106},{12,108},{14,110},{... | collective-permute-start | bytes 1572872 | tf_op jit(solution)/shard_map/ppermute | solution.py:12
  591.8 60.8 %collective-permute-start.56 = (bf16[128,2048]{1,0:T(8,128)(2,1)}, bf16[128,2048]{1,0:T(8,128)(2,1)S(1)}, u32[]{:S(2)}, u32[]{:S(2)}) collective-permute-start(bf16[128,2048]{1,0:T(8,128)(2,1)} %copy.254), channel_id=1, source_target_pairs={{0,112},{2,114},{4,116},{6,118},{8,120},{10,122},{12,124},{14,126}... | collective-permute-start | bytes 1572872 | tf_op jit(solution)/shard_map/ppermute | solution.py:12
  591.8 63.7 %collective-permute-start.48 = (bf16[128,2048]{0,1:T(8,128)(2,1)}, bf16[128,2048]{0,1:T(8,128)(2,1)}, u32[]{:S(2)}, u32[]{:S(2)}) collective-permute-start(bf16[128,2048]{0,1:T(8,128)(2,1)} %bitcast.258), channel_id=1, source_target_pairs={{0,114},{2,116},{4,118},{6,120},{8,122},{10,124},{12,126},{14,0},{... | collective-permute-start | bytes 1572872 | tf_op jit(solution)/shard_map/ppermute | solution.py:12
  610.4 56.5 %collective-permute-start.43 = (bf16[128,2048]{0,1:T(8,128)(2,1)}, bf16[128,2048]{0,1:T(8,128)(2,1)}, u32[]{:S(2)}, u32[]{:S(2)}) collective-permute-start(bf16[128,2048]{0,1:T(8,128)(2,1)} %bitcast.257), channel_id=1, source_target_pairs={{0,124},{2,126},{4,0},{6,2},{8,4},{10,6},{12,8},{14,10},{16,12},{1... | collective-permute-start | bytes 1572872 | tf_op jit(solution)/shard_map/ppermute | solution.py:12
  644.8 42.2 %collective-permute-start.44 = (bf16[128,2048]{0,1:T(8,128)(2,1)}, bf16[128,2048]{0,1:T(8,128)(2,1)}, u32[]{:S(2)}, u32[]{:S(2)}) collective-permute-start(bf16[128,2048]{0,1:T(8,128)(2,1)} %bitcast.26), channel_id=1, source_target_pairs={{0,122},{2,124},{4,126},{6,0},{8,2},{10,4},{12,6},{14,8},{16,10},{... | collective-permute-start | bytes 1572872 | tf_op jit(solution)/shard_map/ppermute | solution.py:12
  648.9 47.7 %collective-permute-start.45 = (bf16[128,2048]{0,1:T(8,128)(2,1)}, bf16[128,2048]{0,1:T(8,128)(2,1)}, u32[]{:S(2)}, u32[]{:S(2)}) collective-permute-start(bf16[128,2048]{0,1:T(8,128)(2,1)} %bitcast.27), channel_id=1, source_target_pairs={{0,120},{2,122},{4,124},{6,126},{8,0},{10,2},{12,4},{14,6},{16,8},... | collective-permute-start | bytes 1572872 | tf_op jit(solution)/shard_map/ppermute | solution.py:12
  652.5 60.5 %collective-permute-start.46 = (bf16[128,2048]{0,1:T(8,128)(2,1)}, bf16[128,2048]{0,1:T(8,128)(2,1)}, u32[]{:S(2)}, u32[]{:S(2)}) collective-permute-start(bf16[128,2048]{0,1:T(8,128)(2,1)} %bitcast.28), channel_id=1, source_target_pairs={{0,118},{2,120},{4,122},{6,124},{8,126},{10,0},{12,2},{14,4},{16,6... | collective-permute-start | bytes 1572872 | tf_op jit(solution)/shard_map/ppermute | solution.py:12
  655.5 68.8 %collective-permute-start.47 = (bf16[128,2048]{0,1:T(8,128)(2,1)}, bf16[128,2048]{0,1:T(8,128)(2,1)}, u32[]{:S(2)}, u32[]{:S(2)}) collective-permute-start(bf16[128,2048]{0,1:T(8,128)(2,1)} %bitcast.29), channel_id=1, source_target_pairs={{0,116},{2,118},{4,120},{6,122},{8,124},{10,126},{12,0},{14,2},{16... | collective-permute-start | bytes 1572872 | tf_op jit(solution)/shard_map/ppermute | solution.py:12
  666.8 57.5 %collective-permute-start.42 = (bf16[128,2048]{0,1:T(8,128)(2,1)}, bf16[128,2048]{0,1:T(8,128)(2,1)}, u32[]{:S(2)}, u32[]{:S(2)}) collective-permute-start(bf16[128,2048]{0,1:T(8,128)(2,1)} %bitcast.24), channel_id=1, source_target_pairs={{0,126},{2,0},{4,2},{6,4},{8,6},{10,8},{12,10},{14,12},{16,14},{18... | collective-permute-start | bytes 1572872 | tf_op jit(solution)/shard_map/ppermute | solution.py:12
  (71 other events, 638.7 us)
Sparse Core Ops, SparseCore 0:
  17.5 31.3 reduce-scatter.2
  389.9 232.4 reduce-scatter.4
  687.1 65.6 all-reduce.1
where the time goes:
time: 771 us; the launch traced here: 761 us
  matrix products  215 us (28%)
  waiting for transfers between devices  210 us (27%)
  starting transfers between devices  205 us (27%)
  local copies, waits for them, and re-layouts  96.6 us (13%)
  other arithmetic  18.7 us (2%)
  between operations  15.1 us (2%)
    ppermute x63, starting transfers between devices, shifted(): lax.ppermute(shard, axis, [(i, (i + by) % count) for i in range(count)])  205 us
    ppermute x63, waiting for transfers between devices, shifted(): lax.ppermute(shard, axis, [(i, (i + by) % count) for i in range(count)])  185 us
    dot_general x8, matrix products, block_core(): jnp.einsum('ahd,bhd->hab', grad_split, value_heads, preferred_element_typ...  65.8 us
    dot_general x8, matrix products, block_core(): jnp.einsum('hab,bhd->ahd', dscores_low, key_heads, preferred_element_type...  60.9 us
    unnamed x167, local copies, waits for them, and re-layouts  36 us
    dot_general x8, matrix products, block_core(): jnp.einsum('hab,ahd->bhd', probs_low, grad_split, preferred_element_type=...  32.8 us
    dot_general x8, matrix products, block_core(): jnp.einsum('ahd,bhd->hab', query_heads, key_heads, preferred_element_type...  30.8 us
    psum x1, waiting for transfers between devices, per_device(): lax.psum(weight_share.astype(jnp.bfloat16), 'dp').astype(jnp.float32)  24.9 us
  transfers between devices with their start and end apart: 66, of which 21 were waited for; matrix products, arithmetic and copies ran while one was open for 40% of the time, Pallas kernels for 0%

commit v1 on v0

v1 whole, which is shorter than its diff:
```python
import functools

import jax, jax.numpy as jnp
from jax import lax
from jax.experimental import pallas as pl
from jax.experimental.pallas import tpu as pltpu
from jax.sharding import Mesh
from jax.sharding import PartitionSpec as P

LOG2E = 1.4426950408889634


def attn_body(plan, q_rank, k_rank, k_base, q_pos, stats, qd_own, qd_far, kv_own, kv_far,
              dq_own, dq_far, dk_own, dv_own, dkv_far,
              qs, dos, ks, vs, dqs, dks, dvs, *, tq, tk, scaling, dq_form):
    rows = qd_own.shape[0] * 128
    half = rows // 64
    for side, ref in enumerate((qd_own, qd_far)):
        for j in range(half):
            at = pl.ds(pl.multiple_of(q_rank[side * half + j] * 64, 64), 64)
            lo = (j % 2) * 64
            qs[at, :] = ref[j // 2, lo : lo + 64, :]
            dos[at, :] = ref[j // 2, 128 + lo : 192 + lo, :]
    for side, ref in enumerate((kv_own, kv_far)):
        for j in range(half):
            at = pl.ds(pl.multiple_of(k_rank[side * half + j] * 64, 64), 64)
            lo = (j % 2) * 64
            ks[at, :] = ref[j // 2, lo : lo + 64, :]
            vs[at, :] = ref[j // 2, 128 + lo : 192 + lo, :]
    dqs[...] = jnp.zeros_like(dqs)
    n_q = 2 * rows // tq
    n_k = 2 * rows // tk

    def k_step(i, _):
        k_at = pl.ds(pl.multiple_of(i * tk, tk), tk)
        dks[k_at, :] = jnp.zeros((tk, 128), jnp.float32)
        dvs[k_at, :] = jnp.zeros((tk, 128), jnp.float32)

        def tile(j, masked):
            q_at = pl.ds(pl.multiple_of(j * tq, tq), tq)
            k = ks[k_at, :]
            q = qs[q_at, :]
            do = dos[q_at, :]
            nt = (((1,), (1,)), ((), ()))
            s = lax.dot_general(k, q, nt, preferred_element_type=jnp.float32)
            p = jnp.exp2(s * (scaling * LOG2E) - stats[0:1, q_at])
            if masked:
                pos = q_pos[0:1, q_at]
                parts = []
                for b in range(tk // 64):
                    at = k_base[i * (tk // 64) + b] * 64 + lax.broadcasted_iota(jnp.int32, (64, tq), 0)
                    parts.append(jnp.where(at <= pos, p[b * 64 : b * 64 + 64], 0.0))
                p = jnp.concatenate(parts, axis=0)
            dvs[k_at, :] += jnp.dot(p.astype(jnp.bfloat16), do, preferred_element_type=jnp.float32)
            dp = lax.dot_general(vs[k_at, :], do, nt, preferred_element_type=jnp.float32)
            ds = (p * (dp - stats[1:2, q_at])).astype(jnp.bfloat16)
            dks[k_at, :] += jnp.dot(ds, q, preferred_element_type=jnp.float32)
            dqs[q_at, :] += lax.dot_general(ds, k, (((0,), (0,)), ((), ())), preferred_element_type=jnp.float32)
            return 0

        lax.fori_loop(plan[0, i], plan[1, i], lambda j, c: tile(j, True), 0)
        lax.fori_loop(plan[1, i], n_q, lambda j, c: tile(j, False), 0)
        return 0

    lax.fori_loop(0, n_k, k_step, 0)
    for j in range(half):
        own = pl.ds(pl.multiple_of(q_rank[j] * 64, 64), 64)
        far = pl.ds(pl.multiple_of(q_rank[half + j] * 64, 64), 64)
        lo = (j % 2) * 64
        dq_own[j // 2, lo : lo + 64, :] = dqs[own, :] * scaling
        dq_far[j // 2, lo : lo + 64, :] = (dqs[far, :] * scaling).astype(jnp.bfloat16)
        own = pl.ds(pl.multiple_of(k_rank[j] * 64, 64), 64)
        far = pl.ds(pl.multiple_of(k_rank[half + j] * 64, 64), 64)
        dk_own[j // 2, lo : lo + 64, :] = dks[own, :] * scaling
        dv_own[j // 2, lo : lo + 64, :] = dvs[own, :]
        dkv_far[j // 2, lo : lo + 64, :] = (dks[far, :] * scaling).astype(jnp.bfloat16)
        dkv_far[j // 2, 128 + lo : 192 + lo, :] = dvs[far, :].astype(jnp.bfloat16)


def attn(plan, q_rank, k_rank, k_base, q_pos, stats, qd_own, qd_far, kv_own, kv_far, *, tq, tk, scaling, dq_form=0):
    n = qd_own.shape[0]
    rows = 2 * n * 128
    smem = pl.BlockSpec(memory_space=pltpu.SMEM)
    vmem = pl.BlockSpec(memory_space=pltpu.VMEM)
    f32, bf = jnp.float32, jnp.bfloat16
    return pl.pallas_call(
        functools.partial(attn_body, tq=tq, tk=tk, scaling=scaling, dq_form=dq_form),
        in_specs=[smem] * 4 + [vmem] * 6,
        out_specs=[vmem] * 5,
        out_shape=[
            jax.ShapeDtypeStruct((n, 128, 128), f32),
            jax.ShapeDtypeStruct((n, 128, 128), bf),
            jax.ShapeDtypeStruct((n, 128, 128), f32),
            jax.ShapeDtypeStruct((n, 128, 128), f32),
            jax.ShapeDtypeStruct((n, 256, 128), bf),
        ],
        scratch_shapes=[pltpu.VMEM((rows, 128), bf)] * 4 + [pltpu.VMEM((rows, 128), f32)] * 3,
        compiler_params=pltpu.CompilerParams(vmem_limit_bytes=58 * 2**20),
        cost_estimate=pl.CostEstimate(flops=14 * 10**9, bytes_accessed=12 * 2**20, transcendentals=10**7),
        name="attn_grads",
    )(plan, q_rank, k_rank, k_base, q_pos, stats, qd_own, qd_far, kv_own, kv_far)


def tables(q_blocks, k_blocks, tq, tk):
    def ranked(b):
        rank = jnp.sum((b[:, None] > b[None, :]).astype(jnp.int32), axis=1)
        hot = rank[None, :] == jnp.arange(b.shape[0], dtype=jnp.int32)[:, None]
        return rank, hot, jnp.sum(jnp.where(hot, b[None, :], 0), axis=1)
    q_rank, q_hot, q_sorted = ranked(q_blocks)
    k_rank, k_hot, k_sorted = ranked(k_blocks)
    q_max = q_sorted[tq // 64 - 1 :: tq // 64]
    q_min = q_sorted[:: tq // 64]
    k_min = k_sorted[:: tk // 64]
    k_max = k_sorted[tk // 64 - 1 :: tk // 64]
    first = jnp.sum((q_max[None, :] < k_min[:, None]).astype(jnp.int32), axis=1)
    whole = jnp.sum((q_min[None, :] <= k_max[:, None]).astype(jnp.int32), axis=1)
    plan = jnp.stack([first, jnp.maximum(first, whole)])
    q_pos = (q_sorted[:, None] * 64 + jnp.arange(64, dtype=jnp.int32)[None, :]).reshape(1, -1)
    return plan, q_rank, k_rank, k_sorted, q_hot, q_pos


SEQ = ("z", "x", "y", "c")
F32, BF16 = jnp.float32, jnp.bfloat16
TQ, TK = 512, 512


def ring(array, axis, by):
    count = lax.axis_size(axis)
    return lax.ppermute(array, axis, [(i, (i + by) % count) for i in range(count)])


def pick(array, index, axis):
    return lax.dynamic_index_in_dim(array, index, axis, keepdims=False)


def pieces(rows):
    hi = lax.reduce_precision(rows, 8, 7)
    rest = rows - hi
    mid = lax.reduce_precision(rest, 8, 7)
    return [part.astype(BF16) for part in (hi, mid, rest - mid)]


def by_head(array):
    return jnp.transpose(array.reshape(128, 16, 128), (1, 0, 2))


def by_token(array):
    return jnp.transpose(array, (1, 0, 2)).reshape(128, 2048)


def weight_gather(saved, cotangent):
    x, y = lax.axis_index("x"), lax.axis_index("y")
    cols = saved.reshape(128, 2, 4, 256)
    own_cols = [pick(cols, (x + s) % 4, 2).reshape(128, 512) for s in range(4)]
    saved_parts = [own_cols[0]] + [ring(own_cols[s], "x", s) for s in range(1, 4)]
    outs = cotangent.reshape(128, 4, 512)
    own_outs = [pick(outs, (y + s) % 4, 1) for s in range(4)]
    cot_parts = [own_outs[0]] + [ring(own_outs[s], "y", s) for s in range(1, 4)]
    saved_own = jnp.stack(saved_parts)
    cot_own = jnp.stack(cot_parts)
    saved_all = [saved_own] + [ring(saved_own, "y", s) for s in range(1, 4)]
    cot_all = [cot_own] + [ring(cot_own, "x", s) for s in range(1, 4)]
    return saved_all, cot_all


def weight_grad(saved_all, cot_all):
    c = lax.axis_index("c")
    saved_rows = jnp.stack(saved_all).reshape(2048, 512)
    cot_rows = jnp.stack(cot_all, axis=1).reshape(2048, 512)
    block = lax.dot_general(saved_rows, cot_rows, (((0,), (0,)), ((), ())), preferred_element_type=F32)
    block = block.reshape(2, 4, 2, 32, 512)
    other = ring(pick(block, 1 - c, 2).astype(BF16), "c", 1)
    block = pick(block, c, 2) + other.astype(F32)
    sent = jnp.broadcast_to(block.astype(BF16)[:, None], (2, 2, 4, 32, 512)).reshape(16, 32, 512)
    got = lax.all_to_all(sent, ("z", "d", "y"), 0, 0, tiled=True)
    total = jnp.sum(got.reshape(4, 4, 32, 512).astype(F32), axis=0)
    return jnp.transpose(total, (1, 0, 2)).reshape(32, 2048)


def per_device(block_pos, queries, keys, values, attn_out, log_sums, grad_out, out_weight):
    z, c = lax.axis_index("z"), lax.axis_index("c")
    scaling = 128**-0.5
    cotangent, saved = grad_out[0], attn_out[0]
    heads = lax.dot_general(
        cotangent, out_weight, (((1,), (1,)), ((), ())), preferred_element_type=F32
    ).astype(BF16)
    delta = jnp.sum(
        (heads.astype(F32) * saved.astype(F32)).reshape(128, 16, 128), axis=-1
    ).T
    stats = pieces(log_sums[0]) + pieces(delta)
    stats = jnp.pad(jnp.stack(stats, axis=1), ((0, 0), (0, 10), (0, 0)))
    qd = jnp.concatenate([by_head(queries[0]), by_head(heads), stats], axis=1)
    kv = jnp.concatenate([by_head(keys[0]), by_head(values[0])], axis=1)
    qd_own = lax.all_to_all(qd, ("x", "y"), 0, 0, tiled=True)
    qd_far = ring(qd_own, "z", 1)
    kv_own = lax.all_to_all(kv, ("x", "y"), 0, 0, tiled=True)
    kv_far = ring(kv_own, "c", 1)
    saved_all, cot_all = weight_gather(saved, cotangent)

    where = block_pos[0].reshape(2, 16, 2, 2)
    q_blocks = pick(where, c, 2)
    q_blocks = jnp.concatenate([pick(q_blocks, z, 0).reshape(-1), pick(q_blocks, 1 - z, 0).reshape(-1)])
    k_blocks = pick(where, z, 0)
    k_blocks = jnp.concatenate([pick(k_blocks, c, 1).reshape(-1), pick(k_blocks, 1 - c, 1).reshape(-1)])
    plan, q_rank, k_rank, k_base, q_hot, q_pos = tables(q_blocks, k_blocks, TQ, TK)
    raw = jnp.concatenate([qd_own[:, 256:262], qd_far[:, 256:262]]).astype(F32).reshape(32, 2, 3, 2, 64)
    raw = jnp.transpose(jnp.sum(raw, axis=2), (1, 0, 2, 3)).reshape(2, 64, 64)
    rows = jnp.sum(jnp.where(q_hot[None, :, :, None], raw[:, None], 0.0), axis=2).reshape(2, -1)
    rows = jnp.concatenate([rows[:1] * LOG2E, rows[1:]])
    dq_own, dq_far, dk_own, dv_own, dkv_far = attn(
        plan, q_rank, k_rank, k_base, q_pos, rows, qd_own, qd_far, kv_own, kv_far,
        tq=TQ, tk=TK, scaling=scaling,
    )
    dq_got = ring(dq_far, "z", 1)
    dkv_got = ring(dkv_far, "c", 1).astype(F32)
    dkv = jnp.concatenate(
        [(dk_own + dkv_got[:, :128]).astype(BF16), (dv_own + dkv_got[:, 128:]).astype(BF16)], axis=1
    )
    dkv = lax.all_to_all(dkv, ("x", "y"), 0, 0, tiled=True)
    dq = (dq_own + dq_got.astype(F32)).astype(BF16)
    dq = lax.all_to_all(dq, ("x", "y"), 0, 0, tiled=True)
    return (
        by_token(dq)[None],
        by_token(dkv[:, :128])[None],
        by_token(dkv[:, 128:])[None],
        weight_grad(saved_all, cot_all),
    )


def solution(mesh):
    split = Mesh(mesh.devices.reshape(2, 4, 4, 2, 2), ("z", "x", "y", "c", "d"))
    rows = P("d", SEQ, None)
    return jax.shard_map(
        per_device,
        mesh=split,
        in_specs=(P("d", None), rows, rows, rows, rows, P("d", None, SEQ), rows, P()),
        out_specs=(rows, rows, rows, P(SEQ, None)),
        check_vma=False,
    )
```

time: 771 us -> 207 us (0.27)
  matrix products: 215 us -> 9.32 us
  waiting for transfers between devices: 210 us -> 53.8 us
  starting transfers between devices: 205 us -> 57.7 us
  local copies, waits for them, and re-layouts: 96.6 us -> 22.8 us
  Pallas kernels: 0 us -> 41 us
  between operations: 15.1 us -> 1.31 us
    dot_general x41 -> x1, matrix products: 207 us -> 2.83 us  [weight_grad(): lax.dot_general(saved_rows, cot_rows, (((0,), (0,)), ((), ())), preferred...]
    ppermute x63 -> x17, starting transfers between devices: 205 us -> 23.2 us  [ring(): lax.ppermute(array, axis, [(i, (i + by) % count) for i in range(count)])]
    ppermute x63 -> x17, waiting for transfers between devices: 185 us -> 25.1 us  [ring(): lax.ppermute(array, axis, [(i, (i + by) % count) for i in range(count)])]
    pallas_call x0 -> x1, Pallas kernels: none -> 41 us  [attn(): pl.pallas_call(functools.partial(attn_body, tq=tq, tk=tk, scaling=scaling...]
    all_to_all x0 -> x5, starting transfers between devices: none -> 34.5 us  [the longest x1 13.2 us: weight_grad(): got = lax.all_to_all(sent, ('z', 'd', 'y'), 0, 0, tiled=True)]
    unnamed x167 -> x38, local copies, waits for them, and re-layouts: 36 us -> 5.87 us
    all_to_all x0 -> x5, waiting for transfers between devices: none -> 28.7 us  [the longest x1 12.5 us: per_device(): dkv = lax.all_to_all(dkv, ('x', 'y'), 0, 0, tiled=True)]
    convert_element_type x17 -> x2, local copies, waits for them, and re-layouts: 26.9 us -> 0.3 us  [the longest x1 0.27 us: per_device(): heads = lax.dot_general(cotangent, out_weight, (((1,), (1,)), ((), ())),...]
  transfers between devices with their start and end apart: 66 -> 22, of which waited for: 21 -> 8; matrix products, arithmetic and copies ran while one was open for 40% -> 18% of each run, Pallas kernels for 0% -> 0%
where the time goes in v1:
time: 207 us; the launch traced here: 204 us
  starting transfers between devices  57.7 us (28%)
  waiting for transfers between devices  53.8 us (26%)
  Pallas kernels  41 us (20%)
  local copies, waits for them, and re-layouts  22.8 us (11%)
  other arithmetic  18.2 us (9%)
  matrix products  9.32 us (5%)
    pallas_call x1, Pallas kernels, attn(): pl.pallas_call(functools.partial(attn_body, tq=tq, tk=tk, scaling=scaling...  41 us
    ppermute x17, waiting for transfers between devices, ring(): lax.ppermute(array, axis, [(i, (i + by) % count) for i in range(count)])  25.1 us
    ppermute x17, starting transfers between devices, ring(): lax.ppermute(array, axis, [(i, (i + by) % count) for i in range(count)])  23.2 us
    all_to_all x1, starting transfers between devices, weight_grad(): got = lax.all_to_all(sent, ('z', 'd', 'y'), 0, 0, tiled=True)  13.2 us
    all_to_all x1, waiting for transfers between devices, per_device(): dkv = lax.all_to_all(dkv, ('x', 'y'), 0, 0, tiled=True)  12.5 us
    all_to_all x1, waiting for transfers between devices, weight_grad(): got = lax.all_to_all(sent, ('z', 'd', 'y'), 0, 0, tiled=True)  9.96 us
    all_to_all x1, starting transfers between devices, per_device(): qd_own = lax.all_to_all(qd, ('x', 'y'), 0, 0, tiled=True)  7.75 us
    dot_general x1, matrix products, per_device(): lax.dot_general(cotangent, out_weight, (((1,), (1,)), ((), ())), preferre...  6.49 us
  transfers between devices with their start and end apart: 22, of which 8 were waited for; matrix products, arithmetic and copies ran while one was open for 18% of the time, Pallas kernels for 0%

profile of v1, /device:TPU:1, one launch (start us, length us, event | category | flops | bytes accessed | tf_op | source)
XLA Modules:
  0.0 204.1 jit_solution(3988629221285894622)
XLA Ops:
  0.6 0.7 fusion.8
  1.4 6.5 %convolution_convert_fusion = bf16[128,2048]{1,0:T(8,128)(2,1)S(1)} fusion(bf16[2048,2048]{1,0:T(8,128)(2,1)} %param.15, bf16[1,128,2048]{2,1,0:T(8,128)(2,1)} %param.14), kind=kOutput, calls=%fused_computation.1 | convolution fusion | flops 1074003968 | bytes 9437184 | tf_op jit(solution)/shard_map/dot_general | solution.py:184
  8.5 0.3 reduce_sum.99
  10.0 1.1 fusion.1
  11.1 7.8 %all-to-all-start = ((bf16[16,272,128]{2,1,0:T(8,128)(2,1)}), bf16[16,272,128]{2,1,0:T(8,128)(2,1)}, u32[]{:S(2)}, u32[]{:S(2)}) async-start(bf16[16,272,128]{2,1,0:T(8,128)(2,1)} %fusion.1), calls=%async_computation | async-start | bytes 2228224 | tf_op jit(solution)/shard_map/all_to_all | solution.py:194
  19.2 2.6 %collective-permute-start.6 = (bf16[128,512]{0,1:T(8,128)(2,1)S(1)}, bf16[128,512]{0,1:T(8,128)(2,1)S(1)}, u32[]{:S(2)}, u32[]{:S(2)}) collective-permute-start(bf16[128,512]{0,1:T(8,128)(2,1)S(1)} %bitcast.134), channel_id=1, source_target_pairs={{0,48},{16,0},{32,16},{48,32},{1,49},{17,1},{33,17},{49,33},{2,50}... | collective-permute-start | bytes 393224 | tf_op jit(solution)/shard_map/ppermute | solution.py:129
  21.8 0.6 collective-permute-start.5
  22.4 0.6 collective-permute-start.4
  23.4 0.8 copy.254
  24.1 2.4 %collective-permute-start.12 = (bf16[128,512]{1,0:T(8,128)(2,1)}, bf16[128,512]{1,0:T(8,128)(2,1)}, u32[]{:S(2)}, u32[]{:S(2)}) collective-permute-start(bf16[128,512]{1,0:T(8,128)(2,1)} %bitcast.46), channel_id=1, source_target_pairs={{0,12},{4,0},{8,4},{12,8},{1,13},{5,1},{9,5},{13,9},{2,14},{6,2},{... | collective-permute-start | bytes 393224 | tf_op jit(solution)/shard_map/ppermute | solution.py:129
  26.5 0.8 copy.253
  27.3 0.6 collective-permute-start.11
  27.9 0.5 broadcast.70
  28.4 0.7 reduce.15
  30.2 0.7 iota_add_fusion
  31.3 0.8 copy.252
  32.2 2.9 %collective-permute-done.6 = bf16[128,512]{0,1:T(8,128)(2,1)S(1)} collective-permute-done((bf16[128,512]{0,1:T(8,128)(2,1)S(1)}, bf16[128,512]{0,1:T(8,128)(2,1)S(1)}, u32[]{:S(2)}, u32[]{:S(2)}) %collective-permute-start.6) | collective-permute-done | bytes 131104 | tf_op jit(solution)/shard_map/ppermute | solution.py:129
  35.1 1.2 collective-permute-start.10
  36.5 2.2 %collective-permute-done.4 = bf16[128,512]{0,1:T(8,128)(2,1)S(1)} collective-permute-done((bf16[128,512]{0,1:T(8,128)(2,1)S(1)}, bf16[128,512]{0,1:T(8,128)(2,1)S(1)}, u32[]{:S(2)}, u32[]{:S(2)}) %collective-permute-start.4) | collective-permute-done | bytes 131104 | tf_op jit(solution)/shard_map/ppermute | solution.py:129
  38.7 0.7 copy-done.8
  39.4 1.1 fusion.14
  40.4 3.0 %collective-permute-start.9 = (bf16[4,128,512]{1,2,0:T(8,128)(2,1)S(1)}, bf16[4,128,512]{1,2,0:T(8,128)(2,1)}, u32[]{:S(2)}, u32[]{:S(2)}) collective-permute-start(bf16[4,128,512]{1,2,0:T(8,128)(2,1)S(1)} %get-tuple-element.56), channel_id=1, source_target_pairs={{0,12},{4,0},{8,4},{12,8},{1,13},{5,1},{9,5},{13,9},{2,14},{6,2},{... | collective-permute-start | bytes 1572872 | tf_op jit(solution)/shard_map/ppermute | solution.py:129
  43.5 0.4 collective-permute-start.8
  45.2 1.1 pad_maximum_fusion.2
  46.3 4.8 %all-to-all-start.1 = ((bf16[16,256,128]{2,1,0:T(8,128)(2,1)}), bf16[16,256,128]{2,1,0:T(8,128)(2,1)}, u32[]{:S(2)}, u32[]{:S(2)}) async-start(bf16[16,256,128]{2,1,0:T(8,128)(2,1)} %pad_maximum_fusion.2), calls=%async_computation.1 | async-start | bytes 2097152 | tf_op jit(solution)/shard_map/all_to_all | solution.py:196
  51.1 1.4 collective-permute-start.7
  52.5 0.7 add.152.q_pos
  53.3 1.9 fusion.13
  55.2 2.4 %collective-permute-start.15 = (bf16[4,128,512]{2,1,0:T(8,128)(2,1)}, bf16[4,128,512]{2,1,0:T(8,128)(2,1)}, u32[]{:S(2)}, u32[]{:S(2)}) collective-permute-start(bf16[4,128,512]{2,1,0:T(8,128)(2,1)} %get-tuple-element.50), channel_id=1, source_target_pairs={{0,48},{16,0},{32,16},{48,32},{1,49},{17,1},{33,17},{49,33},{2,50}... | collective-permute-start | bytes 1572872 | tf_op jit(solution)/shard_map/ppermute | solution.py:129
  57.6 0.6 collective-permute-start.14
  58.2 0.6 collective-permute-start.13
  58.8 3.6 %collective-permute-start = (bf16[16,272,128]{2,1,0:T(8,128)(2,1)}, bf16[16,272,128]{2,1,0:T(8,128)(2,1)}, u32[]{:S(2)}, u32[]{:S(2)}) collective-permute-start(bf16[16,272,128]{2,1,0:T(8,128)(2,1)} %all-to-all-done.qd_own), channel_id=1, source_target_pairs={{0,64},{64,0},{1,65},{65,1},{2,66},{66,2},{3,67},{67,3},{4,68},{68... | collective-permute-start | bytes 3342344 | tf_op jit(solution)/shard_map/ppermute | solution.py:129
  62.3 0.6 pad_add_fusion.plan
  62.9 18.5 %collective-permute-done.7 = bf16[4,128,512]{1,2,0:T(8,128)(2,1)} collective-permute-done((bf16[4,128,512]{1,2,0:T(8,128)(2,1)S(1)}, bf16[4,128,512]{1,2,0:T(8,128)(2,1)}, u32[]{:S(2)}, u32[]{:S(2)}) %collective-permute-start.7) | collective-permute-done | bytes 524320 | tf_op jit(solution)/shard_map/ppermute | solution.py:129
  81.4 1.6 pad_maximum_fusion
  83.0 2.4 %copy.248 = bf16[4,4,128,512]{3,2,1,0:T(8,128)(2,1)} copy(bf16[4,4,128,512]{2,3,1,0:T(8,128)(2,1)S(1)} %pad_maximum_fusion) | data formatting | bytes 4194304 | tf_op jit(solution)/shard_map/stack | solution.py:168
  85.4 2.9 %copy.249 = bf16[512,2048]{1,0:T(8,128)(2,1)S(1)} copy(bf16[512,2048]{0,1:T(8,128)(2,1)} %bitcast.106) | data formatting | bytes 4194304 | tf_op jit(solution)/shard_map/dot_general | solution.py:170
  88.3 1.6 pad_maximum_fusion.1
  90.0 1.5 copy.255
  91.5 0.9 collective-permute-start.1
  92.4 2.8 %fusion.15 = f32[2,4,2,32,512]{4,3,2,1,0:T(8,128)S(1)} fusion(bf16[2,4,2,32,2048]{4,3,2,1,0:T(8,128)(2,1)S(1)} %bitcast.108, bf16[2048,512,1,1,1]{1,0,4,3,2:T(8,128)(2,1)} %bitcast.109), kind=kOutput, calls=%fused_computation.69 | convolution fusion | flops 1073741824 | bytes 5242880 | tf_op jit(solution)/shard_map/dot_general | solution.py:170
  95.3 0.8 slice.53
  96.1 0.8 slice.54
  97.2 1.1 select_reduce_fusion
  98.5 0.6 pad_maximum_fusion.6.stats
  99.1 41.0 %attn_grads.1 = (f32[16,128,128]{2,1,0:T(8,128)}, bf16[16,128,128]{2,1,0:T(8,128)(2,1)}, f32[16,128,128]{2,1,0:T(8,128)}, f32[16,128,128]{2,1,0:T(8,128)}, bf16[16,256,128]{2,1,0:T(8,128)(2,1)}) custom-call(s32[2,8]{1,0:T(2,128)} %pad_add_fusion.plan, s32[64]{0:T(128)} %copy-done.10, s32[64]{0:T(128)} %copy-done.11, s32[64]{0:T(128)} %copy-done.12, ...), custom_call_target="tpu_custom_call" | custom-call | flops 14000000000 | bytes 12582912 | tf_op jit(solution)/shard_map/attn_grads/pallas_call | solution.py:86
  140.1 0.9 collective-permute-start.3
  141.2 1.4 collective-permute-start.2
  142.6 1.3 collective-permute-done.16
  144.0 0.8 broadcast_in_dim.64
  144.9 13.2 %all-to-all-start.4 = ((bf16[16,32,512]{2,1,0:T(8,128)(2,1)}), bf16[16,32,512]{2,1,0:T(8,128)(2,1)S(1)}, u32[]{:S(2)}, u32[]{:S(2)}) async-start(bf16[16,32,512]{2,1,0:T(8,128)(2,1)} %bitcast.57), calls=%async_computation.4 | async-start | bytes 1048576 | tf_op jit(solution)/shard_map/all_to_all | solution.py:175
  158.2 0.9 add_convert_fusion
  159.1 10.0 %all-to-all-done.4 = bf16[16,32,512]{2,1,0:T(8,128)(2,1)S(1)} async-done(((bf16[16,32,512]{2,1,0:T(8,128)(2,1)}), bf16[16,32,512]{2,1,0:T(8,128)(2,1)S(1)}, u32[]{:S(2)}, u32[]{:S(2)}) %all-to-all-start.4) | async-done | bytes 524320 | tf_op jit(solution)/shard_map/all_to_all | solution.py:175
  169.1 4.3 %all-to-all-start.2 = ((bf16[16,128,128]{2,1,0:T(8,128)(2,1)}), bf16[16,128,128]{2,1,0:T(8,128)(2,1)S(1)}, u32[]{:S(2)}, u32[]{:S(2)}) async-start(bf16[16,128,128]{2,1,0:T(8,128)(2,1)} %add_convert_fusion), calls=%async_computation.2 | async-start | bytes 1048576 | tf_op jit(solution)/shard_map/all_to_all | solution.py:221
  173.3 1.4 convert_element_type.119
  174.8 0.3 fusion.3
  175.1 1.0 pad_maximum_fusion.3
  176.2 6.2 %all-to-all-done.2 = bf16[16,128,128]{2,1,0:T(8,128)(2,1)S(1)} async-done(((bf16[16,128,128]{2,1,0:T(8,128)(2,1)}), bf16[16,128,128]{2,1,0:T(8,128)(2,1)S(1)}, u32[]{:S(2)}, u32[]{:S(2)}) %all-to-all-start.2) | async-done | bytes 524320 | tf_op jit(solution)/shard_map/all_to_all | solution.py:221
  182.3 4.5 %all-to-all-start.3 = ((bf16[16,256,128]{2,1,0:T(8,128)(2,1)}), bf16[16,256,128]{2,1,0:T(8,128)(2,1)S(1)}, u32[]{:S(2)}, u32[]{:S(2)}) async-start(bf16[16,256,128]{2,1,0:T(8,128)(2,1)} %pad_maximum_fusion.3), calls=%async_computation.3 | async-start | bytes 2097152 | tf_op jit(solution)/shard_map/all_to_all | solution.py:219
  186.9 0.7 copy.264
  187.9 1.0 copy.257
  188.9 12.5 %all-to-all-done.3 = bf16[16,256,128]{2,1,0:T(8,128)(2,1)S(1)} async-done(((bf16[16,256,128]{2,1,0:T(8,128)(2,1)}), bf16[16,256,128]{2,1,0:T(8,128)(2,1)S(1)}, u32[]{:S(2)}, u32[]{:S(2)}) %all-to-all-start.3) | async-done | bytes 1048608 | tf_op jit(solution)/shard_map/all_to_all | solution.py:219
  201.8 1.0 copy.258
  203.1 1.0 copy.259
  (97 shorter events, 7.4 us)
Async XLA Ops:
  1.4 6.8 %copy-start.1 = (bf16[1,128,2048]{2,1,0:T(8,128)(2,1)S(1)}, bf16[1,128,2048]{2,1,0:T(8,128)(2,1)}, u32[]{:S(2)}) copy-start(bf16[1,128,2048]{2,1,0:T(8,128)(2,1)} %param.12) | copy-start | bytes 1572868
  8.3 1.0 copy-start.5
  11.1 11.9 %copy-start = (bf16[1,128,2048]{2,1,0:T(8,128)(2,1)S(1)}, bf16[1,128,2048]{2,1,0:T(8,128)(2,1)}, u32[]{:S(2)}) copy-start(bf16[1,128,2048]{2,1,0:T(8,128)(2,1)} %param.14) | copy-start | bytes 1572868
  11.1 35.2 %all-to-all-start = ((bf16[16,272,128]{2,1,0:T(8,128)(2,1)}), bf16[16,272,128]{2,1,0:T(8,128)(2,1)}, u32[]{:S(2)}, u32[]{:S(2)}) async-start(bf16[16,272,128]{2,1,0:T(8,128)(2,1)} %fusion.1), calls=%async_computation | async-start | bytes 2228224 | tf_op jit(solution)/shard_map/all_to_all | solution.py:194
  19.1 9.3 %copy-start.13 = (s32[1,128]{1,0:T(1,128)S(1)}, s32[1,128]{1,0:T(1,128)}, u32[]{:S(2)}) copy-start(s32[1,128]{1,0:T(1,128)} %param.8) | copy-start | bytes 1540
  19.2 15.9 %collective-permute-start.6 = (bf16[128,512]{0,1:T(8,128)(2,1)S(1)}, bf16[128,512]{0,1:T(8,128)(2,1)S(1)}, u32[]{:S(2)}, u32[]{:S(2)}) collective-permute-start(bf16[128,512]{0,1:T(8,128)(2,1)S(1)} %bitcast.134), channel_id=1, source_target_pairs={{0,48},{16,0},{32,16},{48,32},{1,49},{17,1},{33,17},{49,33},{2,50}... | collective-permute-start | bytes 393224 | tf_op jit(solution)/shard_map/ppermute | solution.py:129
  21.8 14.7 %collective-permute-start.5 = (bf16[128,512]{0,1:T(8,128)(2,1)S(1)}, bf16[128,512]{0,1:T(8,128)(2,1)}, u32[]{:S(2)}, u32[]{:S(2)}) collective-permute-start(bf16[128,512]{0,1:T(8,128)(2,1)S(1)} %bitcast.133), channel_id=1, source_target_pairs={{0,32},{16,48},{32,0},{48,16},{1,33},{17,49},{33,1},{49,17},{2,34}... | collective-permute-start | bytes 393224 | tf_op jit(solution)/shard_map/ppermute | solution.py:129
  22.4 16.3 %collective-permute-start.4 = (bf16[128,512]{0,1:T(8,128)(2,1)S(1)}, bf16[128,512]{0,1:T(8,128)(2,1)S(1)}, u32[]{:S(2)}, u32[]{:S(2)}) collective-permute-start(bf16[128,512]{0,1:T(8,128)(2,1)S(1)} %bitcast.132), channel_id=1, source_target_pairs={{0,16},{16,32},{32,48},{48,0},{1,17},{17,33},{33,49},{49,1},{2,18}... | collective-permute-start | bytes 393224 | tf_op jit(solution)/shard_map/ppermute | solution.py:129
  23.3 20.8 %copy-start.6 = (bf16[1,128,2048]{2,1,0:T(8,128)(2,1)S(1)}, bf16[1,128,2048]{2,1,0:T(8,128)(2,1)}, u32[]{:S(2)}) copy-start(bf16[1,128,2048]{2,1,0:T(8,128)(2,1)} %param.11) | copy-start | bytes 1572868
  24.1 26.9 %collective-permute-start.12 = (bf16[128,512]{1,0:T(8,128)(2,1)}, bf16[128,512]{1,0:T(8,128)(2,1)}, u32[]{:S(2)}, u32[]{:S(2)}) collective-permute-start(bf16[128,512]{1,0:T(8,128)(2,1)} %bitcast.46), channel_id=1, source_target_pairs={{0,12},{4,0},{8,4},{12,8},{1,13},{5,1},{9,5},{13,9},{2,14},{6,2},{... | collective-permute-start | bytes 393224 | tf_op jit(solution)/shard_map/ppermute | solution.py:129
  27.3 17.3 %copy-start.7 = (bf16[1,128,2048]{2,1,0:T(8,128)(2,1)S(1)}, bf16[1,128,2048]{2,1,0:T(8,128)(2,1)}, u32[]{:S(2)}) copy-start(bf16[1,128,2048]{2,1,0:T(8,128)(2,1)} %param.10) | copy-start | bytes 1572868
  27.3 26.0 %collective-permute-start.11 = (bf16[128,512]{1,0:T(8,128)(2,1)}, bf16[128,512]{1,0:T(8,128)(2,1)}, u32[]{:S(2)}, u32[]{:S(2)}) collective-permute-start(bf16[128,512]{1,0:T(8,128)(2,1)} %bitcast.44), channel_id=1, source_target_pairs={{0,8},{4,12},{8,0},{12,4},{1,9},{5,13},{9,1},{13,5},{2,10},{6,14},... | collective-permute-start | bytes 393224 | tf_op jit(solution)/shard_map/ppermute | solution.py:129
  29.9 15.0 %copy-start.11 = (s32[64]{0:T(128)}, s32[64]{0:T(128)S(1)}, u32[]{:S(2)}) copy-start(s32[64]{0:T(128)S(1)} %convert_reduce_fusion.2.k_rank) | copy-start | bytes 772
  30.1 14.8 %copy-start.12 = (s32[64]{0:T(128)}, s32[64]{0:T(128)S(1)}, u32[]{:S(2)}) copy-start(s32[64]{0:T(128)S(1)} %get-tuple-element.71.k_base) | copy-start | bytes 772
  30.1 32.9 %copy-start.10 = (s32[64]{0:T(128)}, s32[64]{0:T(128)S(1)}, u32[]{:S(2)}) copy-start(s32[64]{0:T(128)S(1)} %get-tuple-element.72.q_rank) | copy-start | bytes 772
  35.1 18.2 %collective-permute-start.10 = (bf16[128,512]{1,0:T(8,128)(2,1)}, bf16[128,512]{1,0:T(8,128)(2,1)}, u32[]{:S(2)}, u32[]{:S(2)}) collective-permute-start(bf16[128,512]{1,0:T(8,128)(2,1)} %bitcast.42), channel_id=1, source_target_pairs={{0,4},{4,8},{8,12},{12,0},{1,5},{5,9},{9,13},{13,1},{2,6},{6,10},{... | collective-permute-start | bytes 393224 | tf_op jit(solution)/shard_map/ppermute | solution.py:129
  38.7 0.7 copy-start.8
  40.4 17.7 %collective-permute-start.9 = (bf16[4,128,512]{1,2,0:T(8,128)(2,1)S(1)}, bf16[4,128,512]{1,2,0:T(8,128)(2,1)}, u32[]{:S(2)}, u32[]{:S(2)}) collective-permute-start(bf16[4,128,512]{1,2,0:T(8,128)(2,1)S(1)} %get-tuple-element.56), channel_id=1, source_target_pairs={{0,12},{4,0},{8,4},{12,8},{1,13},{5,1},{9,5},{13,9},{2,14},{6,2},{... | collective-permute-start | bytes 1572872 | tf_op jit(solution)/shard_map/ppermute | solution.py:129
  43.5 15.3 %collective-permute-start.8 = (bf16[4,128,512]{1,2,0:T(8,128)(2,1)S(1)}, bf16[4,128,512]{1,2,0:T(8,128)(2,1)}, u32[]{:S(2)}, u32[]{:S(2)}) collective-permute-start(bf16[4,128,512]{1,2,0:T(8,128)(2,1)S(1)} %get-tuple-element.56), channel_id=1, source_target_pairs={{0,8},{4,12},{8,0},{12,4},{1,9},{5,13},{9,1},{13,5},{2,10},{6,14},... | collective-permute-start | bytes 1572872 | tf_op jit(solution)/shard_map/ppermute | solution.py:129
  45.2 7.3 %copy-start.9 = (s32[64,64]{1,0:T(8,128)S(1)}, s32[64,64]{1,0:T(8,128)}, u32[]{:S(2)}) copy-start(s32[64,64]{1,0:T(8,128)} %iota_add_fusion) | copy-start | bytes 49156
  46.3 45.2 %all-to-all-start.1 = ((bf16[16,256,128]{2,1,0:T(8,128)(2,1)}), bf16[16,256,128]{2,1,0:T(8,128)(2,1)}, u32[]{:S(2)}, u32[]{:S(2)}) async-start(bf16[16,256,128]{2,1,0:T(8,128)(2,1)} %pad_maximum_fusion.2), calls=%async_computation.1 | async-start | bytes 2097152 | tf_op jit(solution)/shard_map/all_to_all | solution.py:196
  51.1 30.3 %collective-permute-start.7 = (bf16[4,128,512]{1,2,0:T(8,128)(2,1)S(1)}, bf16[4,128,512]{1,2,0:T(8,128)(2,1)}, u32[]{:S(2)}, u32[]{:S(2)}) collective-permute-start(bf16[4,128,512]{1,2,0:T(8,128)(2,1)S(1)} %get-tuple-element.56), channel_id=1, source_target_pairs={{0,4},{4,8},{8,12},{12,0},{1,5},{5,9},{9,13},{13,1},{2,6},{6,10},{... | collective-permute-start | bytes 1572872 | tf_op jit(solution)/shard_map/ppermute | solution.py:129
  55.2 33.1 %collective-permute-start.15 = (bf16[4,128,512]{2,1,0:T(8,128)(2,1)}, bf16[4,128,512]{2,1,0:T(8,128)(2,1)}, u32[]{:S(2)}, u32[]{:S(2)}) collective-permute-start(bf16[4,128,512]{2,1,0:T(8,128)(2,1)} %get-tuple-element.50), channel_id=1, source_target_pairs={{0,48},{16,0},{32,16},{48,32},{1,49},{17,1},{33,17},{49,33},{2,50}... | collective-permute-start | bytes 1572872 | tf_op jit(solution)/shard_map/ppermute | solution.py:129
  57.6 30.7 %collective-permute-start.14 = (bf16[4,128,512]{2,1,0:T(8,128)(2,1)}, bf16[4,128,512]{2,1,0:T(8,128)(2,1)}, u32[]{:S(2)}, u32[]{:S(2)}) collective-permute-start(bf16[4,128,512]{2,1,0:T(8,128)(2,1)} %get-tuple-element.50), channel_id=1, source_target_pairs={{0,32},{16,48},{32,0},{48,16},{1,33},{17,49},{33,1},{49,17},{2,34}... | collective-permute-start | bytes 1572872 | tf_op jit(solution)/shard_map/ppermute | solution.py:129
  58.2 30.2 %collective-permute-start.13 = (bf16[4,128,512]{2,1,0:T(8,128)(2,1)}, bf16[4,128,512]{2,1,0:T(8,128)(2,1)}, u32[]{:S(2)}, u32[]{:S(2)}) collective-permute-start(bf16[4,128,512]{2,1,0:T(8,128)(2,1)} %get-tuple-element.50), channel_id=1, source_target_pairs={{0,16},{16,32},{32,48},{48,0},{1,17},{17,33},{33,49},{49,1},{2,18}... | collective-permute-start | bytes 1572872 | tf_op jit(solution)/shard_map/ppermute | solution.py:129
  58.8 37.4 %collective-permute-start = (bf16[16,272,128]{2,1,0:T(8,128)(2,1)}, bf16[16,272,128]{2,1,0:T(8,128)(2,1)}, u32[]{:S(2)}, u32[]{:S(2)}) collective-permute-start(bf16[16,272,128]{2,1,0:T(8,128)(2,1)} %all-to-all-done.qd_own), channel_id=1, source_target_pairs={{0,64},{64,0},{1,65},{65,1},{2,66},{66,2},{3,67},{67,3},{4,68},{68... | collective-permute-start | bytes 3342344 | tf_op jit(solution)/shard_map/ppermute | solution.py:129
  91.5 7.6 %collective-permute-start.1 = (bf16[16,256,128]{2,1,0:T(8,128)(2,1)}, bf16[16,256,128]{2,1,0:T(8,128)(2,1)}, u32[]{:S(2)}, u32[]{:S(2)}) collective-permute-start(bf16[16,256,128]{2,1,0:T(8,128)(2,1)} %all-to-all-done.1.kv_own), channel_id=1, source_target_pairs={{0,2},{2,0},{1,3},{3,1},{4,6},{6,4},{5,7},{7,5},{8,10},{10,8},{9,1... | collective-permute-start | bytes 3145736 | tf_op jit(solution)/shard_map/ppermute | solution.py:129
  140.1 18.0 %copy-start.4 = (f32[16,128,128]{2,1,0:T(8,128)S(1)}, f32[16,128,128]{2,1,0:T(8,128)}, u32[]{:S(2)}) copy-start(f32[16,128,128]{2,1,0:T(8,128)} %get-tuple-element.9) | copy-start | bytes 3145732
  140.1 33.2 %collective-permute-start.3 = (bf16[16,256,128]{2,1,0:T(8,128)(2,1)}, bf16[16,256,128]{2,1,0:T(8,128)(2,1)}, u32[]{:S(2)}, u32[]{:S(2)}) collective-permute-start(bf16[16,256,128]{2,1,0:T(8,128)(2,1)} %get-tuple-element.12), channel_id=1, source_target_pairs={{0,2},{2,0},{1,3},{3,1},{4,6},{6,4},{5,7},{7,5},{8,10},{10,8},{9,1... | collective-permute-start | bytes 3145736 | tf_op jit(solution)/shard_map/ppermute | solution.py:129
  141.1 2.8 %collective-permute-start.16 = (bf16[2,4,32,512]{3,2,1,0:T(8,128)(2,1)S(1)}, bf16[2,4,32,512]{3,2,1,0:T(8,128)(2,1)S(1)}, u32[]{:S(2)}, u32[]{:S(2)}) collective-permute-start(bf16[2,4,32,512]{3,2,1,0:T(8,128)(2,1)S(1)} %fusion.7), channel_id=1, source_target_pairs={{0,2},{2,0},{1,3},{3,1},{4,6},{6,4},{5,7},{7,5},{8,10},{10,8},{9,1... | collective-permute-start | bytes 786440 | tf_op jit(solution)/shard_map/ppermute | solution.py:129
  141.2 16.9 %collective-permute-start.2 = (bf16[16,128,128]{2,1,0:T(8,128)(2,1)}, bf16[16,128,128]{2,1,0:T(8,128)(2,1)S(1)}, u32[]{:S(2)}, u32[]{:S(2)}) collective-permute-start(bf16[16,128,128]{2,1,0:T(8,128)(2,1)} %get-tuple-element.10), channel_id=1, source_target_pairs={{0,64},{64,0},{1,65},{65,1},{2,66},{66,2},{3,67},{67,3},{4,68},{68... | collective-permute-start | bytes 1572872 | tf_op jit(solution)/shard_map/ppermute | solution.py:129
  144.9 24.2 %all-to-all-start.4 = ((bf16[16,32,512]{2,1,0:T(8,128)(2,1)}), bf16[16,32,512]{2,1,0:T(8,128)(2,1)S(1)}, u32[]{:S(2)}, u32[]{:S(2)}) async-start(bf16[16,32,512]{2,1,0:T(8,128)(2,1)} %bitcast.57), calls=%async_computation.4 | async-start | bytes 1048576 | tf_op jit(solution)/shard_map/all_to_all | solution.py:175
  159.1 15.7 %copy-start.2 = (f32[16,128,128]{2,1,0:T(8,128)S(1)}, f32[16,128,128]{2,1,0:T(8,128)}, u32[]{:S(2)}) copy-start(f32[16,128,128]{2,1,0:T(8,128)} %get-tuple-element.11) | copy-start | bytes 3145732
  159.1 15.7 %copy-start.3 = (f32[16,128,128]{2,1,0:T(8,128)S(1)}, f32[16,128,128]{2,1,0:T(8,128)}, u32[]{:S(2)}) copy-start(f32[16,128,128]{2,1,0:T(8,128)} %get-tuple-element.13) | copy-start | bytes 3145732
  169.1 13.3 %all-to-all-start.2 = ((bf16[16,128,128]{2,1,0:T(8,128)(2,1)}), bf16[16,128,128]{2,1,0:T(8,128)(2,1)S(1)}, u32[]{:S(2)}, u32[]{:S(2)}) async-start(bf16[16,128,128]{2,1,0:T(8,128)(2,1)} %add_convert_fusion), calls=%async_computation.2 | async-start | bytes 1048576 | tf_op jit(solution)/shard_map/all_to_all | solution.py:221
  182.3 19.1 %all-to-all-start.3 = ((bf16[16,256,128]{2,1,0:T(8,128)(2,1)}), bf16[16,256,128]{2,1,0:T(8,128)(2,1)S(1)}, u32[]{:S(2)}, u32[]{:S(2)}) async-start(bf16[16,256,128]{2,1,0:T(8,128)(2,1)} %pad_maximum_fusion.3), calls=%async_computation.3 | async-start | bytes 2097152 | tf_op jit(solution)/shard_map/all_to_all | solution.py:219

commit v2 on v1

v2 whole, which is shorter than its diff:
```python
import functools

import jax
import jax.numpy as jnp
from jax import lax
from jax.experimental import pallas as pl
from jax.experimental.pallas import tpu as pltpu
from jax.sharding import Mesh
from jax.sharding import PartitionSpec as P

F32, BF16 = jnp.float32, jnp.bfloat16
LOG2E = 1.4426950408889634
NT = (((1,), (1,)), ((), ()))
TN = (((0,), (0,)), ((), ()))
SMEM = pl.BlockSpec(memory_space=pltpu.SMEM)
VMEM = pl.BlockSpec(memory_space=pltpu.VMEM)
HBM = pl.BlockSpec(memory_space=pltpu.HBM)


def like(shape, dtype):
    return jax.ShapeDtypeStruct(shape, dtype)


def pieces(row):
    hi = row.astype(BF16).astype(F32)
    mid = (row - hi).astype(BF16).astype(F32)
    return [hi, mid, row - hi - mid]


def first_body(side, queries, keys, values, saved, cot, packed, part0, part1, part2, part3):
    step = pl.program_id(0)
    for a in range(PACK):
        at = slice(a * 128, a * 128 + 128)
        packed[a, 0:128, :] = queries[:, at]
        packed[a, 128:256, :] = keys[:, at]
        packed[a, 256:384, :] = values[:, at]
    for s, part in enumerate((part0, part1, part2, part3)):
        target = (side[0] + s) % 4

        @pl.when(target // 2 == step)
        def _():
            part[:, 0:1024] = saved[...]

        @pl.when(target % 2 == step)
        def _():
            part[:, 1024:2048] = cot[...]


def second_body(cot, weight, saved, logs, packed):
    step = pl.program_id(0)
    heads = lax.dot_general(cot[...], weight[...], NT, preferred_element_type=F32).astype(BF16)
    delta = heads.astype(F32) * saved[...].astype(F32)
    row_id = lax.broadcasted_iota(jnp.int32, (16, 128), 0)
    for a in range(PACK):
        at = slice(a * 128, a * 128 + 128)
        row = jnp.sum(jnp.transpose(delta[:, at]), axis=0, keepdims=True)
        stats = jnp.zeros((16, 128), F32)
        for i, piece in enumerate(pieces(logs[pl.ds(step * PACK + a, 1), :] * LOG2E) + pieces(row)):
            stats = jnp.where(row_id == i, piece, stats)
        packed[a, 0:128, :] = heads[:, at]
        packed[a, 128:144, :] = stats.astype(BF16)


PACK = 8
WHOLE = pl.BlockSpec((128, 2048), lambda h: (0, 0))
COLUMNS = pl.BlockSpec((128, 128 * PACK), lambda h: (0, h))


def pack_first(side, queries, keys, values, saved, cot):
    return pl.pallas_call(
        first_body,
        grid=(16 // PACK,),
        in_specs=[SMEM] + [COLUMNS] * 5,
        out_specs=[pl.BlockSpec((PACK, 384, 128), lambda h: (h, 0, 0))] + [WHOLE] * 4,
        out_shape=[like((16, 384, 128), BF16)] + [like((128, 2048), BF16)] * 4,
        compiler_params=pltpu.CompilerParams(vmem_limit_bytes=60 * 2**20),
        name="pack_first",
    )(side, queries, keys, values, saved, cot)


def pack_second(cot, weight, saved, logs):
    return pl.pallas_call(
        second_body,
        grid=(16 // PACK,),
        in_specs=[WHOLE, pl.BlockSpec((128 * PACK, 2048), lambda h: (h, 0)), COLUMNS,
                  pl.BlockSpec((16, 128), lambda h: (0, 0))],
        out_specs=pl.BlockSpec((PACK, 144, 128), lambda h: (h, 0, 0)),
        out_shape=like((16, 144, 128), BF16),
        compiler_params=pltpu.CompilerParams(vmem_limit_bytes=40 * 2**20),
        name="pack_second",
    )(cot, weight, saved, logs)


def sort_rows(rank, base, count, pairs):
    for j in range(count):
        at = pl.ds(pl.multiple_of(rank[base + j] * 64, 64), 64)
        for src, lo, dst in pairs:
            lo += (j % 2) * 64
            dst[at, :] = src[j // 2, lo : lo + 64, :]


def place_stats(q_rank, qd, stats_s):
    low = lax.broadcasted_iota(jnp.int32, (1, 128), 1) < 64
    for j in range(16):
        raw = qd[j, 128:144, :].astype(F32)
        for kind in range(2):
            row = raw[3 * kind : 3 * kind + 1] + raw[3 * kind + 1 : 3 * kind + 2] + raw[3 * kind + 2 : 3 * kind + 3]
            turned = pltpu.roll(row, 64, 1)
            for sub in range(2):
                r = q_rank[2 * j + sub]
                upper = r % 2
                value = jnp.where(upper == sub, row, turned)
                at = pl.ds(r // 2, 1)
                keep = jnp.logical_xor(low, upper == 1)
                stats_s[kind, at, :] = jnp.where(keep, value, stats_s[kind, at, :])


def tiles(plan, q_base, k_base, qs, dos, ks, vs, stats_s, dqs, dks, dvs, tq, tk, scaling, start, finish):
    n_q = qs.shape[0] // tq
    n_k = ks.shape[0] // tk
    lane = lax.broadcasted_iota(jnp.int32, (1, 128), 1)

    def k_step(i, _):
        k_at = pl.ds(pl.multiple_of(i * tk, tk), tk)
        start(i, k_at)

        def tile(j, masked):
            q_at = pl.ds(pl.multiple_of(j * tq, tq), tq)
            spans = range(tq // 128)
            logs = jnp.concatenate([stats_s[0, pl.ds(j * (tq // 128) + a, 1), :] for a in spans], axis=1)
            delta = jnp.concatenate([stats_s[1, pl.ds(j * (tq // 128) + a, 1), :] for a in spans], axis=1)
            k = ks[k_at, :]
            q = qs[q_at, :]
            do = dos[q_at, :]
            s = lax.dot_general(k, q, NT, preferred_element_type=F32)
            p = jnp.exp2(s * (scaling * LOG2E) - logs)
            if masked:
                pos = []
                for a in spans:
                    b = (j * (tq // 128) + a) * 2
                    pos.append(jnp.where(lane < 64, q_base[b] * 64 + lane, q_base[b + 1] * 64 + lane - 64))
                pos = jnp.concatenate(pos, axis=1)
                parts = []
                for b in range(tk // 64):
                    at = k_base[i * (tk // 64) + b] * 64 + lax.broadcasted_iota(jnp.int32, (64, tq), 0)
                    parts.append(jnp.where(at <= pos, p[b * 64 : b * 64 + 64], 0.0))
                p = jnp.concatenate(parts, axis=0)
            dvs[k_at, :] += jnp.dot(p.astype(BF16), do, preferred_element_type=F32)
            dp = lax.dot_general(vs[k_at, :], do, NT, preferred_element_type=F32)
            ds = (p * (dp - delta)).astype(BF16)
            dks[k_at, :] += jnp.dot(ds, q, preferred_element_type=F32)
            dqs[q_at, :] += lax.dot_general(ds, k, TN, preferred_element_type=F32)
            return 0

        lax.fori_loop(plan[0, i], plan[1, i], lambda j, c: tile(j, True), 0)
        lax.fori_loop(plan[1, i], n_q, lambda j, c: tile(j, False), 0)
        finish(i, k_at)
        return 0

    lax.fori_loop(0, n_k, k_step, 0)


def near_body(plan, q_rank, q_base, k_rank, k_base, own, grads, kv_far, dq, dk_out, dv_out,
              qs, dos, ks, vs, stats_s, dqs, dks, dvs, sems, kv_s, fetch_sem, *, tq, tk, scaling):
    fetch = pltpu.make_async_copy(kv_far, kv_s, fetch_sem)
    fetch.start()
    sort_rows(q_rank, 0, 32, [(own, 0, qs), (grads, 0, dos)])
    sort_rows(k_rank, 0, 32, [(own, 128, ks), (own, 256, vs)])
    place_stats(q_rank, grads, stats_s)
    fetch.wait()
    sort_rows(k_rank, 32, 32, [(kv_s, 0, ks), (kv_s, 128, vs)])
    dqs[...] = jnp.zeros_like(dqs)

    def copies(i, k_at):
        return (
            pltpu.make_async_copy(dks.at[k_at, :], dk_out.at[k_at, :], sems.at[0, i]),
            pltpu.make_async_copy(dvs.at[k_at, :], dv_out.at[k_at, :], sems.at[1, i]),
        )

    def start(i, k_at):
        dks[k_at, :] = jnp.zeros((tk, 128), F32)
        dvs[k_at, :] = jnp.zeros((tk, 128), F32)

    def finish(i, k_at):
        for copy in copies(i, k_at):
            copy.start()

    tiles(plan, q_base, k_base, qs, dos, ks, vs, stats_s, dqs, dks, dvs, tq, tk, scaling, start, finish)
    for i in range(4096 // tk):
        for copy in copies(i, pl.ds(i * tk, tk)):
            copy.wait()
    for j in range(32):
        at = pl.ds(pl.multiple_of(q_rank[j] * 64, 64), 64)
        lo = (j % 2) * 64
        dq[j // 2, lo : lo + 64, :] = dqs[at, :] * scaling


def far_body(plan, q_rank, q_base, k_rank, k_base, own, kv_far, q_far, grads, dk_in, dv_in,
             dq_far, dk_own, dv_own, dkv_far,
             qs, dos, ks, vs, stats_s, dqs, dks, dvs, sems, kv_s, fetch_sem, *, tq, tk, scaling):
    def copies(i, k_at):
        return (
            pltpu.make_async_copy(dk_in.at[k_at, :], dks.at[k_at, :], sems.at[0, i]),
            pltpu.make_async_copy(dv_in.at[k_at, :], dvs.at[k_at, :], sems.at[1, i]),
        )

    for i in range(4096 // tk):
        for copy in copies(i, pl.ds(i * tk, tk)):
            copy.start()
    fetch = pltpu.make_async_copy(kv_far, kv_s, fetch_sem)
    fetch.start()
    sort_rows(q_rank, 0, 32, [(q_far, 0, qs), (grads, 0, dos)])
    sort_rows(k_rank, 0, 32, [(own, 128, ks), (own, 256, vs)])
    place_stats(q_rank, grads, stats_s)
    fetch.wait()
    sort_rows(k_rank, 32, 32, [(kv_s, 0, ks), (kv_s, 128, vs)])
    dqs[...] = jnp.zeros_like(dqs)

    def start(i, k_at):
        for copy in copies(i, k_at):
            copy.wait()

    def finish(i, k_at):
        pass

    tiles(plan, q_base, k_base, qs, dos, ks, vs, stats_s, dqs, dks, dvs, tq, tk, scaling, start, finish)
    for j in range(32):
        at = pl.ds(pl.multiple_of(q_rank[j] * 64, 64), 64)
        own_at = pl.ds(pl.multiple_of(k_rank[j] * 64, 64), 64)
        far_at = pl.ds(pl.multiple_of(k_rank[32 + j] * 64, 64), 64)
        lo = (j % 2) * 64
        dq_far[j // 2, lo : lo + 64, :] = (dqs[at, :] * scaling).astype(BF16)
        dk_own[j // 2, lo : lo + 64, :] = dks[own_at, :] * scaling
        dv_own[j // 2, lo : lo + 64, :] = dvs[own_at, :]
        dkv_far[j // 2, lo : lo + 64, :] = (dks[far_at, :] * scaling).astype(BF16)
        dkv_far[j // 2, 128 + lo : 192 + lo, :] = dvs[far_at, :].astype(BF16)


COST = pl.CostEstimate(flops=7 * 10**9, bytes_accessed=12 * 2**20, transcendentals=10**7)
SORTED = [pltpu.VMEM((2048, 128), BF16)] * 2 + [pltpu.VMEM((4096, 128), BF16)] * 2
SORTED += [pltpu.VMEM((2, 16, 128), F32), pltpu.VMEM((2048, 128), F32)]
FETCH = [pltpu.VMEM((16, 256, 128), BF16), pltpu.SemaphoreType.DMA]
TOTALS = [pltpu.VMEM((4096, 128), F32)] * 2


def in_hbm(array):
    return pltpu.with_memory_space_constraint(array, pltpu.HBM)


def attn_near(tables, own, grads, kv_far, tq, tk, scaling):
    return pl.pallas_call(
        functools.partial(near_body, tq=tq, tk=tk, scaling=scaling),
        in_specs=[SMEM] * 5 + [VMEM] * 2 + [HBM],
        out_specs=[VMEM, HBM, HBM],
        out_shape=[like((16, 128, 128), F32)] + [pltpu.HBM((4096, 128), F32)] * 2,
        scratch_shapes=SORTED + TOTALS + [pltpu.SemaphoreType.DMA((2, 4096 // tk))] + FETCH,
        compiler_params=pltpu.CompilerParams(vmem_limit_bytes=28 * 2**20),
        cost_estimate=COST,
        name="attn_near",
    )(*tables, own, grads, in_hbm(kv_far))


def attn_far(tables, own, kv_far, q_far, grads, dk_in, dv_in, tq, tk, scaling):
    return pl.pallas_call(
        functools.partial(far_body, tq=tq, tk=tk, scaling=scaling),
        in_specs=[SMEM] * 5 + [VMEM, HBM, VMEM, VMEM] + [HBM] * 2,
        out_specs=[VMEM] * 4,
        out_shape=[like((16, 128, 128), BF16), like((16, 128, 128), F32), like((16, 128, 128), F32),
                   like((16, 256, 128), BF16)],
        scratch_shapes=SORTED + TOTALS + [pltpu.SemaphoreType.DMA((2, 4096 // tk))] + FETCH,
        compiler_params=pltpu.CompilerParams(vmem_limit_bytes=28 * 2**20),
        cost_estimate=COST,
        name="attn_far",
    )(*tables, own, in_hbm(kv_far), q_far, grads, in_hbm(dk_in), in_hbm(dv_in))


def ranked(blocks):
    rank = jnp.sum((blocks[:, None] > blocks[None, :]).astype(jnp.int32), axis=1)
    hot = rank[None, :] == jnp.arange(blocks.shape[0], dtype=jnp.int32)[:, None]
    return rank, jnp.sum(jnp.where(hot, blocks[None, :], 0), axis=1)


def make_plan(q_sorted, k_sorted, tq, tk):
    q_max = q_sorted[tq // 64 - 1 :: tq // 64]
    q_min = q_sorted[:: tq // 64]
    k_min = k_sorted[:: tk // 64]
    k_max = k_sorted[tk // 64 - 1 :: tk // 64]
    first = jnp.sum((q_max[None, :] < k_min[:, None]).astype(jnp.int32), axis=1)
    whole = jnp.sum((q_min[None, :] <= k_max[:, None]).astype(jnp.int32), axis=1)
    return jnp.stack([first, jnp.maximum(first, whole)])


def weight_body(side, part0, part1, part2, part3, kept, given, total):
    parts = [part[...] for part in (part0, part1, part2, part3)]
    rows = jnp.concatenate([part[:, :1024] for part in parts], axis=0)
    cols = jnp.concatenate([part[:, 1024:] for part in parts], axis=0)
    total[...] = lax.dot_general(rows, cols, TN, preferred_element_type=F32)
    c = side[0]
    for block in range(16):
        mine = pl.ds(pl.multiple_of((block * 2 + c) * 32, 32), 32)
        other = pl.ds(pl.multiple_of((block * 2 + 1 - c) * 32, 32), 32)
        kept[block, :, :] = total[mine, :]
        given[block, :, :] = total[other, :].astype(BF16)


def weight_block(side, parts):
    return pl.pallas_call(
        weight_body,
        grid=(1,),
        in_specs=[SMEM] + [pl.BlockSpec((128, 2048), lambda i: (0, 0))] * 4,
        out_specs=[pl.BlockSpec((16, 32, 1024), lambda i: (0, 0, 0))] * 2,
        out_shape=[pltpu.HBM((16, 32, 1024), F32), like((16, 32, 1024), BF16)],
        scratch_shapes=[pltpu.VMEM((1024, 1024), F32)],
        compiler_params=pltpu.CompilerParams(vmem_limit_bytes=28 * 2**20),
        cost_estimate=pl.CostEstimate(flops=2 * 10**9, bytes_accessed=6 * 2**20, transcendentals=0),
        name="weight_block",
    )(side, *parts)


SEQ = ("z", "x", "y", "c")
TQ, TK = 512, 1024


def ring(array, axis, by):
    count = lax.axis_size(axis)
    return lax.ppermute(array, axis, [(i, (i + by) % count) for i in range(count)])


def pick(array, index, axis):
    return lax.dynamic_index_in_dim(array, index, axis, keepdims=False)


def by_token(array):
    return jnp.transpose(array, (1, 0, 2)).reshape(1, 128, 2048)


def step(block_pos, queries, keys, values, attn_out, log_sums, grad_out, out_weight):
    z, c, d = lax.axis_index("z"), lax.axis_index("c"), lax.axis_index("d")
    scaling = 128**-0.5
    packed, *parts = pack_first((z * 2 + d).reshape(1), queries[0], keys[0], values[0], attn_out[0], grad_out[0])
    own = lax.all_to_all(packed, ("x", "y"), 0, 0, tiled=True)
    parts = parts[:1] + [ring(parts[s], ("z", "d"), s) for s in range(1, 4)]
    packed = pack_second(grad_out[0], out_weight, attn_out[0], log_sums[0])
    grads = lax.all_to_all(packed, ("x", "y"), 0, 0, tiled=True)

    where = block_pos[0].reshape(2, 16, 2, 2)
    q_blocks = pick(where, c, 2)
    k_blocks = pick(where, z, 0)
    k_blocks = jnp.concatenate([pick(k_blocks, c, 1).reshape(-1), pick(k_blocks, 1 - c, 1).reshape(-1)])
    k_rank, k_sorted = ranked(k_blocks)
    tables = []
    for side in (z, 1 - z):
        q_rank, q_sorted = ranked(pick(q_blocks, side, 0).reshape(-1))
        tables.append((make_plan(q_sorted, k_sorted, TQ, TK), q_rank, q_sorted, k_rank, k_sorted))

    kept, given = weight_block(c.reshape(1), parts)
    given = ring(given, "c", 1)
    grads, tables = lax.optimization_barrier((grads, tables))
    kv_far = ring(own[:, 128:], "c", 1)
    q_far = ring(own[:, :128], "z", 1)
    grads_far = ring(grads, "z", 1)
    dq_near, dk_near, dv_near = attn_near(tables[0], own, grads, kv_far, TQ, TK, scaling)
    dk_near, kept, given = lax.optimization_barrier((dk_near, kept, given))
    blocks = (kept + given.astype(F32)).astype(BF16)
    blocks = lax.all_to_all(blocks, ("x", "y"), 0, 0, tiled=True)
    dq_far, dk_own, dv_own, dkv_far = attn_far(
        tables[1], own, kv_far, q_far, grads_far, dk_near, dv_near, TQ, TK, scaling
    )
    dkv_got = ring(dkv_far, "c", 1).astype(F32)
    dq_got = ring(dq_far, "z", 1)
    dkv = jnp.concatenate(
        [(dk_own + dkv_got[:, :128]).astype(BF16), (dv_own + dkv_got[:, 128:]).astype(BF16)], axis=1
    )
    dkv_out = lax.all_to_all(dkv, ("x", "y"), 0, 0, tiled=True)
    blocks, _ = lax.optimization_barrier((blocks, dkv))
    mine = jnp.sum(blocks.astype(F32), axis=0)
    other = ring(mine, "d", 1)
    weight = jnp.where(d == 0, jnp.concatenate([mine, other], axis=1), jnp.concatenate([other, mine], axis=1))

    dq_near, dq_got, _ = lax.optimization_barrier((dq_near, dq_got, dkv))
    dq = (dq_near + dq_got.astype(F32)).astype(BF16)
    dq, dkv_out = lax.optimization_barrier((dq, dkv_out))
    dq_out = lax.all_to_all(dq, ("x", "y"), 0, 0, tiled=True)
    return by_token(dq_out), by_token(dkv_out[:, :128]), by_token(dkv_out[:, 128:]), weight


def solution(mesh):
    split = Mesh(mesh.devices.reshape(2, 4, 4, 2, 2), ("z", "x", "y", "c", "d"))
    rows = P("d", SEQ, None)
    return jax.shard_map(
        step,
        mesh=split,
        in_specs=(P("d", None), rows, rows, rows, rows, P("d", None, SEQ), rows, P()),
        out_specs=(rows, rows, rows, P(SEQ, None)),
        check_vma=False,
    )
```

time: 207 us -> 168 us (0.81)
  the two profiles are of different devices: /device:TPU:1 before, /device:TPU:32 now
where the time goes in v2:
time: 168 us; the launch traced here: 167 us
  Pallas kernels  56.6 us (34%)
  waiting for transfers between devices  46 us (27%)
  starting transfers between devices  39.7 us (24%)
  local copies, waits for them, and re-layouts  13.1 us (8%)
  other arithmetic  10.4 us (6%)
    pallas_call x1, Pallas kernels, attn_far(): pl.pallas_call(functools.partial(far_body, tq=tq, tk=tk, scaling=scaling)...  23.9 us
    pallas_call x1, Pallas kernels, attn_near(): pl.pallas_call(functools.partial(near_body, tq=tq, tk=tk, scaling=scaling...  20.9 us
    all_to_all x1, waiting for transfers between devices, step(): blocks = lax.all_to_all(blocks, ('x', 'y'), 0, 0, tiled=True)  15.9 us
    ppermute x10, starting transfers between devices, ring(): lax.ppermute(array, axis, [(i, (i + by) % count) for i in range(count)])  12.4 us
    ppermute x10, waiting for transfers between devices, ring(): lax.ppermute(array, axis, [(i, (i + by) % count) for i in range(count)])  11.8 us
    unnamed x26, local copies, waits for them, and re-layouts  9.93 us
    all_to_all x1, waiting for transfers between devices, step(): own = lax.all_to_all(packed, ('x', 'y'), 0, 0, tiled=True)  7.86 us
    all_to_all x1, starting transfers between devices, step(): own = lax.all_to_all(packed, ('x', 'y'), 0, 0, tiled=True)  7.18 us
  transfers between devices with their start and end apart: 15, of which 5 were waited for; matrix products, arithmetic and copies ran while one was open for 9% of the time, Pallas kernels for 18%

profile of v2, /device:TPU:32, one launch (start us, length us, event | category | flops | bytes accessed | tf_op | source)
XLA Modules:
  0.0 166.8 jit_solution(17103782057842235078)
XLA Ops:
  0.6 3.6 %pack_first.1 = (bf16[16,384,128]{2,1,0:T(8,128)(2,1)}, bf16[128,2048]{1,0:T(8,128)(2,1)}, bf16[128,2048]{1,0:T(8,128)(2,1)}, bf16[128,2048]{1,0:T(8,128)(2,1)}, bf16[128,2048]{1,0:T(8,128)(2,1)}) custom-call(s32[1]{0:T(128)} %bitcast.7.side, bf16[128,2048]{1,0:T(8,128)(2,1)} %bitcast.33, bf16[128,2048]{1,0:T(8,128)(2,1)} %bitcast.34, ...), custom_call_target="tpu_custom_call" | custom-call | tf_op jit(solution)/shard_map/pack_first/pallas_call | solution.py:70
  4.2 7.2 %all-to-all-start.1 = ((bf16[16,384,128]{2,1,0:T(8,128)(2,1)}), bf16[16,384,128]{2,1,0:T(8,128)(2,1)S(1)}, u32[]{:S(2)}, u32[]{:S(2)}) async-start(bf16[16,384,128]{2,1,0:T(8,128)(2,1)} %get-tuple-element.42), calls=%async_computation.1 | async-start | bytes 3145728 | tf_op jit(solution)/shard_map/all_to_all | solution.py:341
  11.4 2.0 %collective-permute-start.3 = (bf16[128,2048]{1,0:T(8,128)(2,1)}, bf16[128,2048]{1,0:T(8,128)(2,1)S(1)}, u32[]{:S(2)}, u32[]{:S(2)}) collective-permute-start(bf16[128,2048]{1,0:T(8,128)(2,1)} %get-tuple-element.52), channel_id=1, source_target_pairs={{0,1},{1,64},{64,65},{65,0},{2,3},{3,66},{66,67},{67,2},{4,5},{5,6... | collective-permute-start | bytes 1572872 | tf_op jit(solution)/shard_map/ppermute | solution.py:326
  13.4 1.2 collective-permute-start.4
  14.6 2.5 %collective-permute-start.5 = (bf16[128,2048]{1,0:T(8,128)(2,1)}, bf16[128,2048]{1,0:T(8,128)(2,1)}, u32[]{:S(2)}, u32[]{:S(2)}) collective-permute-start(bf16[128,2048]{1,0:T(8,128)(2,1)} %get-tuple-element.54), channel_id=1, source_target_pairs={{0,65},{1,0},{64,1},{65,64},{2,67},{3,2},{66,3},{67,66},{4,69},{5,... | collective-permute-start | bytes 1572872 | tf_op jit(solution)/shard_map/ppermute | solution.py:326
  17.1 0.5 broadcast.23
  17.6 0.7 reduce.15
  18.3 0.2 reshape_squeeze.3
  18.4 0.1 dynamic-slice_reduce_fusion
  18.5 0.1 gt.43
  18.6 0.1 reshape.78
  18.7 0.1 pad_add_fusion.2
  18.8 0.2 convert_reduce_fusion.1.k_rank
  19.0 0.1 select_reduce_fusion.k_base
  19.1 0.1 slice.39
  19.2 0.1 slice.41
  19.3 0.2 convert_reduce_fusion.3.q_rank
  19.5 0.1 select_reduce_fusion.2.q_base
  19.6 0.1 slice.38
  19.7 0.1 slice.40
  19.8 0.1 gt.50
  19.9 3.4 %copy-done = bf16[2048,2048]{1,0:T(8,128)(2,1)S(1)} copy-done((bf16[2048,2048]{1,0:T(8,128)(2,1)S(1)}, bf16[2048,2048]{1,0:T(8,128)(2,1)}, u32[]{:S(2)}) %copy-start) | copy-done | bytes 8388632
  23.3 4.0 %pack_second.1 = bf16[16,144,128]{2,1,0:T(8,128)(2,1)} custom-call(bf16[128,2048]{1,0:T(8,128)(2,1)S(1)} %bitcast.27, bf16[2048,2048]{1,0:T(8,128)(2,1)S(1)} %copy-done, bf16[128,2048]{1,0:T(8,128)(2,1)S(1)} %bitcast.25, f32[16,128]{1,0:T(8,128)S(1)} %bitcast.28), custom_call_target="tpu_custom_call" | custom-call | tf_op jit(solution)/shard_map/pack_second/pallas_call | solution.py:82
  27.3 7.9 %all-to-all-done.1.own = bf16[16,384,128]{2,1,0:T(8,128)(2,1)S(1)} async-done(((bf16[16,384,128]{2,1,0:T(8,128)(2,1)}), bf16[16,384,128]{2,1,0:T(8,128)(2,1)S(1)}, u32[]{:S(2)}, u32[]{:S(2)}) %all-to-all-start.1) | async-done | bytes 1572896 | tf_op jit(solution)/shard_map/all_to_all | solution.py:341
  35.2 3.9 %all-to-all-start = ((bf16[16,144,128]{2,1,0:T(8,128)(2,1)}), bf16[16,144,128]{2,1,0:T(8,128)(2,1)S(1)}, u32[]{:S(2)}, u32[]{:S(2)}) async-start(bf16[16,144,128]{2,1,0:T(8,128)(2,1)} %pack_second.1), calls=%async_computation | async-start | bytes 1179648 | tf_op jit(solution)/shard_map/all_to_all | solution.py:344
  39.1 1.1 slice.50
  40.2 0.2 convert_reduce_fusion.2.q_rank
  40.3 0.1 select_reduce_fusion.1.q_base
  40.5 0.1 slice.42
  40.6 0.1 slice.43
  40.6 0.2 convert_reduce_fusion.5
  40.8 0.2 convert_reduce_fusion.4
  41.1 4.2 %weight_block.1 = (f32[16,32,1024]{2,1,0:T(8,128)}, bf16[16,32,1024]{2,1,0:T(8,128)(2,1)}) custom-call(s32[1]{0:T(128)} %bitcast.11.side, bf16[128,2048]{1,0:T(8,128)(2,1)S(1)} %copy-done.8, bf16[128,2048]{1,0:T(8,128)(2,1)S(1)} %collective-permute-done.3.part1, bf16[128,2048]{1,0:T(8,128)(2,1)} %collective-permute-done.4.part2, ...), custom_call_target="tpu_custom_call" | custom-call | flops 2000000000 | bytes 6291456 | tf_op jit(solution)/shard_map/weight_block/pallas_call | solution.py:307
  45.3 0.5 collective-permute-start.6
  45.8 3.8 %all-to-all-done.grads = bf16[16,144,128]{2,1,0:T(8,128)(2,1)S(1)} async-done(((bf16[16,144,128]{2,1,0:T(8,128)(2,1)}), bf16[16,144,128]{2,1,0:T(8,128)(2,1)S(1)}, u32[]{:S(2)}, u32[]{:S(2)}) %all-to-all-start) | async-done | bytes 589856 | tf_op jit(solution)/shard_map/all_to_all | solution.py:344
  49.7 3.0 %collective-permute-start.2 = (bf16[16,144,128]{2,1,0:T(8,128)(2,1)S(1)}, bf16[16,144,128]{2,1,0:T(8,128)(2,1)S(1)}, u32[]{:S(2)}, u32[]{:S(2)}) collective-permute-start(bf16[16,144,128]{2,1,0:T(8,128)(2,1)S(1)} %all-to-all-done.grads), channel_id=1, source_target_pairs={{0,64},{64,0},{1,65},{65,1},{2,66},{66,2},{3,67},{67,3},{4,68},{68... | collective-permute-start | bytes 1769480 | tf_op jit(solution)/shard_map/ppermute | solution.py:326
  52.7 0.8 collective-permute-start.1
  53.5 20.9 %attn_near.1 = (f32[16,128,128]{2,1,0:T(8,128)S(1)}, f32[4096,128]{1,0:T(8,128)}, f32[4096,128]{1,0:T(8,128)}) custom-call(s32[2,4]{1,0:T(2,128)S(1)} %pad_add_fusion.plan, s32[32]{0:T(128)S(1)} %convert_reduce_fusion.3.q_rank, s32[32]{0:T(128)S(1)} %select_reduce_fusion.2.q_base, s32[64]{0:T(128)S(1)} %convert_reduce_fusion.1.k_rank, ...), custom_call_target="tpu_custom_call" | custom-call | flops 7000000000 | bytes 12582912 | tf_op jit(solution)/shard_map/attn_near/pallas_call | solution.py:251
  74.4 1.0 copy-done.5
  75.4 23.9 %attn_far.1 = (bf16[16,128,128]{2,1,0:T(8,128)(2,1)S(1)}, f32[16,128,128]{2,1,0:T(8,128)S(1)}, f32[16,128,128]{2,1,0:T(8,128)S(1)}, bf16[16,256,128]{2,1,0:T(8,128)(2,1)}) custom-call(s32[2,4]{1,0:T(2,128)S(1)} %pad_add_fusion.1.plan, s32[32]{0:T(128)S(1)} %convert_reduce_fusion.2.q_rank, s32[32]{0:T(128)S(1)} %select_reduce_fusion.1.q_base, ...), custom_call_target="tpu_custom_call" | custom-call | flops 7000000000 | bytes 12582912 | tf_op jit(solution)/shard_map/attn_far/pallas_call | solution.py:264
  99.3 1.0 copy-done.3
  100.3 2.6 %add_convert_fusion = bf16[16,32,1024]{2,1,0:T(8,128)(2,1)} fusion(f32[16,32,1024]{2,1,0:T(8,128)S(1)} %copy-done.9, bf16[16,32,1024]{2,1,0:T(8,128)(2,1)} %collective-permute-done.6), kind=kLoop, calls=%fused_computation.1 | loop fusion | flops 1572864 | bytes 4194304 | tf_op jit(solution)/shard_map/convert_element_type | solution.py:364
  103.0 5.8 %all-to-all-start.4 = ((bf16[16,32,1024]{2,1,0:T(8,128)(2,1)}), bf16[16,32,1024]{2,1,0:T(8,128)(2,1)}, u32[]{:S(2)}, u32[]{:S(2)}) async-start(bf16[16,32,1024]{2,1,0:T(8,128)(2,1)} %add_convert_fusion), calls=%async_computation.4 | async-start | bytes 2097152 | tf_op jit(solution)/shard_map/all_to_all | solution.py:365
  108.8 0.2 convert_element_type.52
  109.0 1.0 copy-done.4
  110.0 0.3 fusion.1
  110.3 1.1 pad_maximum_fusion
  111.3 15.9 %all-to-all-done.4 = bf16[16,32,1024]{2,1,0:T(8,128)(2,1)} async-done(((bf16[16,32,1024]{2,1,0:T(8,128)(2,1)}), bf16[16,32,1024]{2,1,0:T(8,128)(2,1)}, u32[]{:S(2)}, u32[]{:S(2)}) %all-to-all-start.4) | async-done | bytes 1048608 | tf_op jit(solution)/shard_map/all_to_all | solution.py:365
  127.3 3.7 %all-to-all-start.2 = ((bf16[16,256,128]{2,1,0:T(8,128)(2,1)}), bf16[16,256,128]{2,1,0:T(8,128)(2,1)S(1)}, u32[]{:S(2)}, u32[]{:S(2)}) async-start(bf16[16,256,128]{2,1,0:T(8,128)(2,1)} %pad_maximum_fusion), calls=%async_computation.2 | async-start | bytes 2097152 | tf_op jit(solution)/shard_map/all_to_all | solution.py:374
  130.9 1.4 collective-permute-start.7
  132.3 1.4 convert_reduce_fusion
  133.8 1.0 collective-permute-start.9
  134.8 11.8 %collective-permute-done.7 = bf16[16,128,128]{2,1,0:T(8,128)(2,1)} collective-permute-done((bf16[16,128,128]{2,1,0:T(8,128)(2,1)S(1)}, bf16[16,128,128]{2,1,0:T(8,128)(2,1)}, u32[]{:S(2)}, u32[]{:S(2)}) %collective-permute-start.7) | collective-permute-done | bytes 524320 | tf_op jit(solution)/shard_map/ppermute | solution.py:326
  146.5 2.0 %add_convert_fusion.1 = bf16[16,128,128]{2,1,0:T(8,128)(2,1)} fusion(f32[16,128,128]{2,1,0:T(8,128)S(1)} %copy-done.6, bf16[16,128,128]{2,1,0:T(8,128)(2,1)} %collective-permute-done.7), kind=kLoop, calls=%fused_computation.7 | loop fusion | flops 786432 | bytes 2097152 | tf_op jit(solution)/shard_map/convert_element_type | solution.py:381
  148.5 6.9 %all-to-all-start.3 = ((bf16[16,128,128]{2,1,0:T(8,128)(2,1)}), bf16[16,128,128]{2,1,0:T(8,128)(2,1)S(1)}, u32[]{:S(2)}, u32[]{:S(2)}) async-start(bf16[16,128,128]{2,1,0:T(8,128)(2,1)} %add_convert_fusion.1), calls=%async_computation.3 | async-start | bytes 1048576 | tf_op jit(solution)/shard_map/all_to_all | solution.py:383
  155.4 0.7 maximum_select_fusion
  156.1 0.1 slice_bitcast_fusion
  156.2 0.3 copy.19
  156.5 1.0 copy.22
  157.5 0.3 copy.20
  157.8 1.0 copy.23
  158.8 6.6 %all-to-all-done.3 = bf16[16,128,128]{2,1,0:T(8,128)(2,1)S(1)} async-done(((bf16[16,128,128]{2,1,0:T(8,128)(2,1)}), bf16[16,128,128]{2,1,0:T(8,128)(2,1)S(1)}, u32[]{:S(2)}, u32[]{:S(2)}) %all-to-all-start.3) | async-done | bytes 524320 | tf_op jit(solution)/shard_map/all_to_all | solution.py:383
  165.5 0.3 copy.18
  165.8 1.0 copy.21
  (34 shorter events, 0.1 us)
Async XLA Ops:
  4.2 13.4 %copy-start.10 = (s32[1,128]{1,0:T(1,128)S(1)}, s32[1,128]{1,0:T(1,128)}, u32[]{:S(2)}) copy-start(s32[1,128]{1,0:T(1,128)} %param.8) | copy-start | bytes 1540
  4.2 15.7 %copy-start.1 = (bf16[1,128,2048]{2,1,0:T(8,128)(2,1)S(1)}, bf16[1,128,2048]{2,1,0:T(8,128)(2,1)}, u32[]{:S(2)}) copy-start(bf16[1,128,2048]{2,1,0:T(8,128)(2,1)} %param.12) | copy-start | bytes 1572868
  4.2 15.7 %copy-start.2 = (bf16[1,128,2048]{2,1,0:T(8,128)(2,1)S(1)}, bf16[1,128,2048]{2,1,0:T(8,128)(2,1)}, u32[]{:S(2)}) copy-start(bf16[1,128,2048]{2,1,0:T(8,128)(2,1)} %param.14) | copy-start | bytes 1572868
  4.2 15.7 %copy-start.7 = (f32[1,16,128]{2,1,0:T(8,128)S(1)}, f32[1,16,128]{2,1,0:T(8,128)}, u32[]{:S(2)}) copy-start(f32[1,16,128]{2,1,0:T(8,128)} %param.13) | copy-start | bytes 24580
  4.2 31.0 %all-to-all-start.1 = ((bf16[16,384,128]{2,1,0:T(8,128)(2,1)}), bf16[16,384,128]{2,1,0:T(8,128)(2,1)S(1)}, u32[]{:S(2)}, u32[]{:S(2)}) async-start(bf16[16,384,128]{2,1,0:T(8,128)(2,1)} %get-tuple-element.42), calls=%async_computation.1 | async-start | bytes 3145728 | tf_op jit(solution)/shard_map/all_to_all | solution.py:341
  11.4 29.6 %collective-permute-start.3 = (bf16[128,2048]{1,0:T(8,128)(2,1)}, bf16[128,2048]{1,0:T(8,128)(2,1)S(1)}, u32[]{:S(2)}, u32[]{:S(2)}) collective-permute-start(bf16[128,2048]{1,0:T(8,128)(2,1)} %get-tuple-element.52), channel_id=1, source_target_pairs={{0,1},{1,64},{64,65},{65,0},{2,3},{3,66},{66,67},{67,2},{4,5},{5,6... | collective-permute-start | bytes 1572872 | tf_op jit(solution)/shard_map/ppermute | solution.py:326
  13.4 27.6 %collective-permute-start.4 = (bf16[128,2048]{1,0:T(8,128)(2,1)}, bf16[128,2048]{1,0:T(8,128)(2,1)}, u32[]{:S(2)}, u32[]{:S(2)}) collective-permute-start(bf16[128,2048]{1,0:T(8,128)(2,1)} %get-tuple-element.53), channel_id=1, source_target_pairs={{0,64},{1,65},{64,0},{65,1},{2,66},{3,67},{66,2},{67,3},{4,68},{5,... | collective-permute-start | bytes 1572872 | tf_op jit(solution)/shard_map/ppermute | solution.py:326
  14.6 26.5 %collective-permute-start.5 = (bf16[128,2048]{1,0:T(8,128)(2,1)}, bf16[128,2048]{1,0:T(8,128)(2,1)}, u32[]{:S(2)}, u32[]{:S(2)}) collective-permute-start(bf16[128,2048]{1,0:T(8,128)(2,1)} %get-tuple-element.54), channel_id=1, source_target_pairs={{0,65},{1,0},{64,1},{65,64},{2,67},{3,2},{66,3},{67,66},{4,69},{5,... | collective-permute-start | bytes 1572872 | tf_op jit(solution)/shard_map/ppermute | solution.py:326
  19.9 3.4 %copy-start = (bf16[2048,2048]{1,0:T(8,128)(2,1)S(1)}, bf16[2048,2048]{1,0:T(8,128)(2,1)}, u32[]{:S(2)}) copy-start(bf16[2048,2048]{1,0:T(8,128)(2,1)} %weight.1) | copy-start | bytes 25165828
  27.3 13.7 %copy-start.8 = (bf16[128,2048]{1,0:T(8,128)(2,1)S(1)}, bf16[128,2048]{1,0:T(8,128)(2,1)}, u32[]{:S(2)}) copy-start(bf16[128,2048]{1,0:T(8,128)(2,1)} %get-tuple-element.51.part0) | copy-start | bytes 1572868
  35.2 14.4 %all-to-all-start = ((bf16[16,144,128]{2,1,0:T(8,128)(2,1)}), bf16[16,144,128]{2,1,0:T(8,128)(2,1)S(1)}, u32[]{:S(2)}, u32[]{:S(2)}) async-start(bf16[16,144,128]{2,1,0:T(8,128)(2,1)} %pack_second.1), calls=%async_computation | async-start | bytes 1179648 | tf_op jit(solution)/shard_map/all_to_all | solution.py:344
  40.2 13.3 %collective-permute-start = (bf16[16,256,128]{2,1,0:T(8,128)(2,1)}, bf16[16,256,128]{2,1,0:T(8,128)(2,1)}, u32[]{:S(2)}, u32[]{:S(2)}) collective-permute-start(bf16[16,256,128]{2,1,0:T(8,128)(2,1)} %slice.50), channel_id=1, source_target_pairs={{0,2},{2,0},{1,3},{3,1},{4,6},{6,4},{5,7},{7,5},{8,10},{10,8},{9,1... | collective-permute-start | bytes 3145736 | tf_op jit(solution)/shard_map/ppermute | solution.py:326
  45.3 30.1 %collective-permute-start.6 = (bf16[16,32,1024]{2,1,0:T(8,128)(2,1)}, bf16[16,32,1024]{2,1,0:T(8,128)(2,1)}, u32[]{:S(2)}, u32[]{:S(2)}) collective-permute-start(bf16[16,32,1024]{2,1,0:T(8,128)(2,1)} %get-tuple-element.56), channel_id=1, source_target_pairs={{0,2},{2,0},{1,3},{3,1},{4,6},{6,4},{5,7},{7,5},{8,10},{10,8},{9,1... | collective-permute-start | bytes 3145736 | tf_op jit(solution)/shard_map/ppermute | solution.py:326
  49.7 25.8 %collective-permute-start.2 = (bf16[16,144,128]{2,1,0:T(8,128)(2,1)S(1)}, bf16[16,144,128]{2,1,0:T(8,128)(2,1)S(1)}, u32[]{:S(2)}, u32[]{:S(2)}) collective-permute-start(bf16[16,144,128]{2,1,0:T(8,128)(2,1)S(1)} %all-to-all-done.grads), channel_id=1, source_target_pairs={{0,64},{64,0},{1,65},{65,1},{2,66},{66,2},{3,67},{67,3},{4,68},{68... | collective-permute-start | bytes 1769480 | tf_op jit(solution)/shard_map/ppermute | solution.py:326
  52.7 22.7 %collective-permute-start.1 = (bf16[16,128,128]{2,1,0:T(8,128)(2,1)S(1)}, bf16[16,128,128]{2,1,0:T(8,128)(2,1)S(1)}, u32[]{:S(2)}, u32[]{:S(2)}) collective-permute-start(bf16[16,128,128]{2,1,0:T(8,128)(2,1)S(1)} %slice.51), channel_id=1, source_target_pairs={{0,64},{64,0},{1,65},{65,1},{2,66},{66,2},{3,67},{67,3},{4,68},{68... | collective-permute-start | bytes 1572872 | tf_op jit(solution)/shard_map/ppermute | solution.py:326
  74.4 1.0 copy-start.5
  75.4 24.9 %copy-start.9 = (f32[16,32,1024]{2,1,0:T(8,128)S(1)}, f32[16,32,1024]{2,1,0:T(8,128)}, u32[]{:S(2)}) copy-start(f32[16,32,1024]{2,1,0:T(8,128)} %get-tuple-element.67) | copy-start | bytes 6291460
  99.3 1.0 copy-start.3
  100.3 8.4 %collective-permute-start.8 = (bf16[16,256,128]{2,1,0:T(8,128)(2,1)}, bf16[16,256,128]{2,1,0:T(8,128)(2,1)S(1)}, u32[]{:S(2)}, u32[]{:S(2)}) collective-permute-start(bf16[16,256,128]{2,1,0:T(8,128)(2,1)} %get-tuple-element.61), channel_id=1, source_target_pairs={{0,2},{2,0},{1,3},{3,1},{4,6},{6,4},{5,7},{7,5},{8,10},{10,8},{9,1... | collective-permute-start | bytes 3145736 | tf_op jit(solution)/shard_map/ppermute | solution.py:326
  103.0 24.3 %all-to-all-start.4 = ((bf16[16,32,1024]{2,1,0:T(8,128)(2,1)}), bf16[16,32,1024]{2,1,0:T(8,128)(2,1)}, u32[]{:S(2)}, u32[]{:S(2)}) async-start(bf16[16,32,1024]{2,1,0:T(8,128)(2,1)} %add_convert_fusion), calls=%async_computation.4 | async-start | bytes 2097152 | tf_op jit(solution)/shard_map/all_to_all | solution.py:365
  108.7 1.2 copy-start.4
  111.3 35.2 %copy-start.6 = (f32[16,128,128]{2,1,0:T(8,128)S(1)}, f32[16,128,128]{2,1,0:T(8,128)}, u32[]{:S(2)}) copy-start(f32[16,128,128]{2,1,0:T(8,128)} %copy-done.5) | copy-start | bytes 3145732
  127.3 21.2 %all-to-all-start.2 = ((bf16[16,256,128]{2,1,0:T(8,128)(2,1)}), bf16[16,256,128]{2,1,0:T(8,128)(2,1)S(1)}, u32[]{:S(2)}, u32[]{:S(2)}) async-start(bf16[16,256,128]{2,1,0:T(8,128)(2,1)} %pad_maximum_fusion), calls=%async_computation.2 | async-start | bytes 2097152 | tf_op jit(solution)/shard_map/all_to_all | solution.py:374
  130.9 15.6 %collective-permute-start.7 = (bf16[16,128,128]{2,1,0:T(8,128)(2,1)S(1)}, bf16[16,128,128]{2,1,0:T(8,128)(2,1)}, u32[]{:S(2)}, u32[]{:S(2)}) collective-permute-start(bf16[16,128,128]{2,1,0:T(8,128)(2,1)S(1)} %get-tuple-element.59), channel_id=1, source_target_pairs={{0,64},{64,0},{1,65},{65,1},{2,66},{66,2},{3,67},{67,3},{4,68},{68... | collective-permute-start | bytes 1572872 | tf_op jit(solution)/shard_map/ppermute | solution.py:326
  133.8 21.6 %collective-permute-start.9 = (f32[32,1024]{1,0:T(8,128)S(1)}, f32[32,1024]{1,0:T(8,128)S(1)}, u32[]{:S(2)}, u32[]{:S(2)}) collective-permute-start(f32[32,1024]{1,0:T(8,128)S(1)} %convert_reduce_fusion), channel_id=1, source_target_pairs={{0,1},{1,0},{2,3},{3,2},{4,5},{5,4},{6,7},{7,6},{8,9},{9,8},{10,11... | collective-permute-start | bytes 393224 | tf_op jit(solution)/shard_map/ppermute | solution.py:326
  148.5 17.0 %all-to-all-start.3 = ((bf16[16,128,128]{2,1,0:T(8,128)(2,1)}), bf16[16,128,128]{2,1,0:T(8,128)(2,1)S(1)}, u32[]{:S(2)}, u32[]{:S(2)}) async-start(bf16[16,128,128]{2,1,0:T(8,128)(2,1)} %add_convert_fusion.1), calls=%async_computation.3 | async-start | bytes 1048576 | tf_op jit(solution)/shard_map/all_to_all | solution.py:383

commit v3 on v2

--- a/solution.py
+++ b/solution.py
@@ -124,11 +124,14 @@
         k_at = pl.ds(pl.multiple_of(i * tk, tk), tk)
         start(i, k_at)
 
-        def tile(j, masked):
-            q_at = pl.ds(pl.multiple_of(j * tq, tq), tq)
-            spans = range(tq // 128)
-            logs = jnp.concatenate([stats_s[0, pl.ds(j * (tq // 128) + a, 1), :] for a in spans], axis=1)
-            delta = jnp.concatenate([stats_s[1, pl.ds(j * (tq // 128) + a, 1), :] for a in spans], axis=1)
+        def tile(j, masked, k_rows=tk, q_low=0):
+            q_rows = tq - q_low
+            q_at = pl.ds(pl.multiple_of(j * tq + q_low, 128), q_rows)
+            k_at = pl.ds(pl.multiple_of(i * tk, tk), k_rows)
+            first = j * (tq // 128) + q_low // 128
+            spans = range(q_rows // 128)
+            logs = jnp.concatenate([stats_s[0, pl.ds(first + a, 1), :] for a in spans], axis=1)
+            delta = jnp.concatenate([stats_s[1, pl.ds(first + a, 1), :] for a in spans], axis=1)
             k = ks[k_at, :]
             q = qs[q_at, :]
             do = dos[q_at, :]
@@ -137,12 +140,12 @@
             if masked:
                 pos = []
                 for a in spans:
-                    b = (j * (tq // 128) + a) * 2
+                    b = (first + a) * 2
                     pos.append(jnp.where(lane < 64, q_base[b] * 64 + lane, q_base[b + 1] * 64 + lane - 64))
                 pos = jnp.concatenate(pos, axis=1)
                 parts = []
-                for b in range(tk // 64):
-                    at = k_base[i * (tk // 64) + b] * 64 + lax.broadcasted_iota(jnp.int32, (64, tq), 0)
+                for b in range(k_rows // 64):
+                    at = k_base[i * (tk // 64) + b] * 64 + lax.broadcasted_iota(jnp.int32, (64, q_rows), 0)
                     parts.append(jnp.where(at <= pos, p[b * 64 : b * 64 + 64], 0.0))
                 p = jnp.concatenate(parts, axis=0)
             dvs[k_at, :] += jnp.dot(p.astype(BF16), do, preferred_element_type=F32)
@@ -152,7 +155,19 @@
             dqs[q_at, :] += lax.dot_general(ds, k, TN, preferred_element_type=F32)
             return 0
 
-        lax.fori_loop(plan[0, i], plan[1, i], lambda j, c: tile(j, True), 0)
+        def edge(j, _):
+            late = k_base[i * (tk // 64) + tk // 128] > q_base[(j + 1) * (tq // 64) - 1]
+            early = q_base[j * (tq // 64) + tq // 128 - 1] < k_base[i * (tk // 64)]
+            for short in (False, True):
+                for high in (False, True):
+
+                    @pl.when(jnp.logical_and(late == short, early == high))
+                    def _():
+                        tile(j, True, tk // 2 if short else tk, tq // 2 if high else 0)
+
+            return 0
+
+        lax.fori_loop(plan[0, i], plan[1, i], edge, 0)
         lax.fori_loop(plan[1, i], n_q, lambda j, c: tile(j, False), 0)
         finish(i, k_at)
         return 0

time: 168 us -> 166 us (0.988)
  the two profiles are of different devices: /device:TPU:32 before, /device:TPU:0 now
where the time goes in v3:
time: 166 us; the launch traced here: 165 us
  Pallas kernels  52.4 us (32%)
  starting transfers between devices  45.2 us (27%)
  waiting for transfers between devices  43.5 us (26%)
  local copies, waits for them, and re-layouts  13.1 us (8%)
  other arithmetic  10.4 us (6%)
    pallas_call x1, Pallas kernels, attn_near(): pl.pallas_call(functools.partial(near_body, tq=tq, tk=tk, scaling=scaling...  21 us
    pallas_call x1, Pallas kernels, attn_far(): pl.pallas_call(functools.partial(far_body, tq=tq, tk=tk, scaling=scaling)...  19.6 us
    ppermute x10, starting transfers between devices, ring(): lax.ppermute(array, axis, [(i, (i + by) % count) for i in range(count)])  15.4 us
    all_to_all x1, waiting for transfers between devices, step(): blocks = lax.all_to_all(blocks, ('x', 'y'), 0, 0, tiled=True)  15.4 us
    ppermute x10, waiting for transfers between devices, ring(): lax.ppermute(array, axis, [(i, (i + by) % count) for i in range(count)])  10.6 us
    unnamed x26, local copies, waits for them, and re-layouts  9.93 us
    all_to_all x1, starting transfers between devices, step(): blocks = lax.all_to_all(blocks, ('x', 'y'), 0, 0, tiled=True)  8.06 us
    all_to_all x1, starting transfers between devices, step(): own = lax.all_to_all(packed, ('x', 'y'), 0, 0, tiled=True)  7.29 us
  transfers between devices with their start and end apart: 15, of which 5 were waited for; matrix products, arithmetic and copies ran while one was open for 10% of the time, Pallas kernels for 18%

profile of v3, /device:TPU:0, one launch (start us, length us, event | category | flops | bytes accessed | tf_op | source)
XLA Modules:
  0.0 165.4 jit_solution(20393295062133052)
XLA Ops:
  0.6 3.6 %pack_first.1 = (bf16[16,384,128]{2,1,0:T(8,128)(2,1)}, bf16[128,2048]{1,0:T(8,128)(2,1)}, bf16[128,2048]{1,0:T(8,128)(2,1)}, bf16[128,2048]{1,0:T(8,128)(2,1)}, bf16[128,2048]{1,0:T(8,128)(2,1)}) custom-call(s32[1]{0:T(128)} %bitcast.7.side, bf16[128,2048]{1,0:T(8,128)(2,1)} %bitcast.33, bf16[128,2048]{1,0:T(8,128)(2,1)} %bitcast.34, ...), custom_call_target="tpu_custom_call" | custom-call | tf_op jit(solution)/shard_map/pack_first/pallas_call | solution.py:70
  4.2 7.3 %all-to-all-start.1 = ((bf16[16,384,128]{2,1,0:T(8,128)(2,1)}), bf16[16,384,128]{2,1,0:T(8,128)(2,1)S(1)}, u32[]{:S(2)}, u32[]{:S(2)}) async-start(bf16[16,384,128]{2,1,0:T(8,128)(2,1)} %get-tuple-element.42), calls=%async_computation.1 | async-start | bytes 3145728 | tf_op jit(solution)/shard_map/all_to_all | solution.py:356
  11.5 2.0 %collective-permute-start.3 = (bf16[128,2048]{1,0:T(8,128)(2,1)}, bf16[128,2048]{1,0:T(8,128)(2,1)S(1)}, u32[]{:S(2)}, u32[]{:S(2)}) collective-permute-start(bf16[128,2048]{1,0:T(8,128)(2,1)} %get-tuple-element.52), channel_id=1, source_target_pairs={{0,1},{1,64},{64,65},{65,0},{2,3},{3,66},{66,67},{67,2},{4,5},{5,6... | collective-permute-start | bytes 1572872 | tf_op jit(solution)/shard_map/ppermute | solution.py:341
  13.5 3.6 %collective-permute-start.4 = (bf16[128,2048]{1,0:T(8,128)(2,1)}, bf16[128,2048]{1,0:T(8,128)(2,1)}, u32[]{:S(2)}, u32[]{:S(2)}) collective-permute-start(bf16[128,2048]{1,0:T(8,128)(2,1)} %get-tuple-element.53), channel_id=1, source_target_pairs={{0,64},{1,65},{64,0},{65,1},{2,66},{3,67},{66,2},{67,3},{4,68},{5,... | collective-permute-start | bytes 1572872 | tf_op jit(solution)/shard_map/ppermute | solution.py:341
  17.1 1.0 collective-permute-start.5
  18.1 0.5 broadcast.23
  18.6 0.7 reduce.15
  19.3 0.2 reshape_squeeze.3
  19.5 0.1 dynamic-slice_reduce_fusion
  19.5 0.1 gt.43
  19.6 0.1 reshape.78
  19.7 0.1 pad_add_fusion.2
  19.8 0.2 convert_reduce_fusion.1.k_rank
  20.0 0.1 select_reduce_fusion.k_base
  20.1 0.1 slice.39
  20.2 0.1 slice.41
  20.3 0.2 convert_reduce_fusion.3.q_rank
  20.5 0.1 select_reduce_fusion.2.q_base
  20.6 0.1 slice.38
  20.7 0.1 slice.40
  20.8 0.1 gt.50
  20.9 3.4 %copy-done = bf16[2048,2048]{1,0:T(8,128)(2,1)S(1)} copy-done((bf16[2048,2048]{1,0:T(8,128)(2,1)S(1)}, bf16[2048,2048]{1,0:T(8,128)(2,1)}, u32[]{:S(2)}) %copy-start) | copy-done | bytes 8388632
  24.3 4.0 %pack_second.1 = bf16[16,144,128]{2,1,0:T(8,128)(2,1)} custom-call(bf16[128,2048]{1,0:T(8,128)(2,1)S(1)} %bitcast.27, bf16[2048,2048]{1,0:T(8,128)(2,1)S(1)} %copy-done, bf16[128,2048]{1,0:T(8,128)(2,1)S(1)} %bitcast.25, f32[16,128]{1,0:T(8,128)S(1)} %bitcast.28), custom_call_target="tpu_custom_call" | custom-call | tf_op jit(solution)/shard_map/pack_second/pallas_call | solution.py:82
  28.4 7.0 %all-to-all-done.1.own = bf16[16,384,128]{2,1,0:T(8,128)(2,1)S(1)} async-done(((bf16[16,384,128]{2,1,0:T(8,128)(2,1)}), bf16[16,384,128]{2,1,0:T(8,128)(2,1)S(1)}, u32[]{:S(2)}, u32[]{:S(2)}) %all-to-all-start.1) | async-done | bytes 1572896 | tf_op jit(solution)/shard_map/all_to_all | solution.py:356
  35.3 3.9 %all-to-all-start = ((bf16[16,144,128]{2,1,0:T(8,128)(2,1)}), bf16[16,144,128]{2,1,0:T(8,128)(2,1)S(1)}, u32[]{:S(2)}, u32[]{:S(2)}) async-start(bf16[16,144,128]{2,1,0:T(8,128)(2,1)} %pack_second.1), calls=%async_computation | async-start | bytes 1179648 | tf_op jit(solution)/shard_map/all_to_all | solution.py:359
  39.2 1.1 slice.50
  40.3 0.2 convert_reduce_fusion.2.q_rank
  40.5 0.1 select_reduce_fusion.1.q_base
  40.6 0.1 slice.42
  40.7 0.1 slice.43
  40.8 0.2 convert_reduce_fusion.5
  40.9 0.2 convert_reduce_fusion.4
  41.2 4.2 %weight_block.1 = (f32[16,32,1024]{2,1,0:T(8,128)}, bf16[16,32,1024]{2,1,0:T(8,128)(2,1)}) custom-call(s32[1]{0:T(128)} %bitcast.11.side, bf16[128,2048]{1,0:T(8,128)(2,1)S(1)} %copy-done.8, bf16[128,2048]{1,0:T(8,128)(2,1)S(1)} %collective-permute-done.3.part1, bf16[128,2048]{1,0:T(8,128)(2,1)} %collective-permute-done.4.part2, ...), custom_call_target="tpu_custom_call" | custom-call | flops 2000000000 | bytes 6291456 | tf_op jit(solution)/shard_map/weight_block/pallas_call | solution.py:322
  45.4 0.5 collective-permute-start.6
  46.0 3.8 %all-to-all-done.grads = bf16[16,144,128]{2,1,0:T(8,128)(2,1)S(1)} async-done(((bf16[16,144,128]{2,1,0:T(8,128)(2,1)}), bf16[16,144,128]{2,1,0:T(8,128)(2,1)S(1)}, u32[]{:S(2)}, u32[]{:S(2)}) %all-to-all-start) | async-done | bytes 589856 | tf_op jit(solution)/shard_map/all_to_all | solution.py:359
  49.8 3.9 %collective-permute-start.2 = (bf16[16,144,128]{2,1,0:T(8,128)(2,1)S(1)}, bf16[16,144,128]{2,1,0:T(8,128)(2,1)S(1)}, u32[]{:S(2)}, u32[]{:S(2)}) collective-permute-start(bf16[16,144,128]{2,1,0:T(8,128)(2,1)S(1)} %all-to-all-done.grads), channel_id=1, source_target_pairs={{0,64},{64,0},{1,65},{65,1},{2,66},{66,2},{3,67},{67,3},{4,68},{68... | collective-permute-start | bytes 1769480 | tf_op jit(solution)/shard_map/ppermute | solution.py:341
  53.7 0.1 collective-permute-start.1
  53.8 21.0 %attn_near.1 = (f32[16,128,128]{2,1,0:T(8,128)S(1)}, f32[4096,128]{1,0:T(8,128)}, f32[4096,128]{1,0:T(8,128)}) custom-call(s32[2,4]{1,0:T(2,128)S(1)} %pad_add_fusion.plan, s32[32]{0:T(128)S(1)} %convert_reduce_fusion.3.q_rank, s32[32]{0:T(128)S(1)} %select_reduce_fusion.2.q_base, s32[64]{0:T(128)S(1)} %convert_reduce_fusion.1.k_rank, ...), custom_call_target="tpu_custom_call" | custom-call | flops 7000000000 | bytes 12582912 | tf_op jit(solution)/shard_map/attn_near/pallas_call | solution.py:266
  74.8 1.0 copy-done.5
  75.8 19.6 %attn_far.1 = (bf16[16,128,128]{2,1,0:T(8,128)(2,1)S(1)}, f32[16,128,128]{2,1,0:T(8,128)S(1)}, f32[16,128,128]{2,1,0:T(8,128)S(1)}, bf16[16,256,128]{2,1,0:T(8,128)(2,1)}) custom-call(s32[2,4]{1,0:T(2,128)S(1)} %pad_add_fusion.1.plan, s32[32]{0:T(128)S(1)} %convert_reduce_fusion.2.q_rank, s32[32]{0:T(128)S(1)} %select_reduce_fusion.1.q_base, ...), custom_call_target="tpu_custom_call" | custom-call | flops 7000000000 | bytes 12582912 | tf_op jit(solution)/shard_map/attn_far/pallas_call | solution.py:279
  95.4 1.0 copy-done.3
  96.4 2.6 %add_convert_fusion = bf16[16,32,1024]{2,1,0:T(8,128)(2,1)} fusion(f32[16,32,1024]{2,1,0:T(8,128)S(1)} %copy-done.9, bf16[16,32,1024]{2,1,0:T(8,128)(2,1)} %collective-permute-done.6), kind=kLoop, calls=%fused_computation.1 | loop fusion | flops 1572864 | bytes 4194304 | tf_op jit(solution)/shard_map/convert_element_type | solution.py:379
  99.0 8.1 %all-to-all-start.4 = ((bf16[16,32,1024]{2,1,0:T(8,128)(2,1)}), bf16[16,32,1024]{2,1,0:T(8,128)(2,1)}, u32[]{:S(2)}, u32[]{:S(2)}) async-start(bf16[16,32,1024]{2,1,0:T(8,128)(2,1)} %add_convert_fusion), calls=%async_computation.4 | async-start | bytes 2097152 | tf_op jit(solution)/shard_map/all_to_all | solution.py:380
  107.1 0.2 convert_element_type.52
  107.3 1.0 copy-done.4
  108.3 0.3 fusion.1
  108.6 1.1 pad_maximum_fusion
  109.7 15.4 %all-to-all-done.4 = bf16[16,32,1024]{2,1,0:T(8,128)(2,1)} async-done(((bf16[16,32,1024]{2,1,0:T(8,128)(2,1)}), bf16[16,32,1024]{2,1,0:T(8,128)(2,1)}, u32[]{:S(2)}, u32[]{:S(2)}) %all-to-all-start.4) | async-done | bytes 1048608 | tf_op jit(solution)/shard_map/all_to_all | solution.py:380
  125.1 3.7 %all-to-all-start.2 = ((bf16[16,256,128]{2,1,0:T(8,128)(2,1)}), bf16[16,256,128]{2,1,0:T(8,128)(2,1)S(1)}, u32[]{:S(2)}, u32[]{:S(2)}) async-start(bf16[16,256,128]{2,1,0:T(8,128)(2,1)} %pad_maximum_fusion), calls=%async_computation.2 | async-start | bytes 2097152 | tf_op jit(solution)/shard_map/all_to_all | solution.py:389
  128.8 4.1 %collective-permute-start.7 = (bf16[16,128,128]{2,1,0:T(8,128)(2,1)S(1)}, bf16[16,128,128]{2,1,0:T(8,128)(2,1)}, u32[]{:S(2)}, u32[]{:S(2)}) collective-permute-start(bf16[16,128,128]{2,1,0:T(8,128)(2,1)S(1)} %get-tuple-element.59), channel_id=1, source_target_pairs={{0,64},{64,0},{1,65},{65,1},{2,66},{66,2},{3,67},{67,3},{4,68},{68... | collective-permute-start | bytes 1572872 | tf_op jit(solution)/shard_map/ppermute | solution.py:341
  132.9 1.4 convert_reduce_fusion
  134.3 0.3 collective-permute-start.9
  134.6 10.6 %collective-permute-done.7 = bf16[16,128,128]{2,1,0:T(8,128)(2,1)} collective-permute-done((bf16[16,128,128]{2,1,0:T(8,128)(2,1)S(1)}, bf16[16,128,128]{2,1,0:T(8,128)(2,1)}, u32[]{:S(2)}, u32[]{:S(2)}) %collective-permute-start.7) | collective-permute-done | bytes 524320 | tf_op jit(solution)/shard_map/ppermute | solution.py:341
  145.2 2.0 %add_convert_fusion.1 = bf16[16,128,128]{2,1,0:T(8,128)(2,1)} fusion(f32[16,128,128]{2,1,0:T(8,128)S(1)} %copy-done.6, bf16[16,128,128]{2,1,0:T(8,128)(2,1)} %collective-permute-done.7), kind=kLoop, calls=%fused_computation.7 | loop fusion | flops 786432 | bytes 2097152 | tf_op jit(solution)/shard_map/convert_element_type | solution.py:396
  147.2 6.9 %all-to-all-start.3 = ((bf16[16,128,128]{2,1,0:T(8,128)(2,1)}), bf16[16,128,128]{2,1,0:T(8,128)(2,1)S(1)}, u32[]{:S(2)}, u32[]{:S(2)}) async-start(bf16[16,128,128]{2,1,0:T(8,128)(2,1)} %add_convert_fusion.1), calls=%async_computation.3 | async-start | bytes 1048576 | tf_op jit(solution)/shard_map/all_to_all | solution.py:398
  154.1 0.7 maximum_select_fusion
  154.8 0.1 slice_bitcast_fusion
  154.9 0.3 copy.19
  155.2 1.0 copy.22
  156.2 0.3 copy.20
  156.5 1.0 copy.23
  157.5 6.6 %all-to-all-done.3 = bf16[16,128,128]{2,1,0:T(8,128)(2,1)S(1)} async-done(((bf16[16,128,128]{2,1,0:T(8,128)(2,1)}), bf16[16,128,128]{2,1,0:T(8,128)(2,1)S(1)}, u32[]{:S(2)}, u32[]{:S(2)}) %all-to-all-start.3) | async-done | bytes 524320 | tf_op jit(solution)/shard_map/all_to_all | solution.py:398
  164.1 0.3 copy.18
  164.4 1.0 copy.21
  (34 shorter events, 0.1 us)
Async XLA Ops:
  4.2 14.4 %copy-start.10 = (s32[1,128]{1,0:T(1,128)S(1)}, s32[1,128]{1,0:T(1,128)}, u32[]{:S(2)}) copy-start(s32[1,128]{1,0:T(1,128)} %param.8) | copy-start | bytes 1540
  4.2 16.7 %copy-start.1 = (bf16[1,128,2048]{2,1,0:T(8,128)(2,1)S(1)}, bf16[1,128,2048]{2,1,0:T(8,128)(2,1)}, u32[]{:S(2)}) copy-start(bf16[1,128,2048]{2,1,0:T(8,128)(2,1)} %param.12) | copy-start | bytes 1572868
  4.2 16.7 %copy-start.2 = (bf16[1,128,2048]{2,1,0:T(8,128)(2,1)S(1)}, bf16[1,128,2048]{2,1,0:T(8,128)(2,1)}, u32[]{:S(2)}) copy-start(bf16[1,128,2048]{2,1,0:T(8,128)(2,1)} %param.14) | copy-start | bytes 1572868
  4.2 16.7 %copy-start.7 = (f32[1,16,128]{2,1,0:T(8,128)S(1)}, f32[1,16,128]{2,1,0:T(8,128)}, u32[]{:S(2)}) copy-start(f32[1,16,128]{2,1,0:T(8,128)} %param.13) | copy-start | bytes 24580
  4.2 31.1 %all-to-all-start.1 = ((bf16[16,384,128]{2,1,0:T(8,128)(2,1)}), bf16[16,384,128]{2,1,0:T(8,128)(2,1)S(1)}, u32[]{:S(2)}, u32[]{:S(2)}) async-start(bf16[16,384,128]{2,1,0:T(8,128)(2,1)} %get-tuple-element.42), calls=%async_computation.1 | async-start | bytes 3145728 | tf_op jit(solution)/shard_map/all_to_all | solution.py:356
  11.5 29.6 %collective-permute-start.3 = (bf16[128,2048]{1,0:T(8,128)(2,1)}, bf16[128,2048]{1,0:T(8,128)(2,1)S(1)}, u32[]{:S(2)}, u32[]{:S(2)}) collective-permute-start(bf16[128,2048]{1,0:T(8,128)(2,1)} %get-tuple-element.52), channel_id=1, source_target_pairs={{0,1},{1,64},{64,65},{65,0},{2,3},{3,66},{66,67},{67,2},{4,5},{5,6... | collective-permute-start | bytes 1572872 | tf_op jit(solution)/shard_map/ppermute | solution.py:341
  13.5 27.6 %collective-permute-start.4 = (bf16[128,2048]{1,0:T(8,128)(2,1)}, bf16[128,2048]{1,0:T(8,128)(2,1)}, u32[]{:S(2)}, u32[]{:S(2)}) collective-permute-start(bf16[128,2048]{1,0:T(8,128)(2,1)} %get-tuple-element.53), channel_id=1, source_target_pairs={{0,64},{1,65},{64,0},{65,1},{2,66},{3,67},{66,2},{67,3},{4,68},{5,... | collective-permute-start | bytes 1572872 | tf_op jit(solution)/shard_map/ppermute | solution.py:341
  17.1 24.1 %collective-permute-start.5 = (bf16[128,2048]{1,0:T(8,128)(2,1)}, bf16[128,2048]{1,0:T(8,128)(2,1)}, u32[]{:S(2)}, u32[]{:S(2)}) collective-permute-start(bf16[128,2048]{1,0:T(8,128)(2,1)} %get-tuple-element.54), channel_id=1, source_target_pairs={{0,65},{1,0},{64,1},{65,64},{2,67},{3,2},{66,3},{67,66},{4,69},{5,... | collective-permute-start | bytes 1572872 | tf_op jit(solution)/shard_map/ppermute | solution.py:341
  20.9 3.4 %copy-start = (bf16[2048,2048]{1,0:T(8,128)(2,1)S(1)}, bf16[2048,2048]{1,0:T(8,128)(2,1)}, u32[]{:S(2)}) copy-start(bf16[2048,2048]{1,0:T(8,128)(2,1)} %weight.1) | copy-start | bytes 25165828
  28.4 12.8 %copy-start.8 = (bf16[128,2048]{1,0:T(8,128)(2,1)S(1)}, bf16[128,2048]{1,0:T(8,128)(2,1)}, u32[]{:S(2)}) copy-start(bf16[128,2048]{1,0:T(8,128)(2,1)} %get-tuple-element.51.part0) | copy-start | bytes 1572868
  35.3 14.4 %all-to-all-start = ((bf16[16,144,128]{2,1,0:T(8,128)(2,1)}), bf16[16,144,128]{2,1,0:T(8,128)(2,1)S(1)}, u32[]{:S(2)}, u32[]{:S(2)}) async-start(bf16[16,144,128]{2,1,0:T(8,128)(2,1)} %pack_second.1), calls=%async_computation | async-start | bytes 1179648 | tf_op jit(solution)/shard_map/all_to_all | solution.py:359
  40.3 13.5 %collective-permute-start = (bf16[16,256,128]{2,1,0:T(8,128)(2,1)}, bf16[16,256,128]{2,1,0:T(8,128)(2,1)}, u32[]{:S(2)}, u32[]{:S(2)}) collective-permute-start(bf16[16,256,128]{2,1,0:T(8,128)(2,1)} %slice.50), channel_id=1, source_target_pairs={{0,2},{2,0},{1,3},{3,1},{4,6},{6,4},{5,7},{7,5},{8,10},{10,8},{9,1... | collective-permute-start | bytes 3145736 | tf_op jit(solution)/shard_map/ppermute | solution.py:341
  45.4 30.4 %collective-permute-start.6 = (bf16[16,32,1024]{2,1,0:T(8,128)(2,1)}, bf16[16,32,1024]{2,1,0:T(8,128)(2,1)}, u32[]{:S(2)}, u32[]{:S(2)}) collective-permute-start(bf16[16,32,1024]{2,1,0:T(8,128)(2,1)} %get-tuple-element.56), channel_id=1, source_target_pairs={{0,2},{2,0},{1,3},{3,1},{4,6},{6,4},{5,7},{7,5},{8,10},{10,8},{9,1... | collective-permute-start | bytes 3145736 | tf_op jit(solution)/shard_map/ppermute | solution.py:341
  49.8 26.0 %collective-permute-start.2 = (bf16[16,144,128]{2,1,0:T(8,128)(2,1)S(1)}, bf16[16,144,128]{2,1,0:T(8,128)(2,1)S(1)}, u32[]{:S(2)}, u32[]{:S(2)}) collective-permute-start(bf16[16,144,128]{2,1,0:T(8,128)(2,1)S(1)} %all-to-all-done.grads), channel_id=1, source_target_pairs={{0,64},{64,0},{1,65},{65,1},{2,66},{66,2},{3,67},{67,3},{4,68},{68... | collective-permute-start | bytes 1769480 | tf_op jit(solution)/shard_map/ppermute | solution.py:341
  53.7 22.1 %collective-permute-start.1 = (bf16[16,128,128]{2,1,0:T(8,128)(2,1)S(1)}, bf16[16,128,128]{2,1,0:T(8,128)(2,1)S(1)}, u32[]{:S(2)}, u32[]{:S(2)}) collective-permute-start(bf16[16,128,128]{2,1,0:T(8,128)(2,1)S(1)} %slice.51), channel_id=1, source_target_pairs={{0,64},{64,0},{1,65},{65,1},{2,66},{66,2},{3,67},{67,3},{4,68},{68... | collective-permute-start | bytes 1572872 | tf_op jit(solution)/shard_map/ppermute | solution.py:341
  74.8 1.0 copy-start.5
  75.8 20.6 %copy-start.9 = (f32[16,32,1024]{2,1,0:T(8,128)S(1)}, f32[16,32,1024]{2,1,0:T(8,128)}, u32[]{:S(2)}) copy-start(f32[16,32,1024]{2,1,0:T(8,128)} %get-tuple-element.67) | copy-start | bytes 6291460
  95.4 1.0 copy-start.3
  96.4 10.7 %collective-permute-start.8 = (bf16[16,256,128]{2,1,0:T(8,128)(2,1)}, bf16[16,256,128]{2,1,0:T(8,128)(2,1)S(1)}, u32[]{:S(2)}, u32[]{:S(2)}) collective-permute-start(bf16[16,256,128]{2,1,0:T(8,128)(2,1)} %get-tuple-element.61), channel_id=1, source_target_pairs={{0,2},{2,0},{1,3},{3,1},{4,6},{6,4},{5,7},{7,5},{8,10},{10,8},{9,1... | collective-permute-start | bytes 3145736 | tf_op jit(solution)/shard_map/ppermute | solution.py:341
  99.0 26.1 %all-to-all-start.4 = ((bf16[16,32,1024]{2,1,0:T(8,128)(2,1)}), bf16[16,32,1024]{2,1,0:T(8,128)(2,1)}, u32[]{:S(2)}, u32[]{:S(2)}) async-start(bf16[16,32,1024]{2,1,0:T(8,128)(2,1)} %add_convert_fusion), calls=%async_computation.4 | async-start | bytes 2097152 | tf_op jit(solution)/shard_map/all_to_all | solution.py:380
  107.1 1.2 copy-start.4
  109.7 35.5 %copy-start.6 = (f32[16,128,128]{2,1,0:T(8,128)S(1)}, f32[16,128,128]{2,1,0:T(8,128)}, u32[]{:S(2)}) copy-start(f32[16,128,128]{2,1,0:T(8,128)} %copy-done.5) | copy-start | bytes 3145732
  125.1 22.1 %all-to-all-start.2 = ((bf16[16,256,128]{2,1,0:T(8,128)(2,1)}), bf16[16,256,128]{2,1,0:T(8,128)(2,1)S(1)}, u32[]{:S(2)}, u32[]{:S(2)}) async-start(bf16[16,256,128]{2,1,0:T(8,128)(2,1)} %pad_maximum_fusion), calls=%async_computation.2 | async-start | bytes 2097152 | tf_op jit(solution)/shard_map/all_to_all | solution.py:389
  128.8 16.4 %collective-permute-start.7 = (bf16[16,128,128]{2,1,0:T(8,128)(2,1)S(1)}, bf16[16,128,128]{2,1,0:T(8,128)(2,1)}, u32[]{:S(2)}, u32[]{:S(2)}) collective-permute-start(bf16[16,128,128]{2,1,0:T(8,128)(2,1)S(1)} %get-tuple-element.59), channel_id=1, source_target_pairs={{0,64},{64,0},{1,65},{65,1},{2,66},{66,2},{3,67},{67,3},{4,68},{68... | collective-permute-start | bytes 1572872 | tf_op jit(solution)/shard_map/ppermute | solution.py:341
  134.3 19.7 %collective-permute-start.9 = (f32[32,1024]{1,0:T(8,128)S(1)}, f32[32,1024]{1,0:T(8,128)S(1)}, u32[]{:S(2)}, u32[]{:S(2)}) collective-permute-start(f32[32,1024]{1,0:T(8,128)S(1)} %convert_reduce_fusion), channel_id=1, source_target_pairs={{0,1},{1,0},{2,3},{3,2},{4,5},{5,4},{6,7},{7,6},{8,9},{9,8},{10,11... | collective-permute-start | bytes 393224 | tf_op jit(solution)/shard_map/ppermute | solution.py:341
  147.2 17.0 %all-to-all-start.3 = ((bf16[16,128,128]{2,1,0:T(8,128)(2,1)}), bf16[16,128,128]{2,1,0:T(8,128)(2,1)S(1)}, u32[]{:S(2)}, u32[]{:S(2)}) async-start(bf16[16,128,128]{2,1,0:T(8,128)(2,1)} %add_convert_fusion.1), calls=%async_computation.3 | async-start | bytes 1048576 | tf_op jit(solution)/shard_map/all_to_all | solution.py:398

commit v4 on v3

--- a/solution.py
+++ b/solution.py
@@ -306,9 +306,10 @@
 
 
 def weight_body(side, part0, part1, part2, part3, kept, given, total):
-    parts = [part[...] for part in (part0, part1, part2, part3)]
-    rows = jnp.concatenate([part[:, :1024] for part in parts], axis=0)
-    cols = jnp.concatenate([part[:, 1024:] for part in parts], axis=0)
+    parts = [part[:, :1024] for part in (part0, part1, part2, part3)]
+    rows = jnp.concatenate(parts, axis=0)
+    span = pl.ds(pl.multiple_of(1024 + pl.program_id(0) * 512, 512), 512)
+    cols = jnp.concatenate([part[:, span] for part in (part0, part1, part2, part3)], axis=0)
     total[...] = lax.dot_general(rows, cols, TN, preferred_element_type=F32)
     c = side[0]
     for block in range(16):
@@ -321,11 +322,11 @@
 def weight_block(side, parts):
     return pl.pallas_call(
         weight_body,
-        grid=(1,),
+        grid=(2,),
         in_specs=[SMEM] + [pl.BlockSpec((128, 2048), lambda i: (0, 0))] * 4,
-        out_specs=[pl.BlockSpec((16, 32, 1024), lambda i: (0, 0, 0))] * 2,
+        out_specs=[pl.BlockSpec((16, 32, 512), lambda i: (0, 0, i))] * 2,
         out_shape=[pltpu.HBM((16, 32, 1024), F32), like((16, 32, 1024), BF16)],
-        scratch_shapes=[pltpu.VMEM((1024, 1024), F32)],
+        scratch_shapes=[pltpu.VMEM((1024, 512), F32)],
         compiler_params=pltpu.CompilerParams(vmem_limit_bytes=28 * 2**20),
         cost_estimate=pl.CostEstimate(flops=2 * 10**9, bytes_accessed=6 * 2**20, transcendentals=0),
         name="weight_block",

time: 166 us -> 166 us (level)
  no operation moved by 1% of the time
where the time goes in v4:
time: 166 us; the launch traced here: 165 us
  Pallas kernels  52.3 us (32%)
  starting transfers between devices  45.1 us (27%)
  waiting for transfers between devices  43.5 us (26%)
  local copies, waits for them, and re-layouts  13.1 us (8%)
  other arithmetic  10.4 us (6%)
    pallas_call x1, Pallas kernels, attn_near(): pl.pallas_call(functools.partial(near_body, tq=tq, tk=tk, scaling=scaling...  21 us
    pallas_call x1, Pallas kernels, attn_far(): pl.pallas_call(functools.partial(far_body, tq=tq, tk=tk, scaling=scaling)...  19.6 us
    ppermute x10, starting transfers between devices, ring(): lax.ppermute(array, axis, [(i, (i + by) % count) for i in range(count)])  15.4 us
    all_to_all x1, waiting for transfers between devices, step(): blocks = lax.all_to_all(blocks, ('x', 'y'), 0, 0, tiled=True)  15.4 us
    ppermute x10, waiting for transfers between devices, ring(): lax.ppermute(array, axis, [(i, (i + by) % count) for i in range(count)])  10.6 us
    unnamed x26, local copies, waits for them, and re-layouts  9.93 us
    all_to_all x1, starting transfers between devices, step(): blocks = lax.all_to_all(blocks, ('x', 'y'), 0, 0, tiled=True)  8 us
    all_to_all x1, starting transfers between devices, step(): own = lax.all_to_all(packed, ('x', 'y'), 0, 0, tiled=True)  7.29 us
  transfers between devices with their start and end apart: 15, of which 5 were waited for; matrix products, arithmetic and copies ran while one was open for 10% of the time, Pallas kernels for 18%

profile of v4, /device:TPU:0, one launch (start us, length us, event | category | flops | bytes accessed | tf_op | source)
XLA Modules:
  0.0 165.4 jit_solution(1682532521648871528)
XLA Ops:
  0.6 3.6 %pack_first.1 = (bf16[16,384,128]{2,1,0:T(8,128)(2,1)}, bf16[128,2048]{1,0:T(8,128)(2,1)}, bf16[128,2048]{1,0:T(8,128)(2,1)}, bf16[128,2048]{1,0:T(8,128)(2,1)}, bf16[128,2048]{1,0:T(8,128)(2,1)}) custom-call(s32[1]{0:T(128)} %bitcast.7.side, bf16[128,2048]{1,0:T(8,128)(2,1)} %bitcast.33, bf16[128,2048]{1,0:T(8,128)(2,1)} %bitcast.34, ...), custom_call_target="tpu_custom_call" | custom-call | tf_op jit(solution)/shard_map/pack_first/pallas_call | solution.py:70
  4.2 7.3 %all-to-all-start.1 = ((bf16[16,384,128]{2,1,0:T(8,128)(2,1)}), bf16[16,384,128]{2,1,0:T(8,128)(2,1)S(1)}, u32[]{:S(2)}, u32[]{:S(2)}) async-start(bf16[16,384,128]{2,1,0:T(8,128)(2,1)} %get-tuple-element.42), calls=%async_computation.1 | async-start | bytes 3145728 | tf_op jit(solution)/shard_map/all_to_all | solution.py:357
  11.5 2.0 %collective-permute-start.3 = (bf16[128,2048]{1,0:T(8,128)(2,1)}, bf16[128,2048]{1,0:T(8,128)(2,1)S(1)}, u32[]{:S(2)}, u32[]{:S(2)}) collective-permute-start(bf16[128,2048]{1,0:T(8,128)(2,1)} %get-tuple-element.52), channel_id=1, source_target_pairs={{0,1},{1,64},{64,65},{65,0},{2,3},{3,66},{66,67},{67,2},{4,5},{5,6... | collective-permute-start | bytes 1572872 | tf_op jit(solution)/shard_map/ppermute | solution.py:342
  13.5 3.6 %collective-permute-start.4 = (bf16[128,2048]{1,0:T(8,128)(2,1)}, bf16[128,2048]{1,0:T(8,128)(2,1)}, u32[]{:S(2)}, u32[]{:S(2)}) collective-permute-start(bf16[128,2048]{1,0:T(8,128)(2,1)} %get-tuple-element.53), channel_id=1, source_target_pairs={{0,64},{1,65},{64,0},{65,1},{2,66},{3,67},{66,2},{67,3},{4,68},{5,... | collective-permute-start | bytes 1572872 | tf_op jit(solution)/shard_map/ppermute | solution.py:342
  17.1 1.0 collective-permute-start.5
  18.1 0.5 broadcast.23
  18.6 0.7 reduce.15
  19.3 0.2 reshape_squeeze.3
  19.5 0.1 dynamic-slice_reduce_fusion
  19.5 0.1 gt.43
  19.6 0.1 reshape.78
  19.7 0.1 pad_add_fusion.2
  19.8 0.2 convert_reduce_fusion.1.k_rank
  20.0 0.1 select_reduce_fusion.k_base
  20.1 0.1 slice.39
  20.2 0.1 slice.41
  20.3 0.2 convert_reduce_fusion.3.q_rank
  20.5 0.1 select_reduce_fusion.2.q_base
  20.6 0.1 slice.38
  20.7 0.1 slice.40
  20.8 0.1 gt.50
  20.9 3.4 %copy-done = bf16[2048,2048]{1,0:T(8,128)(2,1)S(1)} copy-done((bf16[2048,2048]{1,0:T(8,128)(2,1)S(1)}, bf16[2048,2048]{1,0:T(8,128)(2,1)}, u32[]{:S(2)}) %copy-start) | copy-done | bytes 8388632
  24.3 4.0 %pack_second.1 = bf16[16,144,128]{2,1,0:T(8,128)(2,1)} custom-call(bf16[128,2048]{1,0:T(8,128)(2,1)S(1)} %bitcast.27, bf16[2048,2048]{1,0:T(8,128)(2,1)S(1)} %copy-done, bf16[128,2048]{1,0:T(8,128)(2,1)S(1)} %bitcast.25, f32[16,128]{1,0:T(8,128)S(1)} %bitcast.28), custom_call_target="tpu_custom_call" | custom-call | tf_op jit(solution)/shard_map/pack_second/pallas_call | solution.py:82
  28.4 7.0 %all-to-all-done.1.own = bf16[16,384,128]{2,1,0:T(8,128)(2,1)S(1)} async-done(((bf16[16,384,128]{2,1,0:T(8,128)(2,1)}), bf16[16,384,128]{2,1,0:T(8,128)(2,1)S(1)}, u32[]{:S(2)}, u32[]{:S(2)}) %all-to-all-start.1) | async-done | bytes 1572896 | tf_op jit(solution)/shard_map/all_to_all | solution.py:357
  35.3 3.9 %all-to-all-start = ((bf16[16,144,128]{2,1,0:T(8,128)(2,1)}), bf16[16,144,128]{2,1,0:T(8,128)(2,1)S(1)}, u32[]{:S(2)}, u32[]{:S(2)}) async-start(bf16[16,144,128]{2,1,0:T(8,128)(2,1)} %pack_second.1), calls=%async_computation | async-start | bytes 1179648 | tf_op jit(solution)/shard_map/all_to_all | solution.py:360
  39.2 1.1 slice.50
  40.3 0.2 convert_reduce_fusion.2.q_rank
  40.5 0.1 select_reduce_fusion.1.q_base
  40.6 0.1 slice.42
  40.7 0.1 slice.43
  40.8 0.2 convert_reduce_fusion.5
  40.9 0.2 convert_reduce_fusion.4
  41.2 4.2 %weight_block.1 = (f32[16,32,1024]{2,1,0:T(8,128)}, bf16[16,32,1024]{2,1,0:T(8,128)(2,1)}) custom-call(s32[1]{0:T(128)} %bitcast.11.side, bf16[128,2048]{1,0:T(8,128)(2,1)S(1)} %copy-done.8, bf16[128,2048]{1,0:T(8,128)(2,1)S(1)} %collective-permute-done.3.part1, bf16[128,2048]{1,0:T(8,128)(2,1)} %collective-permute-done.4.part2, ...), custom_call_target="tpu_custom_call" | custom-call | flops 2000000000 | bytes 6291456 | tf_op jit(solution)/shard_map/weight_block/pallas_call | solution.py:323
  45.4 0.5 collective-permute-start.6
  45.9 3.9 %all-to-all-done.grads = bf16[16,144,128]{2,1,0:T(8,128)(2,1)S(1)} async-done(((bf16[16,144,128]{2,1,0:T(8,128)(2,1)}), bf16[16,144,128]{2,1,0:T(8,128)(2,1)S(1)}, u32[]{:S(2)}, u32[]{:S(2)}) %all-to-all-start) | async-done | bytes 589856 | tf_op jit(solution)/shard_map/all_to_all | solution.py:360
  49.8 3.9 %collective-permute-start.2 = (bf16[16,144,128]{2,1,0:T(8,128)(2,1)S(1)}, bf16[16,144,128]{2,1,0:T(8,128)(2,1)S(1)}, u32[]{:S(2)}, u32[]{:S(2)}) collective-permute-start(bf16[16,144,128]{2,1,0:T(8,128)(2,1)S(1)} %all-to-all-done.grads), channel_id=1, source_target_pairs={{0,64},{64,0},{1,65},{65,1},{2,66},{66,2},{3,67},{67,3},{4,68},{68... | collective-permute-start | bytes 1769480 | tf_op jit(solution)/shard_map/ppermute | solution.py:342
  53.7 0.1 collective-permute-start.1
  53.8 21.0 %attn_near.1 = (f32[16,128,128]{2,1,0:T(8,128)S(1)}, f32[4096,128]{1,0:T(8,128)}, f32[4096,128]{1,0:T(8,128)}) custom-call(s32[2,4]{1,0:T(2,128)S(1)} %pad_add_fusion.plan, s32[32]{0:T(128)S(1)} %convert_reduce_fusion.3.q_rank, s32[32]{0:T(128)S(1)} %select_reduce_fusion.2.q_base, s32[64]{0:T(128)S(1)} %convert_reduce_fusion.1.k_rank, ...), custom_call_target="tpu_custom_call" | custom-call | flops 7000000000 | bytes 12582912 | tf_op jit(solution)/shard_map/attn_near/pallas_call | solution.py:266
  74.8 1.0 copy-done.5
  75.8 19.6 %attn_far.1 = (bf16[16,128,128]{2,1,0:T(8,128)(2,1)S(1)}, f32[16,128,128]{2,1,0:T(8,128)S(1)}, f32[16,128,128]{2,1,0:T(8,128)S(1)}, bf16[16,256,128]{2,1,0:T(8,128)(2,1)}) custom-call(s32[2,4]{1,0:T(2,128)S(1)} %pad_add_fusion.1.plan, s32[32]{0:T(128)S(1)} %convert_reduce_fusion.2.q_rank, s32[32]{0:T(128)S(1)} %select_reduce_fusion.1.q_base, ...), custom_call_target="tpu_custom_call" | custom-call | flops 7000000000 | bytes 12582912 | tf_op jit(solution)/shard_map/attn_far/pallas_call | solution.py:279
  95.4 1.0 copy-done.3
  96.4 2.6 %add_convert_fusion = bf16[16,32,1024]{2,1,0:T(8,128)(2,1)} fusion(f32[16,32,1024]{2,1,0:T(8,128)S(1)} %copy-done.9, bf16[16,32,1024]{2,1,0:T(8,128)(2,1)} %collective-permute-done.6), kind=kLoop, calls=%fused_computation.1 | loop fusion | flops 1572864 | bytes 4194304 | tf_op jit(solution)/shard_map/convert_element_type | solution.py:380
  99.0 8.0 %all-to-all-start.4 = ((bf16[16,32,1024]{2,1,0:T(8,128)(2,1)}), bf16[16,32,1024]{2,1,0:T(8,128)(2,1)}, u32[]{:S(2)}, u32[]{:S(2)}) async-start(bf16[16,32,1024]{2,1,0:T(8,128)(2,1)} %add_convert_fusion), calls=%async_computation.4 | async-start | bytes 2097152 | tf_op jit(solution)/shard_map/all_to_all | solution.py:381
  107.1 0.2 convert_element_type.52
  107.3 1.0 copy-done.4
  108.3 0.3 fusion.1
  108.6 1.1 pad_maximum_fusion
  109.6 15.4 %all-to-all-done.4 = bf16[16,32,1024]{2,1,0:T(8,128)(2,1)} async-done(((bf16[16,32,1024]{2,1,0:T(8,128)(2,1)}), bf16[16,32,1024]{2,1,0:T(8,128)(2,1)}, u32[]{:S(2)}, u32[]{:S(2)}) %all-to-all-start.4) | async-done | bytes 1048608 | tf_op jit(solution)/shard_map/all_to_all | solution.py:381
  125.1 3.7 %all-to-all-start.2 = ((bf16[16,256,128]{2,1,0:T(8,128)(2,1)}), bf16[16,256,128]{2,1,0:T(8,128)(2,1)S(1)}, u32[]{:S(2)}, u32[]{:S(2)}) async-start(bf16[16,256,128]{2,1,0:T(8,128)(2,1)} %pad_maximum_fusion), calls=%async_computation.2 | async-start | bytes 2097152 | tf_op jit(solution)/shard_map/all_to_all | solution.py:390
  128.7 4.1 %collective-permute-start.7 = (bf16[16,128,128]{2,1,0:T(8,128)(2,1)S(1)}, bf16[16,128,128]{2,1,0:T(8,128)(2,1)}, u32[]{:S(2)}, u32[]{:S(2)}) collective-permute-start(bf16[16,128,128]{2,1,0:T(8,128)(2,1)S(1)} %get-tuple-element.59), channel_id=1, source_target_pairs={{0,64},{64,0},{1,65},{65,1},{2,66},{66,2},{3,67},{67,3},{4,68},{68... | collective-permute-start | bytes 1572872 | tf_op jit(solution)/shard_map/ppermute | solution.py:342
  132.9 1.4 convert_reduce_fusion
  134.3 0.3 collective-permute-start.9
  134.6 10.6 %collective-permute-done.7 = bf16[16,128,128]{2,1,0:T(8,128)(2,1)} collective-permute-done((bf16[16,128,128]{2,1,0:T(8,128)(2,1)S(1)}, bf16[16,128,128]{2,1,0:T(8,128)(2,1)}, u32[]{:S(2)}, u32[]{:S(2)}) %collective-permute-start.7) | collective-permute-done | bytes 524320 | tf_op jit(solution)/shard_map/ppermute | solution.py:342
  145.2 2.0 %add_convert_fusion.1 = bf16[16,128,128]{2,1,0:T(8,128)(2,1)} fusion(f32[16,128,128]{2,1,0:T(8,128)S(1)} %copy-done.6, bf16[16,128,128]{2,1,0:T(8,128)(2,1)} %collective-permute-done.7), kind=kLoop, calls=%fused_computation.7 | loop fusion | flops 786432 | bytes 2097152 | tf_op jit(solution)/shard_map/convert_element_type | solution.py:397
  147.1 6.9 %all-to-all-start.3 = ((bf16[16,128,128]{2,1,0:T(8,128)(2,1)}), bf16[16,128,128]{2,1,0:T(8,128)(2,1)S(1)}, u32[]{:S(2)}, u32[]{:S(2)}) async-start(bf16[16,128,128]{2,1,0:T(8,128)(2,1)} %add_convert_fusion.1), calls=%async_computation.3 | async-start | bytes 1048576 | tf_op jit(solution)/shard_map/all_to_all | solution.py:399
  154.0 0.7 maximum_select_fusion
  154.7 0.1 slice_bitcast_fusion
  154.9 0.3 copy.19
  155.1 1.0 copy.22
  156.2 0.3 copy.20
  156.4 1.0 copy.23
  157.5 6.6 %all-to-all-done.3 = bf16[16,128,128]{2,1,0:T(8,128)(2,1)S(1)} async-done(((bf16[16,128,128]{2,1,0:T(8,128)(2,1)}), bf16[16,128,128]{2,1,0:T(8,128)(2,1)S(1)}, u32[]{:S(2)}, u32[]{:S(2)}) %all-to-all-start.3) | async-done | bytes 524320 | tf_op jit(solution)/shard_map/all_to_all | solution.py:399
  164.1 0.3 copy.18
  164.4 1.0 copy.21
  (34 shorter events, 0.1 us)
Async XLA Ops:
  4.2 14.4 %copy-start.10 = (s32[1,128]{1,0:T(1,128)S(1)}, s32[1,128]{1,0:T(1,128)}, u32[]{:S(2)}) copy-start(s32[1,128]{1,0:T(1,128)} %param.8) | copy-start | bytes 1540
  4.2 16.7 %copy-start.1 = (bf16[1,128,2048]{2,1,0:T(8,128)(2,1)S(1)}, bf16[1,128,2048]{2,1,0:T(8,128)(2,1)}, u32[]{:S(2)}) copy-start(bf16[1,128,2048]{2,1,0:T(8,128)(2,1)} %param.12) | copy-start | bytes 1572868
  4.2 16.7 %copy-start.2 = (bf16[1,128,2048]{2,1,0:T(8,128)(2,1)S(1)}, bf16[1,128,2048]{2,1,0:T(8,128)(2,1)}, u32[]{:S(2)}) copy-start(bf16[1,128,2048]{2,1,0:T(8,128)(2,1)} %param.14) | copy-start | bytes 1572868
  4.2 16.7 %copy-start.7 = (f32[1,16,128]{2,1,0:T(8,128)S(1)}, f32[1,16,128]{2,1,0:T(8,128)}, u32[]{:S(2)}) copy-start(f32[1,16,128]{2,1,0:T(8,128)} %param.13) | copy-start | bytes 24580
  4.2 31.1 %all-to-all-start.1 = ((bf16[16,384,128]{2,1,0:T(8,128)(2,1)}), bf16[16,384,128]{2,1,0:T(8,128)(2,1)S(1)}, u32[]{:S(2)}, u32[]{:S(2)}) async-start(bf16[16,384,128]{2,1,0:T(8,128)(2,1)} %get-tuple-element.42), calls=%async_computation.1 | async-start | bytes 3145728 | tf_op jit(solution)/shard_map/all_to_all | solution.py:357
  11.5 29.6 %collective-permute-start.3 = (bf16[128,2048]{1,0:T(8,128)(2,1)}, bf16[128,2048]{1,0:T(8,128)(2,1)S(1)}, u32[]{:S(2)}, u32[]{:S(2)}) collective-permute-start(bf16[128,2048]{1,0:T(8,128)(2,1)} %get-tuple-element.52), channel_id=1, source_target_pairs={{0,1},{1,64},{64,65},{65,0},{2,3},{3,66},{66,67},{67,2},{4,5},{5,6... | collective-permute-start | bytes 1572872 | tf_op jit(solution)/shard_map/ppermute | solution.py:342
  13.5 27.6 %collective-permute-start.4 = (bf16[128,2048]{1,0:T(8,128)(2,1)}, bf16[128,2048]{1,0:T(8,128)(2,1)}, u32[]{:S(2)}, u32[]{:S(2)}) collective-permute-start(bf16[128,2048]{1,0:T(8,128)(2,1)} %get-tuple-element.53), channel_id=1, source_target_pairs={{0,64},{1,65},{64,0},{65,1},{2,66},{3,67},{66,2},{67,3},{4,68},{5,... | collective-permute-start | bytes 1572872 | tf_op jit(solution)/shard_map/ppermute | solution.py:342
  17.1 24.1 %collective-permute-start.5 = (bf16[128,2048]{1,0:T(8,128)(2,1)}, bf16[128,2048]{1,0:T(8,128)(2,1)}, u32[]{:S(2)}, u32[]{:S(2)}) collective-permute-start(bf16[128,2048]{1,0:T(8,128)(2,1)} %get-tuple-element.54), channel_id=1, source_target_pairs={{0,65},{1,0},{64,1},{65,64},{2,67},{3,2},{66,3},{67,66},{4,69},{5,... | collective-permute-start | bytes 1572872 | tf_op jit(solution)/shard_map/ppermute | solution.py:342
  20.9 3.4 %copy-start = (bf16[2048,2048]{1,0:T(8,128)(2,1)S(1)}, bf16[2048,2048]{1,0:T(8,128)(2,1)}, u32[]{:S(2)}) copy-start(bf16[2048,2048]{1,0:T(8,128)(2,1)} %weight.1) | copy-start | bytes 25165828
  28.4 12.8 %copy-start.8 = (bf16[128,2048]{1,0:T(8,128)(2,1)S(1)}, bf16[128,2048]{1,0:T(8,128)(2,1)}, u32[]{:S(2)}) copy-start(bf16[128,2048]{1,0:T(8,128)(2,1)} %get-tuple-element.51.part0) | copy-start | bytes 1572868
  35.3 14.4 %all-to-all-start = ((bf16[16,144,128]{2,1,0:T(8,128)(2,1)}), bf16[16,144,128]{2,1,0:T(8,128)(2,1)S(1)}, u32[]{:S(2)}, u32[]{:S(2)}) async-start(bf16[16,144,128]{2,1,0:T(8,128)(2,1)} %pack_second.1), calls=%async_computation | async-start | bytes 1179648 | tf_op jit(solution)/shard_map/all_to_all | solution.py:360
  40.3 13.5 %collective-permute-start = (bf16[16,256,128]{2,1,0:T(8,128)(2,1)}, bf16[16,256,128]{2,1,0:T(8,128)(2,1)}, u32[]{:S(2)}, u32[]{:S(2)}) collective-permute-start(bf16[16,256,128]{2,1,0:T(8,128)(2,1)} %slice.50), channel_id=1, source_target_pairs={{0,2},{2,0},{1,3},{3,1},{4,6},{6,4},{5,7},{7,5},{8,10},{10,8},{9,1... | collective-permute-start | bytes 3145736 | tf_op jit(solution)/shard_map/ppermute | solution.py:342
  45.4 30.4 %collective-permute-start.6 = (bf16[16,32,1024]{2,1,0:T(8,128)(2,1)}, bf16[16,32,1024]{2,1,0:T(8,128)(2,1)}, u32[]{:S(2)}, u32[]{:S(2)}) collective-permute-start(bf16[16,32,1024]{2,1,0:T(8,128)(2,1)} %get-tuple-element.56), channel_id=1, source_target_pairs={{0,2},{2,0},{1,3},{3,1},{4,6},{6,4},{5,7},{7,5},{8,10},{10,8},{9,1... | collective-permute-start | bytes 3145736 | tf_op jit(solution)/shard_map/ppermute | solution.py:342
  49.8 26.0 %collective-permute-start.2 = (bf16[16,144,128]{2,1,0:T(8,128)(2,1)S(1)}, bf16[16,144,128]{2,1,0:T(8,128)(2,1)S(1)}, u32[]{:S(2)}, u32[]{:S(2)}) collective-permute-start(bf16[16,144,128]{2,1,0:T(8,128)(2,1)S(1)} %all-to-all-done.grads), channel_id=1, source_target_pairs={{0,64},{64,0},{1,65},{65,1},{2,66},{66,2},{3,67},{67,3},{4,68},{68... | collective-permute-start | bytes 1769480 | tf_op jit(solution)/shard_map/ppermute | solution.py:342
  53.7 22.1 %collective-permute-start.1 = (bf16[16,128,128]{2,1,0:T(8,128)(2,1)S(1)}, bf16[16,128,128]{2,1,0:T(8,128)(2,1)S(1)}, u32[]{:S(2)}, u32[]{:S(2)}) collective-permute-start(bf16[16,128,128]{2,1,0:T(8,128)(2,1)S(1)} %slice.51), channel_id=1, source_target_pairs={{0,64},{64,0},{1,65},{65,1},{2,66},{66,2},{3,67},{67,3},{4,68},{68... | collective-permute-start | bytes 1572872 | tf_op jit(solution)/shard_map/ppermute | solution.py:342
  74.8 1.0 copy-start.5
  75.8 20.6 %copy-start.9 = (f32[16,32,1024]{2,1,0:T(8,128)S(1)}, f32[16,32,1024]{2,1,0:T(8,128)}, u32[]{:S(2)}) copy-start(f32[16,32,1024]{2,1,0:T(8,128)} %get-tuple-element.67) | copy-start | bytes 6291460
  95.4 1.0 copy-start.3
  96.4 10.7 %collective-permute-start.8 = (bf16[16,256,128]{2,1,0:T(8,128)(2,1)}, bf16[16,256,128]{2,1,0:T(8,128)(2,1)S(1)}, u32[]{:S(2)}, u32[]{:S(2)}) collective-permute-start(bf16[16,256,128]{2,1,0:T(8,128)(2,1)} %get-tuple-element.61), channel_id=1, source_target_pairs={{0,2},{2,0},{1,3},{3,1},{4,6},{6,4},{5,7},{7,5},{8,10},{10,8},{9,1... | collective-permute-start | bytes 3145736 | tf_op jit(solution)/shard_map/ppermute | solution.py:342
  99.0 26.0 %all-to-all-start.4 = ((bf16[16,32,1024]{2,1,0:T(8,128)(2,1)}), bf16[16,32,1024]{2,1,0:T(8,128)(2,1)}, u32[]{:S(2)}, u32[]{:S(2)}) async-start(bf16[16,32,1024]{2,1,0:T(8,128)(2,1)} %add_convert_fusion), calls=%async_computation.4 | async-start | bytes 2097152 | tf_op jit(solution)/shard_map/all_to_all | solution.py:381
  107.0 1.2 copy-start.4
  109.6 35.5 %copy-start.6 = (f32[16,128,128]{2,1,0:T(8,128)S(1)}, f32[16,128,128]{2,1,0:T(8,128)}, u32[]{:S(2)}) copy-start(f32[16,128,128]{2,1,0:T(8,128)} %copy-done.5) | copy-start | bytes 3145732
  125.1 22.1 %all-to-all-start.2 = ((bf16[16,256,128]{2,1,0:T(8,128)(2,1)}), bf16[16,256,128]{2,1,0:T(8,128)(2,1)S(1)}, u32[]{:S(2)}, u32[]{:S(2)}) async-start(bf16[16,256,128]{2,1,0:T(8,128)(2,1)} %pad_maximum_fusion), calls=%async_computation.2 | async-start | bytes 2097152 | tf_op jit(solution)/shard_map/all_to_all | solution.py:390
  128.7 16.4 %collective-permute-start.7 = (bf16[16,128,128]{2,1,0:T(8,128)(2,1)S(1)}, bf16[16,128,128]{2,1,0:T(8,128)(2,1)}, u32[]{:S(2)}, u32[]{:S(2)}) collective-permute-start(bf16[16,128,128]{2,1,0:T(8,128)(2,1)S(1)} %get-tuple-element.59), channel_id=1, source_target_pairs={{0,64},{64,0},{1,65},{65,1},{2,66},{66,2},{3,67},{67,3},{4,68},{68... | collective-permute-start | bytes 1572872 | tf_op jit(solution)/shard_map/ppermute | solution.py:342
  134.3 19.7 %collective-permute-start.9 = (f32[32,1024]{1,0:T(8,128)S(1)}, f32[32,1024]{1,0:T(8,128)S(1)}, u32[]{:S(2)}, u32[]{:S(2)}) collective-permute-start(f32[32,1024]{1,0:T(8,128)S(1)} %convert_reduce_fusion), channel_id=1, source_target_pairs={{0,1},{1,0},{2,3},{3,2},{4,5},{5,4},{6,7},{7,6},{8,9},{9,8},{10,11... | collective-permute-start | bytes 393224 | tf_op jit(solution)/shard_map/ppermute | solution.py:342
  147.1 17.0 %all-to-all-start.3 = ((bf16[16,128,128]{2,1,0:T(8,128)(2,1)}), bf16[16,128,128]{2,1,0:T(8,128)(2,1)S(1)}, u32[]{:S(2)}, u32[]{:S(2)}) async-start(bf16[16,128,128]{2,1,0:T(8,128)(2,1)} %add_convert_fusion.1), calls=%async_computation.3 | async-start | bytes 1048576 | tf_op jit(solution)/shard_map/all_to_all | solution.py:399
